TPU v7x, 768 devices: a whole 4x8x12 slice. The times are simulated.
768 devices in a mesh: dp: 96 (over z_lo, y, x), tp: 8 (over z_hi, core).
Axes of the slice: x: 4, y: 8, z: 12 (z_hi: 4, z_lo: 3; z = z_hi * 3 + z_lo), core: 2. Of those that a mesh axis runs over, the one named last changes fastest.
Arguments:
- resid: bfloat16 [24576, 4096], P('dp'), may hold values from -6 to 6
- gain: bfloat16 [4096], replicated, may hold values from 0.25 to 1.75
- grad_q: bfloat16 [24576, 3072], P('dp', 'tp'), may hold values from -3 to 3
- w_query: bfloat16 [3072, 4096], P('tp'), may hold values from -0.375 to 0.375
- grad_in: bfloat16 [24576, 4096], P('dp'), may hold values from -2 to 2
Outputs:
- weight_grad: float32 [3072, 4096], P(('tp', 'dp'))
- gain_grad: float32 [4096], replicated
- grad_out: bfloat16 [24576, 4096], P('dp')
All inputs are finite; a program needn't handle non-finite values.
Results may differ from a plain program's by a relative error of at most 0.014.
Values may be sent and summed in bfloat16 or wider, within the bound.
No kernel may reach another device: no remote copies, remote signals or barrier semaphores. Data moves between devices by JAX's collectives and lax.ppermute only.
A program may use at most 64 MiB of HBM per device.

v0:
```python
import jax
import jax.numpy as jnp
from jax import lax
from jax.sharding import Mesh
from jax.sharding import PartitionSpec as P


DP = ("zl", "y", "x")
TP = ("zh", "c")
F32 = jnp.float32
BF16 = jnp.bfloat16


def exchange(blocks, axes):
    return lax.all_to_all(blocks, axes, 0, 0, tiled=True)


def total(blocks):
    return jnp.sum(blocks.astype(F32), axis=0)


def shifted(block, axis, shift):
    peers = lax.axis_size(axis)
    return lax.ppermute(block, axis, [(i, (i + shift) % peers) for i in range(peers)])


def swapped(block, axis, bit):
    return lax.ppermute(block, axis, [(i, i ^ bit) for i in range(lax.axis_size(axis))])


def owner_columns(cols, x_index):
    zl, y, x = (lax.axis_size(a) for a in DP)
    rows = cols // (zl * y * x)
    place = jnp.arange(cols)
    shift, owner, row = place // (zl * y * rows), place // rows % (zl * y), place % rows
    source = owner * (x * rows) + lax.rem(shift + x_index, x) * rows + row
    return (place[:, None] == source[None, :]).astype(BF16)


def body(resid, gain, grad_q, w_query, grad_in):
    tokens, width = resid.shape
    cols = grad_q.shape[1]
    core, zh = lax.axis_index("c"), lax.axis_index("zh")
    n_zh, n_x, n_y, n_zl = (lax.axis_size(a) for a in ("zh", "x", "y", "zl"))
    half = tokens // 2
    own = half // n_zh
    gain_f = gain.astype(F32)

    def rows_of(array, start, size):
        return lax.dynamic_slice_in_dim(array, start, size, 0)

    def inverse(rows):
        rows_f = rows.astype(F32)
        return lax.rsqrt(jnp.mean(rows_f * rows_f, axis=-1, keepdims=True) + 1e-05)

    def term(start):
        return jnp.dot(rows_of(grad_q, start, half), w_query, preferred_element_type=F32)

    other_start, own_start = (1 - core) * half, core * half
    sent = term(other_start)
    got = swapped(sent.astype(BF16), "c", 1)
    kept = lax.optimization_barrier(term(own_start))
    pair = (kept + got.astype(F32)).astype(BF16)
    inv = inverse(resid)
    pair, inv = lax.optimization_barrier((pair, inv))
    dnormed = total(exchange(pair.reshape(n_zh, own, width), "zh"))

    unit = resid.astype(F32) * inv
    normed = (unit * gain_f).astype(BF16)
    ordered = jnp.dot(grad_q, owner_columns(cols, lax.axis_index("x")), preferred_element_type=F32)
    ordered = lax.optimization_barrier(ordered.astype(BF16))
    share = cols // n_x

    def block(shift):
        columns = ordered[:, shift * share : (shift + 1) * share]
        return lax.dot_general(
            columns, normed, (((0,), (0,)), ((), ())), preferred_element_type=F32
        )

    blocks = [block(s).astype(BF16) for s in range(1, n_x)]
    inv, *blocks = lax.optimization_barrier((inv, *blocks))
    by_x = [shifted(b, "x", s + 1) for s, b in enumerate(blocks)]
    unit = resid.astype(F32) * inv
    part = jnp.sum(sent * rows_of(unit, other_start, half), axis=0)
    part = part + jnp.sum(kept * rows_of(unit, own_start, half), axis=0)
    part = part.reshape(n_y, -1, 128)
    for bit in (1, 2, 4):
        part = part + swapped(part, "y", bit)
    part = lax.dynamic_index_in_dim(part, lax.axis_index("y"), 0, keepdims=False)
    axes = ("x", "zh", "c")
    part, dnormed = lax.optimization_barrier((part, dnormed))
    part = jnp.broadcast_to(part[None], (lax.axis_size(axes), *part.shape))
    part = total(exchange(part, axes))

    first = own_start + zh * own
    resid_rows = rows_of(resid, first, own)
    inv_rows = inverse(resid_rows)
    unit_rows = resid_rows.astype(F32) * inv_rows
    dunit = dnormed * gain_f
    inner = jnp.mean(dunit * unit_rows, axis=-1, keepdims=True)
    rows = rows_of(grad_in, first, own).astype(F32) + inv_rows * (dunit - unit_rows * inner)
    first_block, rows = lax.optimization_barrier((block(0), rows.astype(BF16)))

    by_x = first_block + sum(b.astype(F32) for b in by_x)
    mine = share // (n_y * n_zl)
    by_x = by_x.astype(BF16).reshape(n_zl * n_y, mine, width)

    upper = part.astype(BF16)
    lower = (part - upper.astype(F32)).astype(BF16)
    rider = jnp.concatenate([upper, lower], axis=1)
    rider = jnp.broadcast_to(rider[None], (n_zl * n_y, *rider.shape))
    last = exchange(jnp.concatenate([by_x, rider], axis=2), ("zl", "y"))
    weight_grad = total(last[:, :, :width])
    parts = last[:, :, width:].astype(F32)
    parts = (parts[:, :, :128] + parts[:, :, 128:]).reshape(n_zl, n_y, -1, 128)
    gain_grad = jnp.sum(parts, axis=0).reshape(-1)

    result = jnp.zeros((tokens, width), BF16)
    for shift in range(n_zh):
        piece = rows if shift == 0 else shifted(rows, "zh", shift)
        source = lax.rem(zh + n_zh - shift, n_zh) * own
        result = lax.dynamic_update_slice_in_dim(result, piece, own_start + source, 0)
        piece = swapped(piece, "c", 1)
        result = lax.dynamic_update_slice_in_dim(result, piece, other_start + source, 0)
    return weight_grad, gain_grad, result


def solution(mesh):
    finer = Mesh(mesh.devices.reshape(3, 8, 4, 4, 2), ("zl", "y", "x", "zh", "c"))
    in_specs = (P(DP, None), P(), P(DP, TP), P(TP, None), P(DP, None))
    out_specs = (P(TP + DP, None), P(), P(DP, None))
    return jax.shard_map(body, mesh=finer, in_specs=in_specs, out_specs=out_specs, check_vma=False)
```

profile of v0, /device:TPU:6, one launch (start us, length us, event | category | flops | bytes accessed | tf_op | source)
XLA Modules:
  0.0 156.8 jit_solution(8556249868899228807)
XLA Ops:
  0.7 1.9 %copy-done = bf16[384,4096]{1,0:T(8,128)(2,1)S(1)} copy-done((bf16[384,4096]{1,0:T(8,128)(2,1)S(1)}, bf16[384,4096]{1,0:T(8,128)(2,1)}, u32[]{:S(2)}) %copy-start) | copy-done | bytes 3145752
  2.5 3.3 %fusion.47 = (bf16[128,4096]{1,0:T(8,128)(2,1)}, f32[128,4096]{1,0:T(8,128)}) fusion(bf16[384,4096]{1,0:T(8,128)(2,1)S(1)} %copy-done, bf16[256,384]{1,0:T(8,128)(2,1)} %param.7, s32[]{:T(128)S(6)} %select_n.80), kind=kOutput, calls=%fused_computation.86 | convolution fusion | flops 403177472 | bytes 6389764 | tf_op jit(solution)/shard_map/dot_general | solution.py:57
  5.8 1.9 %collective-permute-start = (bf16[128,4096]{1,0:T(8,128)(2,1)}, bf16[128,4096]{1,0:T(8,128)(2,1)}, u32[]{:S(2)}, u32[]{:S(2)}) collective-permute-start(bf16[128,4096]{1,0:T(8,128)(2,1)} %get-tuple-element.27), channel_id=1, source_target_pairs={{0,1},{1,0},{2,3},{3,2},{4,5},{5,4},{6,7},{7,6},{8,9},{9,8},{10,11... | collective-permute-start | bytes 3145736 | tf_op jit(solution)/shard_map/ppermute | solution.py:28
  7.8 2.0 %fusion.17 = f32[128,4096]{1,0:T(8,128)} fusion(bf16[384,4096]{1,0:T(8,128)(2,1)S(1)} %copy-done, bf16[256,384]{1,0:T(8,128)(2,1)S(1)} %copy-done.5, s32[]{:T(128)S(6)} %select_n.79), kind=kOutput, calls=%fused_computation.33 | convolution fusion | flops 402653184 | bytes 5341188 | tf_op jit(solution)/shard_map/dot_general | solution.py:57
  9.9 1.0 fusion.3
  10.8 2.1 %fusion = f32[256]{0:T(256)S(1)} fusion(bf16[256,4096]{1,0:T(8,128)(2,1)} %param.5), kind=kLoop, calls=%fused_computation.6 | loop fusion | flops 3145472 | bytes 2098176 | tf_op jit(solution)/shard_map/reduce_sum | solution.py:54
  12.9 2.5 %add_convert_fusion = bf16[128,4096]{1,0:T(8,128)(2,1)} fusion(f32[128,4096]{1,0:T(8,128)S(1)} %copy-done.1, bf16[128,4096]{1,0:T(8,128)(2,1)} %collective-permute-done), kind=kLoop, calls=%fused_computation.12 | loop fusion | flops 1572864 | bytes 4194304 | tf_op jit(solution)/shard_map/convert_element_type | solution.py:63
  15.4 14.6 %all-to-all-start = ((bf16[4,32,4096]{2,1,0:T(8,128)(2,1)}), bf16[4,32,4096]{2,1,0:T(8,128)(2,1)}, u32[]{:S(2)}, u32[]{:S(2)}) async-start(bf16[4,32,4096]{2,1,0:T(8,128)(2,1)} %bitcast.14), calls=%async_computation | async-start | bytes 2097152 | tf_op jit(solution)/shard_map/all_to_all | solution.py:15
  30.1 3.4 %convolution_convert_fusion = bf16[96,4096]{1,0:T(8,128)(2,1)} fusion(bf16[256,384]{0,1:T(8,128)(2,1)S(1)} %copy-done.7, bf16[256,4096]{1,0:T(8,128)(2,1)} %param.5, f32[4096]{0:T(1024)S(1)} %convert_element_type.82, f32[256]{0:T(256)S(1)} %add_rsqrt_fusion), kind=kOutput, calls=%fused_computation.3 | convolution fusion | flops 205914112 | bytes 2950144 | tf_op jit(solution)/shard_map/dot_general | solution.py:76
  33.5 1.7 %convolution_convert_fusion.1 = bf16[96,4096]{1,0:T(8,128)(2,1)} fusion(bf16[256,384]{0,1:T(8,128)(2,1)S(1)} %copy-done.7, bf16[256,4096]{1,0:T(8,128)(2,1)S(1)} %copy-done.3, f32[4096]{0:T(1024)S(1)} %convert_element_type.82, f32[256]{0:T(256)S(1)} %add_rsqrt_fusion), kind=kOutput, calls=%fused_computation.4 | convolution fusion | flops 205914112 | bytes 2950144 | tf_op jit(solution)/shard_map/dot_general | solution.py:76
  35.2 1.7 %convolution_convert_fusion.2 = bf16[96,4096]{1,0:T(8,128)(2,1)} fusion(bf16[256,384]{0,1:T(8,128)(2,1)S(1)} %copy-done.7, bf16[256,4096]{1,0:T(8,128)(2,1)S(1)} %copy-done.3, f32[4096]{0:T(1024)S(1)} %convert_element_type.82, f32[256]{0:T(256)S(1)} %add_rsqrt_fusion), kind=kOutput, calls=%fused_computation.5 | convolution fusion | flops 205914112 | bytes 2950144 | tf_op jit(solution)/shard_map/dot_general | solution.py:76
  37.5 1.1 copy-done.2
  39.8 3.5 %collective-permute-start.1 = (f32[8,4,128]{2,1,0:T(4,128)S(1)}, f32[8,4,128]{2,1,0:T(4,128)S(1)}, u32[]{:S(2)}, u32[]{:S(2)}) collective-permute-start(f32[8,4,128]{2,1,0:T(4,128)S(1)} %bitcast.16), channel_id=1, source_target_pairs={{0,32},{32,0},{64,96},{96,64},{128,160},{160,128},{192,224},{224,1... | collective-permute-start | bytes 49160 | tf_op jit(solution)/shard_map/ppermute | solution.py:28
  43.3 1.1 fusion.12
  44.4 1.0 collective-permute-done.1
  45.4 4.5 %collective-permute-start.2 = (f32[8,4,128]{2,1,0:T(4,128)S(1)}, f32[8,4,128]{2,1,0:T(4,128)S(1)}, u32[]{:S(2)}, u32[]{:S(2)}) collective-permute-start(f32[8,4,128]{2,1,0:T(4,128)S(1)} %add.211), channel_id=1, source_target_pairs={{0,64},{32,96},{64,0},{96,32},{128,192},{160,224},{192,128},{224,1... | collective-permute-start | bytes 49160 | tf_op jit(solution)/shard_map/ppermute | solution.py:28
  50.0 1.9 %collective-permute-done.2 = f32[8,4,128]{2,1,0:T(4,128)S(1)} collective-permute-done((f32[8,4,128]{2,1,0:T(4,128)S(1)}, f32[8,4,128]{2,1,0:T(4,128)S(1)}, u32[]{:S(2)}, u32[]{:S(2)}) %collective-permute-start.2) | collective-permute-done | bytes 16416 | tf_op jit(solution)/shard_map/ppermute | solution.py:28
  51.9 7.7 %collective-permute-start.3 = (f32[8,4,128]{2,1,0:T(4,128)S(1)}, f32[8,4,128]{2,1,0:T(4,128)S(1)}, u32[]{:S(2)}, u32[]{:S(2)}) collective-permute-start(f32[8,4,128]{2,1,0:T(4,128)S(1)} %add.212), channel_id=1, source_target_pairs={{0,128},{32,160},{64,192},{96,224},{128,0},{160,32},{192,64},{224,... | collective-permute-start | bytes 49160 | tf_op jit(solution)/shard_map/ppermute | solution.py:28
  59.7 3.5 %fusion.22 = f32[96,4096]{1,0:T(8,128)} fusion(bf16[256,384]{0,1:T(8,128)(2,1)S(1)} %copy-done.7, bf16[256,4096]{1,0:T(8,128)(2,1)} %param.5, f32[4096]{0:T(1024)S(1)} %convert_element_type.82, f32[256]{0:T(256)S(1)} %add_rsqrt_fusion), kind=kOutput, calls=%fused_computation.40 | convolution fusion | flops 205520896 | bytes 3736576 | tf_op jit(solution)/shard_map/dot_general | solution.py:76
  63.2 2.4 %collective-permute-start.4 = (bf16[96,4096]{1,0:T(8,128)(2,1)}, bf16[96,4096]{1,0:T(8,128)(2,1)}, u32[]{:S(2)}, u32[]{:S(2)}) collective-permute-start(bf16[96,4096]{1,0:T(8,128)(2,1)} %convolution_convert_fusion.2), channel_id=1, source_target_pairs={{0,8},{8,16},{16,24},{24,0},{1,9},{9,17},{17,25},{25,1},{2,10},{10... | collective-permute-start | bytes 2359304 | tf_op jit(solution)/shard_map/ppermute | solution.py:24
  65.6 4.3 %collective-permute-start.5 = (bf16[96,4096]{1,0:T(8,128)(2,1)}, bf16[96,4096]{1,0:T(8,128)(2,1)}, u32[]{:S(2)}, u32[]{:S(2)}) collective-permute-start(bf16[96,4096]{1,0:T(8,128)(2,1)} %convolution_convert_fusion.1), channel_id=1, source_target_pairs={{0,16},{8,24},{16,0},{24,8},{1,17},{9,25},{17,1},{25,9},{2,18},{10... | collective-permute-start | bytes 2359304 | tf_op jit(solution)/shard_map/ppermute | solution.py:24
  69.9 1.9 %collective-permute-start.6 = (bf16[96,4096]{1,0:T(8,128)(2,1)}, bf16[96,4096]{1,0:T(8,128)(2,1)}, u32[]{:S(2)}, u32[]{:S(2)}) collective-permute-start(bf16[96,4096]{1,0:T(8,128)(2,1)} %convolution_convert_fusion), channel_id=1, source_target_pairs={{0,24},{8,0},{16,8},{24,16},{1,25},{9,1},{17,9},{25,17},{2,26},{10... | collective-permute-start | bytes 2359304 | tf_op jit(solution)/shard_map/ppermute | solution.py:24
  71.9 1.4 convert_reduce_fusion
  73.3 1.2 fusion.7
  74.5 1.2 fusion.11
  75.8 1.9 %collective-permute-start.7 = (bf16[32,4096]{1,0:T(8,128)(2,1)S(1)}, bf16[32,4096]{1,0:T(8,128)(2,1)}, u32[]{:S(2)}, u32[]{:S(2)}) collective-permute-start(bf16[32,4096]{1,0:T(8,128)(2,1)S(1)} %fusion.11), channel_id=1, source_target_pairs={{0,1},{1,0},{2,3},{3,2},{4,5},{5,4},{6,7},{7,6},{8,9},{9,8},{10,11... | collective-permute-start | bytes 786440 | tf_op jit(solution)/shard_map/ppermute | solution.py:28
  77.7 5.7 %collective-permute-start.8 = (bf16[32,4096]{1,0:T(8,128)(2,1)S(1)}, bf16[32,4096]{1,0:T(8,128)(2,1)}, u32[]{:S(2)}, u32[]{:S(2)}) collective-permute-start(bf16[32,4096]{1,0:T(8,128)(2,1)S(1)} %fusion.11), channel_id=1, source_target_pairs={{0,2},{2,4},{4,6},{6,0},{1,3},{3,5},{5,7},{7,1},{8,10},{10,12},{12... | collective-permute-start | bytes 786440 | tf_op jit(solution)/shard_map/ppermute | solution.py:24
  84.1 10.4 %all-to-all-start.1 = ((f32[32,4,128]{2,1,0:T(4,128)}), f32[32,4,128]{2,1,0:T(4,128)S(1)}, u32[]{:S(2)}, u32[]{:S(2)}) async-start(f32[32,4,128]{2,1,0:T(4,128)} %broadcast_in_dim.6), calls=%async_computation.1 | async-start | bytes 131072 | tf_op jit(solution)/shard_map/all_to_all | solution.py:15
  94.5 9.7 %collective-permute-start.10 = (bf16[32,4096]{1,0:T(8,128)(2,1)S(1)}, bf16[32,4096]{1,0:T(8,128)(2,1)}, u32[]{:S(2)}, u32[]{:S(2)}) collective-permute-start(bf16[32,4096]{1,0:T(8,128)(2,1)S(1)} %fusion.11), channel_id=1, source_target_pairs={{0,4},{2,6},{4,0},{6,2},{1,5},{3,7},{5,1},{7,3},{8,12},{10,14},{12... | collective-permute-start | bytes 786440 | tf_op jit(solution)/shard_map/ppermute | solution.py:24
  104.2 1.9 %collective-permute-start.12 = (bf16[32,4096]{1,0:T(8,128)(2,1)S(1)}, bf16[32,4096]{1,0:T(8,128)(2,1)}, u32[]{:S(2)}, u32[]{:S(2)}) collective-permute-start(bf16[32,4096]{1,0:T(8,128)(2,1)S(1)} %fusion.11), channel_id=1, source_target_pairs={{0,6},{2,0},{4,2},{6,4},{1,7},{3,1},{5,3},{7,5},{8,14},{10,8},{12,... | collective-permute-start | bytes 786440 | tf_op jit(solution)/shard_map/ppermute | solution.py:24
  106.2 3.3 %add_convert_fusion.1 = bf16[96,4096]{1,0:T(8,128)(2,1)} fusion(f32[96,4096]{1,0:T(8,128)} %fusion.22, bf16[96,4096]{1,0:T(8,128)(2,1)} %collective-permute-done.6, bf16[96,4096]{1,0:T(8,128)(2,1)} %collective-permute-done.5, bf16[96,4096]{1,0:T(8,128)(2,1)} %collective-permute-done.4), kind=kLoop, calls=%fused_computation.14 | loop fusion | flops 2752512 | bytes 4718592 | tf_op jit(solution)/shard_map/convert_element_type | solution.py:106
  109.5 1.6 broadcast_in_dim.8
  111.8 2.4 %reshape.104 = bf16[24,4,4096]{2,1,0:T(4,128)(2,1)} reshape(bf16[96,4096]{1,0:T(8,128)(2,1)} %add_convert_fusion.1) | data formatting | bytes 1572864 | tf_op jit(solution)/shard_map/reshape | solution.py:106
  114.2 1.6 all-to-all-done.1
  115.8 2.4 %pad_maximum_fusion = bf16[24,4,4352]{2,1,0:T(4,128)(2,1)} fusion(bf16[24,4,256]{2,1,0:T(4,128)(2,1)S(1)} %broadcast_in_dim.7, bf16[24,4,4096]{2,1,0:T(4,128)(2,1)} %reshape.104), kind=kLoop, calls=%fused_computation.17 | loop fusion | flops 1671168 | bytes 1671168 | tf_op jit(solution)/shard_map/concatenate | solution.py:112
  118.3 8.1 %all-to-all-start.2 = ((bf16[24,4,4352]{2,1,0:T(4,128)(2,1)}), bf16[24,4,4352]{2,1,0:T(4,128)(2,1)}, u32[]{:S(2)}, u32[]{:S(2)}) async-start(bf16[24,4,4352]{2,1,0:T(4,128)(2,1)} %pad_maximum_fusion), calls=%async_computation.2 | async-start | bytes 1671168 | tf_op jit(solution)/shard_map/all_to_all | solution.py:15
  126.4 1.9 %collective-permute-start.9 = (bf16[32,4096]{1,0:T(8,128)(2,1)}, bf16[32,4096]{1,0:T(8,128)(2,1)S(1)}, u32[]{:S(2)}, u32[]{:S(2)}) collective-permute-start(bf16[32,4096]{1,0:T(8,128)(2,1)} %collective-permute-done.8), channel_id=1, source_target_pairs={{0,1},{1,0},{2,3},{3,2},{4,5},{5,4},{6,7},{7,6},{8,9},{9,8},{10,11... | collective-permute-start | bytes 786440 | tf_op jit(solution)/shard_map/ppermute | solution.py:28
  128.7 2.1 %collective-permute-start.11 = (bf16[32,4096]{1,0:T(8,128)(2,1)}, bf16[32,4096]{1,0:T(8,128)(2,1)S(1)}, u32[]{:S(2)}, u32[]{:S(2)}) collective-permute-start(bf16[32,4096]{1,0:T(8,128)(2,1)} %collective-permute-done.10), channel_id=1, source_target_pairs={{0,1},{1,0},{2,3},{3,2},{4,5},{5,4},{6,7},{7,6},{8,9},{9,8},{10,11... | collective-permute-start | bytes 786440 | tf_op jit(solution)/shard_map/ppermute | solution.py:28
  130.7 2.5 %collective-permute-done.12 = bf16[32,4096]{1,0:T(8,128)(2,1)} collective-permute-done((bf16[32,4096]{1,0:T(8,128)(2,1)S(1)}, bf16[32,4096]{1,0:T(8,128)(2,1)}, u32[]{:S(2)}, u32[]{:S(2)}) %collective-permute-start.12) | collective-permute-done | bytes 262176 | tf_op jit(solution)/shard_map/ppermute | solution.py:24
  133.3 1.9 %collective-permute-start.13 = (bf16[32,4096]{1,0:T(8,128)(2,1)}, bf16[32,4096]{1,0:T(8,128)(2,1)S(1)}, u32[]{:S(2)}, u32[]{:S(2)}) collective-permute-start(bf16[32,4096]{1,0:T(8,128)(2,1)} %collective-permute-done.12), channel_id=1, source_target_pairs={{0,1},{1,0},{2,3},{3,2},{4,5},{5,4},{6,7},{7,6},{8,9},{9,8},{10,11... | collective-permute-start | bytes 786440 | tf_op jit(solution)/shard_map/ppermute | solution.py:28
  135.2 1.7 %constant_dynamic-update-slice_fusion.6 = bf16[256,4096]{1,0:T(8,128)(2,1)} fusion(bf16[256,4096]{1,0:T(8,128)(2,1)} %constant_dynamic-update-slice_fusion.7, bf16[32,4096]{1,0:T(8,128)(2,1)} %collective-permute-done.7, s32[]{:T(128)S(6)} %select_n.84), kind=kLoop, calls=%fused_computation.49 | loop fusion | bytes 524292 | tf_op jit(solution)/shard_map/dynamic_update_slice | solution.py:124
  136.9 1.7 %constant_dynamic-update-slice_fusion.5 = bf16[256,4096]{1,0:T(8,128)(2,1)} fusion(bf16[256,4096]{1,0:T(8,128)(2,1)} %constant_dynamic-update-slice_fusion.6, bf16[32,4096]{1,0:T(8,128)(2,1)} %collective-permute-done.8, s32[]{:T(128)S(6)} %select_n.85), kind=kLoop, calls=%fused_computation.48 | loop fusion | bytes 524292 | tf_op jit(solution)/shard_map/dynamic_update_slice | solution.py:122
  138.5 0.7 constant_dynamic-update-slice_fusion.4
  139.3 1.7 %constant_dynamic-update-slice_fusion.3 = bf16[256,4096]{1,0:T(8,128)(2,1)} fusion(bf16[256,4096]{1,0:T(8,128)(2,1)} %constant_dynamic-update-slice_fusion.4, bf16[32,4096]{1,0:T(8,128)(2,1)} %collective-permute-done.10, s32[]{:T(128)S(6)} %select_n.87), kind=kLoop, calls=%fused_computation.46 | loop fusion | bytes 524292 | tf_op jit(solution)/shard_map/dynamic_update_slice | solution.py:122
  141.7 1.7 %constant_dynamic-update-slice_fusion.1 = bf16[256,4096]{1,0:T(8,128)(2,1)} fusion(bf16[256,4096]{1,0:T(8,128)(2,1)} %constant_dynamic-update-slice_fusion.2, bf16[32,4096]{1,0:T(8,128)(2,1)} %collective-permute-done.12, s32[]{:T(128)S(6)} %select_n.89), kind=kLoop, calls=%fused_computation.44 | loop fusion | bytes 524292 | tf_op jit(solution)/shard_map/dynamic_update_slice | solution.py:122
  144.0 9.2 %all-to-all-done.2 = bf16[24,4,4352]{2,1,0:T(4,128)(2,1)} async-done(((bf16[24,4,4352]{2,1,0:T(4,128)(2,1)}), bf16[24,4,4352]{2,1,0:T(4,128)(2,1)}, u32[]{:S(2)}, u32[]{:S(2)}) %all-to-all-start.2) | async-done | bytes 835616 | tf_op jit(solution)/shard_map/all_to_all | solution.py:15
  153.3 0.8 slice_convert_fusion
  154.7 2.1 %convert_reduce_fusion.1 = f32[4,4096]{1,0:T(4,128)} fusion(bf16[24,4,4352]{2,1,0:T(4,128)(2,1)} %all-to-all-done.2), kind=kLoop, calls=%fused_computation.13 | loop fusion | flops 770048 | bytes 851968 | tf_op jit(solution)/shard_map/reduce_sum | solution.py:19
  (47 shorter events, 5.7 us)
Async XLA Ops:
  0.6 1.9 %copy-start = (bf16[384,4096]{1,0:T(8,128)(2,1)S(1)}, bf16[384,4096]{1,0:T(8,128)(2,1)}, u32[]{:S(2)}) copy-start(bf16[384,4096]{1,0:T(8,128)(2,1)} %param.8) | copy-start | bytes 9437188
  2.5 5.2 %copy-start.5 = (bf16[256,384]{1,0:T(8,128)(2,1)S(1)}, bf16[256,384]{1,0:T(8,128)(2,1)}, u32[]{:S(2)}) copy-start(bf16[256,384]{1,0:T(8,128)(2,1)} %param.7) | copy-start | bytes 589828
  5.8 7.1 %collective-permute-start = (bf16[128,4096]{1,0:T(8,128)(2,1)}, bf16[128,4096]{1,0:T(8,128)(2,1)}, u32[]{:S(2)}, u32[]{:S(2)}) collective-permute-start(bf16[128,4096]{1,0:T(8,128)(2,1)} %get-tuple-element.27), channel_id=1, source_target_pairs={{0,1},{1,0},{2,3},{3,2},{4,5},{5,4},{6,7},{7,6},{8,9},{9,8},{10,11... | collective-permute-start | bytes 3145736 | tf_op jit(solution)/shard_map/ppermute | solution.py:28
  7.8 3.1 %copy-start.6 = (bf16[4096]{0:T(1024)(128)(2,1)S(1)}, bf16[4096]{0:T(1024)(128)(2,1)}, u32[]{:S(2)}) copy-start(bf16[4096]{0:T(1024)(128)(2,1)} %param.6) | copy-start | bytes 24580
  9.8 3.1 %copy-start.1 = (f32[128,4096]{1,0:T(8,128)S(1)}, f32[128,4096]{1,0:T(8,128)}, u32[]{:S(2)}) copy-start(f32[128,4096]{1,0:T(8,128)} %fusion.17) | copy-start | bytes 6291460
  15.4 14.6 %copy-start.7 = (bf16[256,384]{0,1:T(8,128)(2,1)S(1)}, bf16[256,384]{0,1:T(8,128)(2,1)}, u32[]{:S(2)}) copy-start(bf16[256,384]{0,1:T(8,128)(2,1)} %fusion.3) | copy-start | bytes 589828
  15.4 56.4 %all-to-all-start = ((bf16[4,32,4096]{2,1,0:T(8,128)(2,1)}), bf16[4,32,4096]{2,1,0:T(8,128)(2,1)}, u32[]{:S(2)}, u32[]{:S(2)}) async-start(bf16[4,32,4096]{2,1,0:T(8,128)(2,1)} %bitcast.14), calls=%async_computation | async-start | bytes 2097152 | tf_op jit(solution)/shard_map/all_to_all | solution.py:15
  30.1 3.4 %copy-start.3 = (bf16[256,4096]{1,0:T(8,128)(2,1)S(1)}, bf16[256,4096]{1,0:T(8,128)(2,1)}, u32[]{:S(2)}) copy-start(bf16[256,4096]{1,0:T(8,128)(2,1)} %param.5) | copy-start | bytes 6291460
  37.0 1.6 %copy-start.2 = (f32[128,4096]{1,0:T(8,128)S(1)}, f32[128,4096]{1,0:T(8,128)}, u32[]{:S(2)}) copy-start(f32[128,4096]{1,0:T(8,128)} %fusion.17) | copy-start | bytes 6291460
  37.0 2.2 %copy-start.4 = (f32[128,4096]{1,0:T(8,128)S(1)}, f32[128,4096]{1,0:T(8,128)}, u32[]{:S(2)}) copy-start(f32[128,4096]{1,0:T(8,128)} %get-tuple-element.28) | copy-start | bytes 6291460
  39.8 5.6 %collective-permute-start.1 = (f32[8,4,128]{2,1,0:T(4,128)S(1)}, f32[8,4,128]{2,1,0:T(4,128)S(1)}, u32[]{:S(2)}, u32[]{:S(2)}) collective-permute-start(f32[8,4,128]{2,1,0:T(4,128)S(1)} %bitcast.16), channel_id=1, source_target_pairs={{0,32},{32,0},{64,96},{96,64},{128,160},{160,128},{192,224},{224,1... | collective-permute-start | bytes 49160 | tf_op jit(solution)/shard_map/ppermute | solution.py:28
  45.4 6.5 %collective-permute-start.2 = (f32[8,4,128]{2,1,0:T(4,128)S(1)}, f32[8,4,128]{2,1,0:T(4,128)S(1)}, u32[]{:S(2)}, u32[]{:S(2)}) collective-permute-start(f32[8,4,128]{2,1,0:T(4,128)S(1)} %add.211), channel_id=1, source_target_pairs={{0,64},{32,96},{64,0},{96,32},{128,192},{160,224},{192,128},{224,1... | collective-permute-start | bytes 49160 | tf_op jit(solution)/shard_map/ppermute | solution.py:28
  51.9 19.9 %collective-permute-start.3 = (f32[8,4,128]{2,1,0:T(4,128)S(1)}, f32[8,4,128]{2,1,0:T(4,128)S(1)}, u32[]{:S(2)}, u32[]{:S(2)}) collective-permute-start(f32[8,4,128]{2,1,0:T(4,128)S(1)} %add.212), channel_id=1, source_target_pairs={{0,128},{32,160},{64,192},{96,224},{128,0},{160,32},{192,64},{224,... | collective-permute-start | bytes 49160 | tf_op jit(solution)/shard_map/ppermute | solution.py:28
  63.2 31.3 %collective-permute-start.4 = (bf16[96,4096]{1,0:T(8,128)(2,1)}, bf16[96,4096]{1,0:T(8,128)(2,1)}, u32[]{:S(2)}, u32[]{:S(2)}) collective-permute-start(bf16[96,4096]{1,0:T(8,128)(2,1)} %convolution_convert_fusion.2), channel_id=1, source_target_pairs={{0,8},{8,16},{16,24},{24,0},{1,9},{9,17},{17,25},{25,1},{2,10},{10... | collective-permute-start | bytes 2359304 | tf_op jit(solution)/shard_map/ppermute | solution.py:24
  65.6 38.6 %collective-permute-start.5 = (bf16[96,4096]{1,0:T(8,128)(2,1)}, bf16[96,4096]{1,0:T(8,128)(2,1)}, u32[]{:S(2)}, u32[]{:S(2)}) collective-permute-start(bf16[96,4096]{1,0:T(8,128)(2,1)} %convolution_convert_fusion.1), channel_id=1, source_target_pairs={{0,16},{8,24},{16,0},{24,8},{1,17},{9,25},{17,1},{25,9},{2,18},{10... | collective-permute-start | bytes 2359304 | tf_op jit(solution)/shard_map/ppermute | solution.py:24
  69.9 36.2 %collective-permute-start.6 = (bf16[96,4096]{1,0:T(8,128)(2,1)}, bf16[96,4096]{1,0:T(8,128)(2,1)}, u32[]{:S(2)}, u32[]{:S(2)}) collective-permute-start(bf16[96,4096]{1,0:T(8,128)(2,1)} %convolution_convert_fusion), channel_id=1, source_target_pairs={{0,24},{8,0},{16,8},{24,16},{1,25},{9,1},{17,9},{25,17},{2,26},{10... | collective-permute-start | bytes 2359304 | tf_op jit(solution)/shard_map/ppermute | solution.py:24
  75.8 59.4 %collective-permute-start.7 = (bf16[32,4096]{1,0:T(8,128)(2,1)S(1)}, bf16[32,4096]{1,0:T(8,128)(2,1)}, u32[]{:S(2)}, u32[]{:S(2)}) collective-permute-start(bf16[32,4096]{1,0:T(8,128)(2,1)S(1)} %fusion.11), channel_id=1, source_target_pairs={{0,1},{1,0},{2,3},{3,2},{4,5},{5,4},{6,7},{7,6},{8,9},{9,8},{10,11... | collective-permute-start | bytes 786440 | tf_op jit(solution)/shard_map/ppermute | solution.py:28
  77.7 48.7 %collective-permute-start.8 = (bf16[32,4096]{1,0:T(8,128)(2,1)S(1)}, bf16[32,4096]{1,0:T(8,128)(2,1)}, u32[]{:S(2)}, u32[]{:S(2)}) collective-permute-start(bf16[32,4096]{1,0:T(8,128)(2,1)S(1)} %fusion.11), channel_id=1, source_target_pairs={{0,2},{2,4},{4,6},{6,0},{1,3},{3,5},{5,7},{7,1},{8,10},{10,12},{12... | collective-permute-start | bytes 786440 | tf_op jit(solution)/shard_map/ppermute | solution.py:24
  84.1 31.7 %all-to-all-start.1 = ((f32[32,4,128]{2,1,0:T(4,128)}), f32[32,4,128]{2,1,0:T(4,128)S(1)}, u32[]{:S(2)}, u32[]{:S(2)}) async-start(f32[32,4,128]{2,1,0:T(4,128)} %broadcast_in_dim.6), calls=%async_computation.1 | async-start | bytes 131072 | tf_op jit(solution)/shard_map/all_to_all | solution.py:15
  94.5 34.2 %collective-permute-start.10 = (bf16[32,4096]{1,0:T(8,128)(2,1)S(1)}, bf16[32,4096]{1,0:T(8,128)(2,1)}, u32[]{:S(2)}, u32[]{:S(2)}) collective-permute-start(bf16[32,4096]{1,0:T(8,128)(2,1)S(1)} %fusion.11), channel_id=1, source_target_pairs={{0,4},{2,6},{4,0},{6,2},{1,5},{3,7},{5,1},{7,3},{8,12},{10,14},{12... | collective-permute-start | bytes 786440 | tf_op jit(solution)/shard_map/ppermute | solution.py:24
  104.2 29.0 %collective-permute-start.12 = (bf16[32,4096]{1,0:T(8,128)(2,1)S(1)}, bf16[32,4096]{1,0:T(8,128)(2,1)}, u32[]{:S(2)}, u32[]{:S(2)}) collective-permute-start(bf16[32,4096]{1,0:T(8,128)(2,1)S(1)} %fusion.11), channel_id=1, source_target_pairs={{0,6},{2,0},{4,2},{6,4},{1,7},{3,1},{5,3},{7,5},{8,14},{10,8},{12,... | collective-permute-start | bytes 786440 | tf_op jit(solution)/shard_map/ppermute | solution.py:24
  118.3 35.0 %all-to-all-start.2 = ((bf16[24,4,4352]{2,1,0:T(4,128)(2,1)}), bf16[24,4,4352]{2,1,0:T(4,128)(2,1)}, u32[]{:S(2)}, u32[]{:S(2)}) async-start(bf16[24,4,4352]{2,1,0:T(4,128)(2,1)} %pad_maximum_fusion), calls=%async_computation.2 | async-start | bytes 1671168 | tf_op jit(solution)/shard_map/all_to_all | solution.py:15
  126.4 12.1 %collective-permute-start.9 = (bf16[32,4096]{1,0:T(8,128)(2,1)}, bf16[32,4096]{1,0:T(8,128)(2,1)S(1)}, u32[]{:S(2)}, u32[]{:S(2)}) collective-permute-start(bf16[32,4096]{1,0:T(8,128)(2,1)} %collective-permute-done.8), channel_id=1, source_target_pairs={{0,1},{1,0},{2,3},{3,2},{4,5},{5,4},{6,7},{7,6},{8,9},{9,8},{10,11... | collective-permute-start | bytes 786440 | tf_op jit(solution)/shard_map/ppermute | solution.py:28
  128.7 12.3 %collective-permute-start.11 = (bf16[32,4096]{1,0:T(8,128)(2,1)}, bf16[32,4096]{1,0:T(8,128)(2,1)S(1)}, u32[]{:S(2)}, u32[]{:S(2)}) collective-permute-start(bf16[32,4096]{1,0:T(8,128)(2,1)} %collective-permute-done.10), channel_id=1, source_target_pairs={{0,1},{1,0},{2,3},{3,2},{4,5},{5,4},{6,7},{7,6},{8,9},{9,8},{10,11... | collective-permute-start | bytes 786440 | tf_op jit(solution)/shard_map/ppermute | solution.py:28
  133.3 10.1 %collective-permute-start.13 = (bf16[32,4096]{1,0:T(8,128)(2,1)}, bf16[32,4096]{1,0:T(8,128)(2,1)S(1)}, u32[]{:S(2)}, u32[]{:S(2)}) collective-permute-start(bf16[32,4096]{1,0:T(8,128)(2,1)} %collective-permute-done.12), channel_id=1, source_target_pairs={{0,1},{1,0},{2,3},{3,2},{4,5},{5,4},{6,7},{7,6},{8,9},{9,8},{10,11... | collective-permute-start | bytes 786440 | tf_op jit(solution)/shard_map/ppermute | solution.py:28
where the time goes:
time: 158 us; the launch traced here: 157 us
  starting transfers between devices  84.6 us (54%)
  other arithmetic  20.1 us (13%)
  local copies, waits for them, and re-layouts  17.8 us (11%)
  matrix products  16.7 us (11%)
  waiting for transfers between devices  16.6 us (11%)
    all_to_all x3, starting transfers between devices, exchange(): return lax.all_to_all(blocks, axes, 0, 0, tiled=True)  33.2 us
    ppermute x6, starting transfers between devices, shifted(): lax.ppermute(block, axis, [(i, (i + shift) % peers) for i in range(peers)])  26 us
    ppermute x8, starting transfers between devices, swapped(): lax.ppermute(block, axis, [(i, i ^ bit) for i in range(lax.axis_size(axis...  25.4 us
    all_to_all x3, waiting for transfers between devices, exchange(): return lax.all_to_all(blocks, axes, 0, 0, tiled=True)  10.8 us
    dot_general x4, matrix products, block(): lax.dot_general(columns, normed, (((0,), (0,)), ((), ())), preferred_elem...  10.4 us
    dynamic_update_slice x4, local copies, waits for them, and re-layouts, body(): lax.dynamic_update_slice_in_dim(result, piece, own_start + source, 0)  5.72 us
    dot_general x2, matrix products, term(): jnp.dot(rows_of(grad_q, start, half), w_query, preferred_element_type=F32)  5.36 us
    dynamic_update_slice x4, local copies, waits for them, and re-layouts, body(): lax.dynamic_update_slice_in_dim(result, piece, other_start + source, 0)  3.84 us
  transfers between devices with their start and end apart: 17, of which 6 were waited for; matrix products, arithmetic and copies ran while one was open for 27% of the time, Pallas kernels for 0%

commit v1 on v0

--- a/solution.py
+++ b/solution.py
@@ -54,35 +54,39 @@
         return lax.rsqrt(jnp.mean(rows_f * rows_f, axis=-1, keepdims=True) + 1e-05)
 
     def term(start):
-        return jnp.dot(rows_of(grad_q, start, half), w_query, preferred_element_type=F32)
+        rows = rows_of(grad_q, start, half)
+        return jnp.dot(rows, w_query, preferred_element_type=F32).astype(BF16)
+
+    inv = inverse(resid)
+    ordered = jnp.dot(grad_q, owner_columns(cols, lax.axis_index("x")), preferred_element_type=F32)
+    inv, ordered, grad_q = lax.optimization_barrier((inv, ordered.astype(BF16), grad_q))
 
     other_start, own_start = (1 - core) * half, core * half
     sent = term(other_start)
-    got = swapped(sent.astype(BF16), "c", 1)
+    got = swapped(sent, "c", 1)
     kept = lax.optimization_barrier(term(own_start))
-    pair = (kept + got.astype(F32)).astype(BF16)
-    inv = inverse(resid)
+    pair = (kept.astype(F32) + got.astype(F32)).astype(BF16)
     pair, inv = lax.optimization_barrier((pair, inv))
     dnormed = total(exchange(pair.reshape(n_zh, own, width), "zh"))
 
     unit = resid.astype(F32) * inv
     normed = (unit * gain_f).astype(BF16)
-    ordered = jnp.dot(grad_q, owner_columns(cols, lax.axis_index("x")), preferred_element_type=F32)
-    ordered = lax.optimization_barrier(ordered.astype(BF16))
     share = cols // n_x
 
-    def block(shift):
-        columns = ordered[:, shift * share : (shift + 1) * share]
+    def columns(shift):
+        return ordered[:, shift * share : (shift + 1) * share]
+
+    def block(columns):
         return lax.dot_general(
             columns, normed, (((0,), (0,)), ((), ())), preferred_element_type=F32
         )
 
-    blocks = [block(s).astype(BF16) for s in range(1, n_x)]
+    blocks = [block(columns(s)).astype(BF16) for s in range(1, n_x)]
     inv, *blocks = lax.optimization_barrier((inv, *blocks))
     by_x = [shifted(b, "x", s + 1) for s, b in enumerate(blocks)]
     unit = resid.astype(F32) * inv
-    part = jnp.sum(sent * rows_of(unit, other_start, half), axis=0)
-    part = part + jnp.sum(kept * rows_of(unit, own_start, half), axis=0)
+    part = jnp.sum(sent.astype(F32) * rows_of(unit, other_start, half), axis=0)
+    part = part + jnp.sum(kept.astype(F32) * rows_of(unit, own_start, half), axis=0)
     part = part.reshape(n_y, -1, 128)
     for bit in (1, 2, 4):
         part = part + swapped(part, "y", bit)
@@ -94,14 +98,14 @@
 
     first = own_start + zh * own
     resid_rows = rows_of(resid, first, own)
-    inv_rows = inverse(resid_rows)
+    inv_rows = rows_of(inv, first, own)
     unit_rows = resid_rows.astype(F32) * inv_rows
     dunit = dnormed * gain_f
     inner = jnp.mean(dunit * unit_rows, axis=-1, keepdims=True)
     rows = rows_of(grad_in, first, own).astype(F32) + inv_rows * (dunit - unit_rows * inner)
-    first_block, rows = lax.optimization_barrier((block(0), rows.astype(BF16)))
+    own_columns, rows = lax.optimization_barrier((columns(0), rows.astype(BF16)))
 
-    by_x = first_block + sum(b.astype(F32) for b in by_x)
+    by_x = block(own_columns) + sum(b.astype(F32) for b in by_x)
     mine = share // (n_y * n_zl)
     by_x = by_x.astype(BF16).reshape(n_zl * n_y, mine, width)
 
@@ -116,12 +120,12 @@
     gain_grad = jnp.sum(parts, axis=0).reshape(-1)
 
     result = jnp.zeros((tokens, width), BF16)
-    for shift in range(n_zh):
+    for shift in (0, 1, n_zh - 1, 2):
         piece = rows if shift == 0 else shifted(rows, "zh", shift)
+        other = swapped(piece, "c", 1)
         source = lax.rem(zh + n_zh - shift, n_zh) * own
         result = lax.dynamic_update_slice_in_dim(result, piece, own_start + source, 0)
-        piece = swapped(piece, "c", 1)
-        result = lax.dynamic_update_slice_in_dim(result, piece, other_start + source, 0)
+        result = lax.dynamic_update_slice_in_dim(result, other, other_start + source, 0)
     return weight_grad, gain_grad, result
 
 

time: 158 us -> 151 us (0.956)
  the two profiles are of different devices: /device:TPU:6 before, /device:TPU:81 now
where the time goes in v1:
time: 151 us; the launch traced here: 149 us
  starting transfers between devices  81.4 us (54%)
  waiting for transfers between devices  21.3 us (14%)
  other arithmetic  17 us (11%)
  local copies, waits for them, and re-layouts  14.9 us (10%)
  matrix products  13.8 us (9%)
    all_to_all x3, starting transfers between devices, exchange(): return lax.all_to_all(blocks, axes, 0, 0, tiled=True)  27.7 us
    ppermute x8, starting transfers between devices, swapped(): lax.ppermute(block, axis, [(i, i ^ bit) for i in range(lax.axis_size(axis...  27.3 us
    ppermute x6, starting transfers between devices, shifted(): lax.ppermute(block, axis, [(i, (i + shift) % peers) for i in range(peers)])  26.3 us
    dot_general x4, matrix products, block(): lax.dot_general(columns, normed, (((0,), (0,)), ((), ())), preferred_elem...  10.4 us
    ppermute x6, waiting for transfers between devices, shifted(): lax.ppermute(block, axis, [(i, (i + shift) % peers) for i in range(peers)])  9.9 us
    ppermute x8, waiting for transfers between devices, swapped(): lax.ppermute(block, axis, [(i, i ^ bit) for i in range(lax.axis_size(axis...  7.25 us
    dynamic_update_slice x4, local copies, waits for them, and re-layouts, body(): lax.dynamic_update_slice_in_dim(result, piece, own_start + source, 0)  5.72 us
    all_to_all x3, waiting for transfers between devices, exchange(): return lax.all_to_all(blocks, axes, 0, 0, tiled=True)  4.17 us
  transfers between devices with their start and end apart: 17, of which 6 were waited for; matrix products, arithmetic and copies ran while one was open for 23% of the time, Pallas kernels for 0%

profile of v1, /device:TPU:81, one launch (start us, length us, event | category | flops | bytes accessed | tf_op | source)
XLA Modules:
  0.0 149.5 jit_solution(12508162205986257340)
XLA Ops:
  0.7 2.3 %fusion = f32[256]{0:T(256)S(1)} fusion(bf16[256,4096]{1,0:T(8,128)(2,1)} %param.5), kind=kLoop, calls=%fused_computation.8 | loop fusion | flops 3145472 | bytes 2098176 | tf_op jit(solution)/shard_map/reduce_sum | solution.py:54
  3.0 1.0 fusion.5
  4.0 1.7 %convolution_convert_fusion = bf16[128,4096]{1,0:T(8,128)(2,1)} fusion(bf16[384,4096]{1,0:T(8,128)(2,1)S(1)} %copy-done, bf16[256,384]{1,0:T(8,128)(2,1)S(1)} %copy-done.5, s32[]{:T(128)S(6)} %select_n.82), kind=kOutput, calls=%fused_computation.3 | convolution fusion | flops 403177472 | bytes 4292612 | tf_op jit(solution)/shard_map/dot_general | solution.py:58
  5.7 2.6 %collective-permute-start = (bf16[128,4096]{1,0:T(8,128)(2,1)}, bf16[128,4096]{1,0:T(8,128)(2,1)}, u32[]{:S(2)}, u32[]{:S(2)}) collective-permute-start(bf16[128,4096]{1,0:T(8,128)(2,1)} %convolution_convert_fusion), channel_id=1, source_target_pairs={{0,1},{1,0},{2,3},{3,2},{4,5},{5,4},{6,7},{7,6},{8,9},{9,8},{10,11... | collective-permute-start | bytes 3145736 | tf_op jit(solution)/shard_map/ppermute | solution.py:28
  9.1 1.8 %collective-permute-done = bf16[128,4096]{1,0:T(8,128)(2,1)} collective-permute-done((bf16[128,4096]{1,0:T(8,128)(2,1)}, bf16[128,4096]{1,0:T(8,128)(2,1)}, u32[]{:S(2)}, u32[]{:S(2)}) %collective-permute-start) | collective-permute-done | bytes 1048608 | tf_op jit(solution)/shard_map/ppermute | solution.py:28
  10.9 2.4 %fusion.3 = bf16[128,4096]{1,0:T(8,128)(2,1)} fusion(bf16[128,4096]{1,0:T(8,128)(2,1)S(1)} %convolution_convert_fusion.1, bf16[128,4096]{1,0:T(8,128)(2,1)} %collective-permute-done), kind=kLoop, calls=%fused_computation.13 | loop fusion | flops 2097152 | bytes 3145728 | tf_op jit(solution)/shard_map/convert_element_type | solution.py:68
  13.3 13.3 %all-to-all-start = ((bf16[4,32,4096]{2,1,0:T(8,128)(2,1)}), bf16[4,32,4096]{2,1,0:T(8,128)(2,1)}, u32[]{:S(2)}, u32[]{:S(2)}) async-start(bf16[4,32,4096]{2,1,0:T(8,128)(2,1)} %bitcast.17), calls=%async_computation | async-start | bytes 2097152 | tf_op jit(solution)/shard_map/all_to_all | solution.py:15
  26.6 3.4 %convolution_convert_fusion.2 = bf16[96,4096]{1,0:T(8,128)(2,1)} fusion(bf16[256,384]{0,1:T(8,128)(2,1)S(1)} %copy-done.6, bf16[256,4096]{1,0:T(8,128)(2,1)} %param.5, f32[4096]{0:T(1024)S(1)} %convert_element_type.94, f32[256]{0:T(256)S(1)} %add_rsqrt_fusion), kind=kOutput, calls=%fused_computation.5 | convolution fusion | flops 205914112 | bytes 2950144 | tf_op jit(solution)/shard_map/dot_general | solution.py:80
  30.1 1.7 %convolution_convert_fusion.3 = bf16[96,4096]{1,0:T(8,128)(2,1)} fusion(bf16[256,384]{0,1:T(8,128)(2,1)S(1)} %copy-done.6, bf16[256,4096]{1,0:T(8,128)(2,1)S(1)} %copy-done.1, f32[4096]{0:T(1024)S(1)} %convert_element_type.94, f32[256]{0:T(256)S(1)} %add_rsqrt_fusion), kind=kOutput, calls=%fused_computation.6 | convolution fusion | flops 205914112 | bytes 2950144 | tf_op jit(solution)/shard_map/dot_general | solution.py:80
  31.8 1.7 %convolution_convert_fusion.4 = bf16[96,4096]{1,0:T(8,128)(2,1)} fusion(bf16[256,384]{0,1:T(8,128)(2,1)S(1)} %copy-done.6, bf16[256,4096]{1,0:T(8,128)(2,1)S(1)} %copy-done.1, f32[4096]{0:T(1024)S(1)} %convert_element_type.94, f32[256]{0:T(256)S(1)} %add_rsqrt_fusion), kind=kOutput, calls=%fused_computation.7 | convolution fusion | flops 205914112 | bytes 2950144 | tf_op jit(solution)/shard_map/dot_general | solution.py:80
  34.7 1.8 %fusion.4 = (f32[4096]{0:T(1024)S(1)}, f32[4096]{0:T(1024)S(1)}) fusion(bf16[128,4096]{1,0:T(8,128)(2,1)S(1)} %copy-done.4, f32[256,4096]{1,0:T(8,128)S(1)} %convert_multiply_fusion, s32[]{:T(128)S(6)} %select_n.81, s32[]{:T(128)S(6)} %select_n.82, bf16[128,4096]{1,0:T(8,128)(2,1)} %convolution_convert_fusion), kind=kLoop, calls=%fused_computation.14 | loop fusion | flops 3137536 | bytes 6324232 | tf_op jit(solution)/shard_map/reduce_sum | solution.py:89
  36.6 3.2 %collective-permute-start.1 = (f32[8,4,128]{2,1,0:T(4,128)S(1)}, f32[8,4,128]{2,1,0:T(4,128)S(1)}, u32[]{:S(2)}, u32[]{:S(2)}) collective-permute-start(f32[8,4,128]{2,1,0:T(4,128)S(1)} %bitcast.19), channel_id=1, source_target_pairs={{0,32},{32,0},{64,96},{96,64},{128,160},{160,128},{192,224},{224,1... | collective-permute-start | bytes 49160 | tf_op jit(solution)/shard_map/ppermute | solution.py:28
  39.8 1.7 %collective-permute-done.1 = f32[8,4,128]{2,1,0:T(4,128)S(1)} collective-permute-done((f32[8,4,128]{2,1,0:T(4,128)S(1)}, f32[8,4,128]{2,1,0:T(4,128)S(1)}, u32[]{:S(2)}, u32[]{:S(2)}) %collective-permute-start.1) | collective-permute-done | bytes 16416 | tf_op jit(solution)/shard_map/ppermute | solution.py:28
  41.4 2.0 %collective-permute-start.2 = (f32[8,4,128]{2,1,0:T(4,128)S(1)}, f32[8,4,128]{2,1,0:T(4,128)S(1)}, u32[]{:S(2)}, u32[]{:S(2)}) collective-permute-start(f32[8,4,128]{2,1,0:T(4,128)S(1)} %add.199), channel_id=1, source_target_pairs={{0,64},{32,96},{64,0},{96,32},{128,192},{160,224},{192,128},{224,1... | collective-permute-start | bytes 49160 | tf_op jit(solution)/shard_map/ppermute | solution.py:28
  43.5 3.7 %collective-permute-done.2 = f32[8,4,128]{2,1,0:T(4,128)S(1)} collective-permute-done((f32[8,4,128]{2,1,0:T(4,128)S(1)}, f32[8,4,128]{2,1,0:T(4,128)S(1)}, u32[]{:S(2)}, u32[]{:S(2)}) %collective-permute-start.2) | collective-permute-done | bytes 16416 | tf_op jit(solution)/shard_map/ppermute | solution.py:28
  47.2 5.6 %collective-permute-start.3 = (f32[8,4,128]{2,1,0:T(4,128)S(1)}, f32[8,4,128]{2,1,0:T(4,128)S(1)}, u32[]{:S(2)}, u32[]{:S(2)}) collective-permute-start(f32[8,4,128]{2,1,0:T(4,128)S(1)} %add.200), channel_id=1, source_target_pairs={{0,128},{32,160},{64,192},{96,224},{128,0},{160,32},{192,64},{224,... | collective-permute-start | bytes 49160 | tf_op jit(solution)/shard_map/ppermute | solution.py:28
  53.0 3.1 %collective-permute-start.4 = (bf16[96,4096]{1,0:T(8,128)(2,1)}, bf16[96,4096]{1,0:T(8,128)(2,1)}, u32[]{:S(2)}, u32[]{:S(2)}) collective-permute-start(bf16[96,4096]{1,0:T(8,128)(2,1)} %convolution_convert_fusion.4), channel_id=1, source_target_pairs={{0,8},{8,16},{16,24},{24,0},{1,9},{9,17},{17,25},{25,1},{2,10},{10... | collective-permute-start | bytes 2359304 | tf_op jit(solution)/shard_map/ppermute | solution.py:24
  56.1 4.4 %collective-permute-start.5 = (bf16[96,4096]{1,0:T(8,128)(2,1)}, bf16[96,4096]{1,0:T(8,128)(2,1)}, u32[]{:S(2)}, u32[]{:S(2)}) collective-permute-start(bf16[96,4096]{1,0:T(8,128)(2,1)} %convolution_convert_fusion.3), channel_id=1, source_target_pairs={{0,16},{8,24},{16,0},{24,8},{1,17},{9,25},{17,1},{25,9},{2,18},{10... | collective-permute-start | bytes 2359304 | tf_op jit(solution)/shard_map/ppermute | solution.py:24
  60.4 3.1 %collective-permute-start.6 = (bf16[96,4096]{1,0:T(8,128)(2,1)}, bf16[96,4096]{1,0:T(8,128)(2,1)}, u32[]{:S(2)}, u32[]{:S(2)}) collective-permute-start(bf16[96,4096]{1,0:T(8,128)(2,1)} %convolution_convert_fusion.2), channel_id=1, source_target_pairs={{0,24},{8,0},{16,8},{24,16},{1,25},{9,1},{17,9},{25,17},{2,26},{10... | collective-permute-start | bytes 2359304 | tf_op jit(solution)/shard_map/ppermute | solution.py:24
  63.5 4.2 %all-to-all-done = bf16[4,32,4096]{2,1,0:T(8,128)(2,1)} async-done(((bf16[4,32,4096]{2,1,0:T(8,128)(2,1)}), bf16[4,32,4096]{2,1,0:T(8,128)(2,1)}, u32[]{:S(2)}, u32[]{:S(2)}) %all-to-all-start) | async-done | bytes 1048608 | tf_op jit(solution)/shard_map/all_to_all | solution.py:15
  67.7 1.4 convert_reduce_fusion
  69.1 1.2 multiply_reduce_fusion.1
  70.4 1.2 add_convert_fusion.1
  71.6 3.4 %collective-permute-start.7 = (bf16[32,4096]{1,0:T(8,128)(2,1)S(1)}, bf16[32,4096]{1,0:T(8,128)(2,1)}, u32[]{:S(2)}, u32[]{:S(2)}) collective-permute-start(bf16[32,4096]{1,0:T(8,128)(2,1)S(1)} %add_convert_fusion.1), channel_id=1, source_target_pairs={{0,1},{1,0},{2,3},{3,2},{4,5},{5,4},{6,7},{7,6},{8,9},{9,8},{10,11... | collective-permute-start | bytes 786440 | tf_op jit(solution)/shard_map/ppermute | solution.py:28
  75.0 4.3 %collective-permute-start.8 = (bf16[32,4096]{1,0:T(8,128)(2,1)S(1)}, bf16[32,4096]{1,0:T(8,128)(2,1)}, u32[]{:S(2)}, u32[]{:S(2)}) collective-permute-start(bf16[32,4096]{1,0:T(8,128)(2,1)S(1)} %add_convert_fusion.1), channel_id=1, source_target_pairs={{0,2},{2,4},{4,6},{6,0},{1,3},{3,5},{5,7},{7,1},{8,10},{10,12},{12... | collective-permute-start | bytes 786440 | tf_op jit(solution)/shard_map/ppermute | solution.py:24
  79.9 6.5 %all-to-all-start.1 = ((f32[32,4,128]{2,1,0:T(4,128)}), f32[32,4,128]{2,1,0:T(4,128)S(1)}, u32[]{:S(2)}, u32[]{:S(2)}) async-start(f32[32,4,128]{2,1,0:T(4,128)} %broadcast_in_dim.6), calls=%async_computation.1 | async-start | bytes 131072 | tf_op jit(solution)/shard_map/all_to_all | solution.py:15
  86.5 1.6 %broadcast_in_dim.8 = bf16[256,4096]{1,0:T(8,128)(2,1)} broadcast(bf16[]{:T(256)} %constant.105.clone.1), dimensions={} | broadcast | bytes 2097154 | tf_op jit(solution)/shard_map/broadcast_in_dim | solution.py:122
  88.0 0.7 constant_dynamic-update-slice_fusion.7
  88.8 6.3 %collective-permute-start.10 = (bf16[32,4096]{1,0:T(8,128)(2,1)S(1)}, bf16[32,4096]{1,0:T(8,128)(2,1)}, u32[]{:S(2)}, u32[]{:S(2)}) collective-permute-start(bf16[32,4096]{1,0:T(8,128)(2,1)S(1)} %add_convert_fusion.1), channel_id=1, source_target_pairs={{0,6},{2,0},{4,2},{6,4},{1,7},{3,1},{5,3},{7,5},{8,14},{10,8},{12,... | collective-permute-start | bytes 786440 | tf_op jit(solution)/shard_map/ppermute | solution.py:24
  95.0 5.2 %collective-permute-start.12 = (bf16[32,4096]{1,0:T(8,128)(2,1)S(1)}, bf16[32,4096]{1,0:T(8,128)(2,1)}, u32[]{:S(2)}, u32[]{:S(2)}) collective-permute-start(bf16[32,4096]{1,0:T(8,128)(2,1)S(1)} %add_convert_fusion.1), channel_id=1, source_target_pairs={{0,4},{2,6},{4,0},{6,2},{1,5},{3,7},{5,1},{7,3},{8,12},{10,14},{12... | collective-permute-start | bytes 786440 | tf_op jit(solution)/shard_map/ppermute | solution.py:24
  100.3 3.5 %add_convert_fusion = bf16[96,4096]{1,0:T(8,128)(2,1)} fusion(bf16[96,4096]{1,0:T(8,128)(2,1)} %collective-permute-done.6, bf16[96,4096]{1,0:T(8,128)(2,1)} %collective-permute-done.5, bf16[96,4096]{1,0:T(8,128)(2,1)} %collective-permute-done.4, bf16[256,96]{0,1:T(8,128)(2,1)S(1)} %slice-done, bf16[256,4096]{1,0:T(8,128)(2,1)S(1)} %copy-done.2, ...), kind=kOutput, calls=%fused_computation.18 | convolution fusion | flops 208273408 | bytes 5309440 | tf_op jit(solution)/shard_map/dot_general | solution.py:80
  103.8 2.4 %reshape.96 = bf16[24,4,4096]{2,1,0:T(4,128)(2,1)} reshape(bf16[96,4096]{1,0:T(8,128)(2,1)} %add_convert_fusion) | data formatting | bytes 1572864 | tf_op jit(solution)/shard_map/reshape | solution.py:110
  106.3 2.4 %pad_maximum_fusion = bf16[24,4,4352]{2,1,0:T(4,128)(2,1)} fusion(bf16[24,4,256]{2,1,0:T(4,128)(2,1)S(1)} %broadcast_in_dim.7, bf16[24,4,4096]{2,1,0:T(4,128)(2,1)} %reshape.96), kind=kLoop, calls=%fused_computation.21 | loop fusion | flops 1671168 | bytes 1671168 | tf_op jit(solution)/shard_map/concatenate | solution.py:116
  108.7 7.9 %all-to-all-start.2 = ((bf16[24,4,4352]{2,1,0:T(4,128)(2,1)}), bf16[24,4,4352]{2,1,0:T(4,128)(2,1)}, u32[]{:S(2)}, u32[]{:S(2)}) async-start(bf16[24,4,4352]{2,1,0:T(4,128)(2,1)} %pad_maximum_fusion), calls=%async_computation.2 | async-start | bytes 1671168 | tf_op jit(solution)/shard_map/all_to_all | solution.py:15
  116.6 4.7 %collective-permute-start.9 = (bf16[32,4096]{1,0:T(8,128)(2,1)}, bf16[32,4096]{1,0:T(8,128)(2,1)S(1)}, u32[]{:S(2)}, u32[]{:S(2)}) collective-permute-start(bf16[32,4096]{1,0:T(8,128)(2,1)} %collective-permute-done.8), channel_id=1, source_target_pairs={{0,1},{1,0},{2,3},{3,2},{4,5},{5,4},{6,7},{7,6},{8,9},{9,8},{10,11... | collective-permute-start | bytes 786440 | tf_op jit(solution)/shard_map/ppermute | solution.py:28
  121.3 0.7 collective-permute-done.10
  122.0 2.4 %collective-permute-start.11 = (bf16[32,4096]{1,0:T(8,128)(2,1)}, bf16[32,4096]{1,0:T(8,128)(2,1)S(1)}, u32[]{:S(2)}, u32[]{:S(2)}) collective-permute-start(bf16[32,4096]{1,0:T(8,128)(2,1)} %collective-permute-done.10), channel_id=1, source_target_pairs={{0,1},{1,0},{2,3},{3,2},{4,5},{5,4},{6,7},{7,6},{8,9},{9,8},{10,11... | collective-permute-start | bytes 786440 | tf_op jit(solution)/shard_map/ppermute | solution.py:28
  124.4 9.2 %collective-permute-done.12 = bf16[32,4096]{1,0:T(8,128)(2,1)} collective-permute-done((bf16[32,4096]{1,0:T(8,128)(2,1)S(1)}, bf16[32,4096]{1,0:T(8,128)(2,1)}, u32[]{:S(2)}, u32[]{:S(2)}) %collective-permute-start.12) | collective-permute-done | bytes 262176 | tf_op jit(solution)/shard_map/ppermute | solution.py:24
  133.5 3.5 %collective-permute-start.13 = (bf16[32,4096]{1,0:T(8,128)(2,1)}, bf16[32,4096]{1,0:T(8,128)(2,1)S(1)}, u32[]{:S(2)}, u32[]{:S(2)}) collective-permute-start(bf16[32,4096]{1,0:T(8,128)(2,1)} %collective-permute-done.12), channel_id=1, source_target_pairs={{0,1},{1,0},{2,3},{3,2},{4,5},{5,4},{6,7},{7,6},{8,9},{9,8},{10,11... | collective-permute-start | bytes 786440 | tf_op jit(solution)/shard_map/ppermute | solution.py:28
  137.1 1.7 %constant_dynamic-update-slice_fusion.6 = bf16[256,4096]{1,0:T(8,128)(2,1)} fusion(bf16[256,4096]{1,0:T(8,128)(2,1)} %constant_dynamic-update-slice_fusion.7, bf16[32,4096]{1,0:T(8,128)(2,1)} %collective-permute-done.7, s32[]{:T(128)S(6)} %select_n.85), kind=kLoop, calls=%fused_computation.42 | loop fusion | bytes 524292 | tf_op jit(solution)/shard_map/dynamic_update_slice | solution.py:128
  138.7 1.7 %constant_dynamic-update-slice_fusion.5 = bf16[256,4096]{1,0:T(8,128)(2,1)} fusion(bf16[256,4096]{1,0:T(8,128)(2,1)} %constant_dynamic-update-slice_fusion.6, bf16[32,4096]{1,0:T(8,128)(2,1)} %collective-permute-done.8, s32[]{:T(128)S(6)} %select_n.86), kind=kLoop, calls=%fused_computation.41 | loop fusion | bytes 524292 | tf_op jit(solution)/shard_map/dynamic_update_slice | solution.py:127
  140.4 0.7 constant_dynamic-update-slice_fusion.4
  141.1 1.7 %constant_dynamic-update-slice_fusion.3 = bf16[256,4096]{1,0:T(8,128)(2,1)} fusion(bf16[256,4096]{1,0:T(8,128)(2,1)} %constant_dynamic-update-slice_fusion.4, bf16[32,4096]{1,0:T(8,128)(2,1)} %collective-permute-done.10, s32[]{:T(128)S(6)} %select_n.88), kind=kLoop, calls=%fused_computation.39 | loop fusion | bytes 524292 | tf_op jit(solution)/shard_map/dynamic_update_slice | solution.py:127
  142.8 0.7 constant_dynamic-update-slice_fusion.2
  143.5 1.7 %constant_dynamic-update-slice_fusion.1 = bf16[256,4096]{1,0:T(8,128)(2,1)} fusion(bf16[256,4096]{1,0:T(8,128)(2,1)} %constant_dynamic-update-slice_fusion.2, bf16[32,4096]{1,0:T(8,128)(2,1)} %collective-permute-done.12, s32[]{:T(128)S(6)} %select_n.90), kind=kLoop, calls=%fused_computation.37 | loop fusion | bytes 524292 | tf_op jit(solution)/shard_map/dynamic_update_slice | solution.py:127
  145.2 0.7 constant_dynamic-update-slice_fusion
  145.9 0.8 slice_convert_fusion
  147.4 2.1 %convert_reduce_fusion.1 = f32[4,4096]{1,0:T(4,128)} fusion(bf16[24,4,4352]{2,1,0:T(4,128)(2,1)} %all-to-all-done.2), kind=kLoop, calls=%fused_computation.17 | loop fusion | flops 770048 | bytes 851968 | tf_op jit(solution)/shard_map/reduce_sum | solution.py:19
  (47 shorter events, 3.5 us)
Async XLA Ops:
  0.6 3.4 %copy-start = (bf16[384,4096]{1,0:T(8,128)(2,1)S(1)}, bf16[384,4096]{1,0:T(8,128)(2,1)}, u32[]{:S(2)}) copy-start(bf16[384,4096]{1,0:T(8,128)(2,1)} %param.8) | copy-start | bytes 9437188
  0.6 2.3 %copy-start.5 = (bf16[256,384]{1,0:T(8,128)(2,1)S(1)}, bf16[256,384]{1,0:T(8,128)(2,1)}, u32[]{:S(2)}) copy-start(bf16[256,384]{1,0:T(8,128)(2,1)} %param.7) | copy-start | bytes 589828
  5.7 5.2 %collective-permute-start = (bf16[128,4096]{1,0:T(8,128)(2,1)}, bf16[128,4096]{1,0:T(8,128)(2,1)}, u32[]{:S(2)}, u32[]{:S(2)}) collective-permute-start(bf16[128,4096]{1,0:T(8,128)(2,1)} %convolution_convert_fusion), channel_id=1, source_target_pairs={{0,1},{1,0},{2,3},{3,2},{4,5},{5,4},{6,7},{7,6},{8,9},{9,8},{10,11... | collective-permute-start | bytes 3145736 | tf_op jit(solution)/shard_map/ppermute | solution.py:28
  8.3 0.7 copy-start.7
  9.0 1.9 %copy-start.3 = (bf16[128,4096]{1,0:T(8,128)(2,1)}, bf16[128,4096]{1,0:T(8,128)(2,1)S(1)}, u32[]{:S(2)}) copy-start(bf16[128,4096]{1,0:T(8,128)(2,1)S(1)} %convolution_convert_fusion.1) | copy-start | bytes 3145732
  9.0 17.6 %copy-start.6 = (bf16[256,384]{0,1:T(8,128)(2,1)S(1)}, bf16[256,384]{0,1:T(8,128)(2,1)}, u32[]{:S(2)}) copy-start(bf16[256,384]{0,1:T(8,128)(2,1)} %fusion.5) | copy-start | bytes 589828
  13.3 54.4 %all-to-all-start = ((bf16[4,32,4096]{2,1,0:T(8,128)(2,1)}), bf16[4,32,4096]{2,1,0:T(8,128)(2,1)}, u32[]{:S(2)}, u32[]{:S(2)}) async-start(bf16[4,32,4096]{2,1,0:T(8,128)(2,1)} %bitcast.17), calls=%async_computation | async-start | bytes 2097152 | tf_op jit(solution)/shard_map/all_to_all | solution.py:15
  26.6 3.4 %copy-start.1 = (bf16[256,4096]{1,0:T(8,128)(2,1)S(1)}, bf16[256,4096]{1,0:T(8,128)(2,1)}, u32[]{:S(2)}) copy-start(bf16[256,4096]{1,0:T(8,128)(2,1)} %param.5) | copy-start | bytes 6291460
  33.5 1.2 copy-start.4
  36.6 4.9 %collective-permute-start.1 = (f32[8,4,128]{2,1,0:T(4,128)S(1)}, f32[8,4,128]{2,1,0:T(4,128)S(1)}, u32[]{:S(2)}, u32[]{:S(2)}) collective-permute-start(f32[8,4,128]{2,1,0:T(4,128)S(1)} %bitcast.19), channel_id=1, source_target_pairs={{0,32},{32,0},{64,96},{96,64},{128,160},{160,128},{192,224},{224,1... | collective-permute-start | bytes 49160 | tf_op jit(solution)/shard_map/ppermute | solution.py:28
  41.4 5.8 %collective-permute-start.2 = (f32[8,4,128]{2,1,0:T(4,128)S(1)}, f32[8,4,128]{2,1,0:T(4,128)S(1)}, u32[]{:S(2)}, u32[]{:S(2)}) collective-permute-start(f32[8,4,128]{2,1,0:T(4,128)S(1)} %add.199), channel_id=1, source_target_pairs={{0,64},{32,96},{64,0},{96,32},{128,192},{160,224},{192,128},{224,1... | collective-permute-start | bytes 49160 | tf_op jit(solution)/shard_map/ppermute | solution.py:28
  47.2 16.3 %collective-permute-start.3 = (f32[8,4,128]{2,1,0:T(4,128)S(1)}, f32[8,4,128]{2,1,0:T(4,128)S(1)}, u32[]{:S(2)}, u32[]{:S(2)}) collective-permute-start(f32[8,4,128]{2,1,0:T(4,128)S(1)} %add.200), channel_id=1, source_target_pairs={{0,128},{32,160},{64,192},{96,224},{128,0},{160,32},{192,64},{224,... | collective-permute-start | bytes 49160 | tf_op jit(solution)/shard_map/ppermute | solution.py:28
  53.0 35.8 %collective-permute-start.4 = (bf16[96,4096]{1,0:T(8,128)(2,1)}, bf16[96,4096]{1,0:T(8,128)(2,1)}, u32[]{:S(2)}, u32[]{:S(2)}) collective-permute-start(bf16[96,4096]{1,0:T(8,128)(2,1)} %convolution_convert_fusion.4), channel_id=1, source_target_pairs={{0,8},{8,16},{16,24},{24,0},{1,9},{9,17},{17,25},{25,1},{2,10},{10... | collective-permute-start | bytes 2359304 | tf_op jit(solution)/shard_map/ppermute | solution.py:24
  56.1 39.0 %collective-permute-start.5 = (bf16[96,4096]{1,0:T(8,128)(2,1)}, bf16[96,4096]{1,0:T(8,128)(2,1)}, u32[]{:S(2)}, u32[]{:S(2)}) collective-permute-start(bf16[96,4096]{1,0:T(8,128)(2,1)} %convolution_convert_fusion.3), channel_id=1, source_target_pairs={{0,16},{8,24},{16,0},{24,8},{1,17},{9,25},{17,1},{25,9},{2,18},{10... | collective-permute-start | bytes 2359304 | tf_op jit(solution)/shard_map/ppermute | solution.py:24
  60.4 39.8 %collective-permute-start.6 = (bf16[96,4096]{1,0:T(8,128)(2,1)}, bf16[96,4096]{1,0:T(8,128)(2,1)}, u32[]{:S(2)}, u32[]{:S(2)}) collective-permute-start(bf16[96,4096]{1,0:T(8,128)(2,1)} %convolution_convert_fusion.2), channel_id=1, source_target_pairs={{0,24},{8,0},{16,8},{24,16},{1,25},{9,1},{17,9},{25,17},{2,26},{10... | collective-permute-start | bytes 2359304 | tf_op jit(solution)/shard_map/ppermute | solution.py:24
  70.3 30.0 %slice-start = ((bf16[256,384]{0,1:T(8,128)(2,1)}), bf16[256,96]{0,1:T(8,128)(2,1)S(1)}, s32[]{:S(2)}) async-start(bf16[256,384]{0,1:T(8,128)(2,1)} %fusion.5), calls=%async_computation.3 | async-start | bytes 98304 | tf_op jit(solution)/shard_map/slice | solution.py:77
  71.6 65.5 %collective-permute-start.7 = (bf16[32,4096]{1,0:T(8,128)(2,1)S(1)}, bf16[32,4096]{1,0:T(8,128)(2,1)}, u32[]{:S(2)}, u32[]{:S(2)}) collective-permute-start(bf16[32,4096]{1,0:T(8,128)(2,1)S(1)} %add_convert_fusion.1), channel_id=1, source_target_pairs={{0,1},{1,0},{2,3},{3,2},{4,5},{5,4},{6,7},{7,6},{8,9},{9,8},{10,11... | collective-permute-start | bytes 786440 | tf_op jit(solution)/shard_map/ppermute | solution.py:28
  75.0 41.6 %collective-permute-start.8 = (bf16[32,4096]{1,0:T(8,128)(2,1)S(1)}, bf16[32,4096]{1,0:T(8,128)(2,1)}, u32[]{:S(2)}, u32[]{:S(2)}) collective-permute-start(bf16[32,4096]{1,0:T(8,128)(2,1)S(1)} %add_convert_fusion.1), channel_id=1, source_target_pairs={{0,2},{2,4},{4,6},{6,0},{1,3},{3,5},{5,7},{7,1},{8,10},{10,12},{12... | collective-permute-start | bytes 786440 | tf_op jit(solution)/shard_map/ppermute | solution.py:24
  79.9 26.2 %all-to-all-start.1 = ((f32[32,4,128]{2,1,0:T(4,128)}), f32[32,4,128]{2,1,0:T(4,128)S(1)}, u32[]{:S(2)}, u32[]{:S(2)}) async-start(f32[32,4,128]{2,1,0:T(4,128)} %broadcast_in_dim.6), calls=%async_computation.1 | async-start | bytes 131072 | tf_op jit(solution)/shard_map/all_to_all | solution.py:15
  86.5 13.8 %copy-start.2 = (bf16[256,4096]{1,0:T(8,128)(2,1)S(1)}, bf16[256,4096]{1,0:T(8,128)(2,1)}, u32[]{:S(2)}) copy-start(bf16[256,4096]{1,0:T(8,128)(2,1)} %param.5) | copy-start | bytes 6291460
  88.8 33.2 %collective-permute-start.10 = (bf16[32,4096]{1,0:T(8,128)(2,1)S(1)}, bf16[32,4096]{1,0:T(8,128)(2,1)}, u32[]{:S(2)}, u32[]{:S(2)}) collective-permute-start(bf16[32,4096]{1,0:T(8,128)(2,1)S(1)} %add_convert_fusion.1), channel_id=1, source_target_pairs={{0,6},{2,0},{4,2},{6,4},{1,7},{3,1},{5,3},{7,5},{8,14},{10,8},{12,... | collective-permute-start | bytes 786440 | tf_op jit(solution)/shard_map/ppermute | solution.py:24
  95.0 38.5 %collective-permute-start.12 = (bf16[32,4096]{1,0:T(8,128)(2,1)S(1)}, bf16[32,4096]{1,0:T(8,128)(2,1)}, u32[]{:S(2)}, u32[]{:S(2)}) collective-permute-start(bf16[32,4096]{1,0:T(8,128)(2,1)S(1)} %add_convert_fusion.1), channel_id=1, source_target_pairs={{0,4},{2,6},{4,0},{6,2},{1,5},{3,7},{5,1},{7,3},{8,12},{10,14},{12... | collective-permute-start | bytes 786440 | tf_op jit(solution)/shard_map/ppermute | solution.py:24
  108.7 37.2 %all-to-all-start.2 = ((bf16[24,4,4352]{2,1,0:T(4,128)(2,1)}), bf16[24,4,4352]{2,1,0:T(4,128)(2,1)}, u32[]{:S(2)}, u32[]{:S(2)}) async-start(bf16[24,4,4352]{2,1,0:T(4,128)(2,1)} %pad_maximum_fusion), calls=%async_computation.2 | async-start | bytes 1671168 | tf_op jit(solution)/shard_map/all_to_all | solution.py:15
  116.6 23.8 %collective-permute-start.9 = (bf16[32,4096]{1,0:T(8,128)(2,1)}, bf16[32,4096]{1,0:T(8,128)(2,1)S(1)}, u32[]{:S(2)}, u32[]{:S(2)}) collective-permute-start(bf16[32,4096]{1,0:T(8,128)(2,1)} %collective-permute-done.8), channel_id=1, source_target_pairs={{0,1},{1,0},{2,3},{3,2},{4,5},{5,4},{6,7},{7,6},{8,9},{9,8},{10,11... | collective-permute-start | bytes 786440 | tf_op jit(solution)/shard_map/ppermute | solution.py:28
  122.0 20.8 %collective-permute-start.11 = (bf16[32,4096]{1,0:T(8,128)(2,1)}, bf16[32,4096]{1,0:T(8,128)(2,1)S(1)}, u32[]{:S(2)}, u32[]{:S(2)}) collective-permute-start(bf16[32,4096]{1,0:T(8,128)(2,1)} %collective-permute-done.10), channel_id=1, source_target_pairs={{0,1},{1,0},{2,3},{3,2},{4,5},{5,4},{6,7},{7,6},{8,9},{9,8},{10,11... | collective-permute-start | bytes 786440 | tf_op jit(solution)/shard_map/ppermute | solution.py:28
  133.5 11.7 %collective-permute-start.13 = (bf16[32,4096]{1,0:T(8,128)(2,1)}, bf16[32,4096]{1,0:T(8,128)(2,1)S(1)}, u32[]{:S(2)}, u32[]{:S(2)}) collective-permute-start(bf16[32,4096]{1,0:T(8,128)(2,1)} %collective-permute-done.12), channel_id=1, source_target_pairs={{0,1},{1,0},{2,3},{3,2},{4,5},{5,4},{6,7},{7,6},{8,9},{9,8},{10,11... | collective-permute-start | bytes 786440 | tf_op jit(solution)/shard_map/ppermute | solution.py:28

commit v2 on v1

--- a/solution.py
+++ b/solution.py
@@ -1,6 +1,8 @@
 import jax
 import jax.numpy as jnp
 from jax import lax
+from jax.experimental import pallas as pl
+from jax.experimental.pallas import tpu as pltpu
 from jax.sharding import Mesh
 from jax.sharding import PartitionSpec as P
 
@@ -37,6 +39,37 @@
     return (place[:, None] == source[None, :]).astype(BF16)
 
 
+def pack_kernel(first, second, third, fourth, rider, packed):
+    owners, rows, _ = packed.shape
+    width = first.shape[1]
+    per_tile = 8 // rows
+    for tile in range(owners // per_tile):
+        place = slice(tile * 8, tile * 8 + 8)
+        parts = [ref[place, :].astype(F32) for ref in (first, second, third, fourth)]
+        summed = (parts[0] + parts[1]) + (parts[2] + parts[3])
+        for one in range(per_tile):
+            owner = tile * per_tile + one
+            packed[owner, :, :width] = summed[one * rows : (one + 1) * rows, :].astype(BF16)
+            packed[owner, :, width:] = rider[...]
+
+
+def pack(blocks, rider):
+    share, width = blocks[0].shape
+    rows, extra = rider.shape
+    shape = (share // rows, rows, width + extra)
+    return pl.pallas_call(
+        pack_kernel,
+        out_shape=jax.ShapeDtypeStruct(shape, BF16),
+        in_specs=[pl.BlockSpec(memory_space=pltpu.VMEM)] * 5,
+        out_specs=pl.BlockSpec(memory_space=pltpu.VMEM),
+        compiler_params=pltpu.CompilerParams(vmem_limit_bytes=10 * 2**20),
+        cost_estimate=pl.CostEstimate(
+            flops=3 * share * width, bytes_accessed=10 * share * width, transcendentals=0
+        ),
+        name="pack",
+    )(*blocks, rider)
+
+
 def body(resid, gain, grad_q, w_query, grad_in):
     tokens, width = resid.shape
     cols = grad_q.shape[1]
@@ -57,44 +90,39 @@
         rows = rows_of(grad_q, start, half)
         return jnp.dot(rows, w_query, preferred_element_type=F32).astype(BF16)
 
-    inv = inverse(resid)
+    inv, grad_q = lax.optimization_barrier((inverse(resid), grad_q))
     ordered = jnp.dot(grad_q, owner_columns(cols, lax.axis_index("x")), preferred_element_type=F32)
-    inv, ordered, grad_q = lax.optimization_barrier((inv, ordered.astype(BF16), grad_q))
+    ordered = ordered.astype(BF16)
 
     other_start, own_start = (1 - core) * half, core * half
     sent = term(other_start)
     got = swapped(sent, "c", 1)
     kept = lax.optimization_barrier(term(own_start))
     pair = (kept.astype(F32) + got.astype(F32)).astype(BF16)
-    pair, inv = lax.optimization_barrier((pair, inv))
+    pair, inv, ordered = lax.optimization_barrier((pair, inv, ordered))
     dnormed = total(exchange(pair.reshape(n_zh, own, width), "zh"))
 
     unit = resid.astype(F32) * inv
-    normed = (unit * gain_f).astype(BF16)
+    part = jnp.sum(sent.astype(F32) * rows_of(unit, other_start, half), axis=0)
+    part = part + jnp.sum(kept.astype(F32) * rows_of(unit, own_start, half), axis=0)
+    part, inv_x = lax.optimization_barrier((part.reshape(n_y, -1, 128), inv))
+    part = part + swapped(part, "y", 1)
+
+    normed = (resid.astype(F32) * inv_x * gain_f).astype(BF16)
     share = cols // n_x
 
-    def columns(shift):
-        return ordered[:, shift * share : (shift + 1) * share]
-
-    def block(columns):
-        return lax.dot_general(
+    def block(shift):
+        columns = ordered[:, shift * share : (shift + 1) * share]
+        local = lax.dot_general(
             columns, normed, (((0,), (0,)), ((), ())), preferred_element_type=F32
         )
+        return lax.optimization_barrier(local.astype(BF16))
 
-    blocks = [block(columns(s)).astype(BF16) for s in range(1, n_x)]
-    inv, *blocks = lax.optimization_barrier((inv, *blocks))
-    by_x = [shifted(b, "x", s + 1) for s, b in enumerate(blocks)]
-    unit = resid.astype(F32) * inv
-    part = jnp.sum(sent.astype(F32) * rows_of(unit, other_start, half), axis=0)
-    part = part + jnp.sum(kept.astype(F32) * rows_of(unit, own_start, half), axis=0)
-    part = part.reshape(n_y, -1, 128)
-    for bit in (1, 2, 4):
+    blocks = [block(s) for s in range(n_x)]
+    blocks = [b if s == 0 else shifted(b, "x", s) for s, b in enumerate(blocks)]
+    for bit in (2, 4):
         part = part + swapped(part, "y", bit)
     part = lax.dynamic_index_in_dim(part, lax.axis_index("y"), 0, keepdims=False)
-    axes = ("x", "zh", "c")
-    part, dnormed = lax.optimization_barrier((part, dnormed))
-    part = jnp.broadcast_to(part[None], (lax.axis_size(axes), *part.shape))
-    part = total(exchange(part, axes))
 
     first = own_start + zh * own
     resid_rows = rows_of(resid, first, own)
@@ -102,18 +130,17 @@
     unit_rows = resid_rows.astype(F32) * inv_rows
     dunit = dnormed * gain_f
     inner = jnp.mean(dunit * unit_rows, axis=-1, keepdims=True)
+    axes = ("x", "zh", "c")
+    part, inner = lax.optimization_barrier((part, inner))
+    part = jnp.broadcast_to(part[None], (lax.axis_size(axes), *part.shape))
+    part = total(exchange(part, axes))
     rows = rows_of(grad_in, first, own).astype(F32) + inv_rows * (dunit - unit_rows * inner)
-    own_columns, rows = lax.optimization_barrier((columns(0), rows.astype(BF16)))
-
-    by_x = block(own_columns) + sum(b.astype(F32) for b in by_x)
-    mine = share // (n_y * n_zl)
-    by_x = by_x.astype(BF16).reshape(n_zl * n_y, mine, width)
+    own_block, rows = lax.optimization_barrier((blocks[0], rows.astype(BF16)))
 
     upper = part.astype(BF16)
     lower = (part - upper.astype(F32)).astype(BF16)
-    rider = jnp.concatenate([upper, lower], axis=1)
-    rider = jnp.broadcast_to(rider[None], (n_zl * n_y, *rider.shape))
-    last = exchange(jnp.concatenate([by_x, rider], axis=2), ("zl", "y"))
+    packed = pack([own_block, *blocks[1:]], jnp.concatenate([upper, lower], axis=1))
+    last = exchange(packed, ("zl", "y"))
     weight_grad = total(last[:, :, :width])
     parts = last[:, :, width:].astype(F32)
     parts = (parts[:, :, :128] + parts[:, :, 128:]).reshape(n_zl, n_y, -1, 128)

time: 151 us -> 165 us (1.093)
  the two profiles are of different devices: /device:TPU:81 before, /device:TPU:121 now
where the time goes in v2:
time: 165 us; the launch traced here: 164 us
  starting transfers between devices  81.6 us (49%)
  waiting for transfers between devices  37 us (22%)
  other arithmetic  16.7 us (10%)
  local copies, waits for them, and re-layouts  14.2 us (9%)
  matrix products  11.2 us (7%)
  Pallas kernels  2.04 us (1%)
    ppermute x8, starting transfers between devices, swapped(): lax.ppermute(block, axis, [(i, i ^ bit) for i in range(lax.axis_size(axis...  31.2 us
    all_to_all x3, starting transfers between devices, exchange(): return lax.all_to_all(blocks, axes, 0, 0, tiled=True)  26.5 us
    ppermute x6, starting transfers between devices, shifted(): lax.ppermute(block, axis, [(i, (i + shift) % peers) for i in range(peers)])  23.9 us
    all_to_all x3, waiting for transfers between devices, exchange(): return lax.all_to_all(blocks, axes, 0, 0, tiled=True)  21.7 us
    ppermute x6, waiting for transfers between devices, shifted(): lax.ppermute(block, axis, [(i, (i + shift) % peers) for i in range(peers)])  15 us
    dot_general x4, matrix products, block(): lax.dot_general(columns, normed, (((0,), (0,)), ((), ())), preferred_elem...  6.85 us
    dynamic_update_slice x4, local copies, waits for them, and re-layouts, body(): lax.dynamic_update_slice_in_dim(result, piece, own_start + source, 0)  5.72 us
    dynamic_update_slice x4, local copies, waits for them, and re-layouts, body(): lax.dynamic_update_slice_in_dim(result, other, other_start + source, 0)  3.84 us
  transfers between devices with their start and end apart: 17, of which 5 were waited for; matrix products, arithmetic and copies ran while one was open for 18% of the time, Pallas kernels for 1%

profile of v2, /device:TPU:121, one launch (start us, length us, event | category | flops | bytes accessed | tf_op | source)
XLA Modules:
  0.0 163.7 jit_solution(1987025629948377043)
XLA Ops:
  0.7 2.2 %fusion = f32[256]{0:T(256)S(1)} fusion(bf16[256,4096]{1,0:T(8,128)(2,1)} %param.5), kind=kLoop, calls=%fused_computation.9 | loop fusion | flops 3145472 | bytes 2098176 | tf_op jit(solution)/shard_map/reduce_sum | solution.py:87
  3.2 1.7 %convolution_convert_fusion = bf16[128,4096]{1,0:T(8,128)(2,1)} fusion(bf16[384,4096]{1,0:T(8,128)(2,1)S(1)} %copy-done, bf16[256,384]{1,0:T(8,128)(2,1)S(1)} %copy-done.5, s32[]{:T(128)S(6)} %select_n.77), kind=kOutput, calls=%fused_computation.3 | convolution fusion | flops 403177472 | bytes 4292612 | tf_op jit(solution)/shard_map/dot_general | solution.py:91
  4.8 2.6 %collective-permute-start = (bf16[128,4096]{1,0:T(8,128)(2,1)}, bf16[128,4096]{1,0:T(8,128)(2,1)}, u32[]{:S(2)}, u32[]{:S(2)}) collective-permute-start(bf16[128,4096]{1,0:T(8,128)(2,1)} %convolution_convert_fusion), channel_id=1, source_target_pairs={{0,1},{1,0},{2,3},{3,2},{4,5},{5,4},{6,7},{7,6},{8,9},{9,8},{10,11... | collective-permute-start | bytes 3145736 | tf_op jit(solution)/shard_map/ppermute | solution.py:30
  7.5 1.7 %convolution_convert_fusion.1 = bf16[128,4096]{1,0:T(8,128)(2,1)} fusion(bf16[384,4096]{1,0:T(8,128)(2,1)S(1)} %copy-done, bf16[256,384]{1,0:T(8,128)(2,1)S(1)} %copy-done.5, s32[]{:T(128)S(6)} %select_n.76), kind=kOutput, calls=%fused_computation.4 | convolution fusion | flops 403177472 | bytes 4292612 | tf_op jit(solution)/shard_map/dot_general | solution.py:91
  9.2 1.0 convolution_convert_fusion.6
  10.2 2.8 %fusion.3 = bf16[128,4096]{1,0:T(8,128)(2,1)} fusion(bf16[128,4096]{1,0:T(8,128)(2,1)} %convolution_convert_fusion.1, bf16[128,4096]{1,0:T(8,128)(2,1)} %collective-permute-done), kind=kLoop, calls=%fused_computation.14 | loop fusion | flops 2097152 | bytes 3145728 | tf_op jit(solution)/shard_map/convert_element_type | solution.py:101
  13.0 13.3 %all-to-all-start = ((bf16[4,32,4096]{2,1,0:T(8,128)(2,1)}), bf16[4,32,4096]{2,1,0:T(8,128)(2,1)}, u32[]{:S(2)}, u32[]{:S(2)}) async-start(bf16[4,32,4096]{2,1,0:T(8,128)(2,1)} %bitcast.17), calls=%async_computation | async-start | bytes 2097152 | tf_op jit(solution)/shard_map/all_to_all | solution.py:17
  26.3 2.2 %convert_multiply_fusion.1 = f32[256,4096]{1,0:T(8,128)S(1)} fusion(bf16[256,4096]{1,0:T(8,128)(2,1)} %param.5, f32[256]{0:T(256)S(1)} %add_rsqrt_fusion), kind=kLoop, calls=%fused_computation.1 | loop fusion | flops 2097152 | bytes 6292480 | tf_op jit(solution)/shard_map/mul | solution.py:105
  28.6 2.0 %fusion.4 = (f32[4096]{0:T(1024)S(1)}, f32[4096]{0:T(1024)S(1)}) fusion(bf16[128,4096]{1,0:T(8,128)(2,1)S(1)} %copy-done.4, f32[256,4096]{1,0:T(8,128)S(1)} %convert_multiply_fusion.1, s32[]{:T(128)S(6)} %select_n.76, s32[]{:T(128)S(6)} %select_n.77, bf16[128,4096]{1,0:T(8,128)(2,1)} %convolution_convert_fusion), kind=kLoop, calls=%fused_computation.15 | loop fusion | flops 3137536 | bytes 6324232 | tf_op jit(solution)/shard_map/reduce_sum | solution.py:107
  30.5 3.0 %collective-permute-start.1 = (f32[8,4,128]{2,1,0:T(4,128)S(1)}, f32[8,4,128]{2,1,0:T(4,128)S(1)}, u32[]{:S(2)}, u32[]{:S(2)}) collective-permute-start(f32[8,4,128]{2,1,0:T(4,128)S(1)} %bitcast.19), channel_id=1, source_target_pairs={{0,32},{32,0},{64,96},{96,64},{128,160},{160,128},{192,224},{224,1... | collective-permute-start | bytes 49160 | tf_op jit(solution)/shard_map/ppermute | solution.py:30
  33.5 1.7 %convolution_convert_fusion.5.first = bf16[96,4096]{1,0:T(8,128)(2,1)} fusion(bf16[256,384]{1,0:T(8,128)(2,1)S(1)} %copy-done.7, bf16[256,4096]{1,0:T(8,128)(2,1)S(1)} %copy-done.3, f32[4096]{0:T(1024)S(1)} %convert_element_type.81, f32[256]{0:T(256)S(1)} %add_rsqrt_fusion), kind=kOutput, calls=%fused_computation.8 | convolution fusion | flops 205914112 | bytes 2966528 | tf_op jit(solution)/shard_map/dot_general | solution.py:116
  35.3 1.7 %convolution_convert_fusion.2 = bf16[96,4096]{1,0:T(8,128)(2,1)} fusion(bf16[256,384]{1,0:T(8,128)(2,1)S(1)} %copy-done.7, bf16[256,4096]{1,0:T(8,128)(2,1)S(1)} %copy-done.3, f32[4096]{0:T(1024)S(1)} %convert_element_type.81, f32[256]{0:T(256)S(1)} %add_rsqrt_fusion), kind=kOutput, calls=%fused_computation.5 | convolution fusion | flops 205914112 | bytes 2966528 | tf_op jit(solution)/shard_map/dot_general | solution.py:116
  37.0 1.7 %convolution_convert_fusion.3 = bf16[96,4096]{1,0:T(8,128)(2,1)} fusion(bf16[256,384]{1,0:T(8,128)(2,1)S(1)} %copy-done.7, bf16[256,4096]{1,0:T(8,128)(2,1)S(1)} %copy-done.3, f32[4096]{0:T(1024)S(1)} %convert_element_type.81, f32[256]{0:T(256)S(1)} %add_rsqrt_fusion), kind=kOutput, calls=%fused_computation.6 | convolution fusion | flops 205914112 | bytes 2966528 | tf_op jit(solution)/shard_map/dot_general | solution.py:116
  38.7 3.8 %collective-permute-start.2 = (f32[8,4,128]{2,1,0:T(4,128)S(1)}, f32[8,4,128]{2,1,0:T(4,128)S(1)}, u32[]{:S(2)}, u32[]{:S(2)}) collective-permute-start(f32[8,4,128]{2,1,0:T(4,128)S(1)} %add.190), channel_id=1, source_target_pairs={{0,64},{32,96},{64,0},{96,32},{128,192},{160,224},{192,128},{224,1... | collective-permute-start | bytes 49160 | tf_op jit(solution)/shard_map/ppermute | solution.py:30
  42.5 1.7 %convolution_convert_fusion.4 = bf16[96,4096]{1,0:T(8,128)(2,1)} fusion(bf16[256,384]{1,0:T(8,128)(2,1)S(1)} %copy-done.7, bf16[256,4096]{1,0:T(8,128)(2,1)S(1)} %copy-done.3, f32[4096]{0:T(1024)S(1)} %convert_element_type.81, f32[256]{0:T(256)S(1)} %add_rsqrt_fusion), kind=kOutput, calls=%fused_computation.7 | convolution fusion | flops 205914112 | bytes 2966528 | tf_op jit(solution)/shard_map/dot_general | solution.py:116
  44.5 3.5 %collective-permute-start.3 = (f32[8,4,128]{2,1,0:T(4,128)S(1)}, f32[8,4,128]{2,1,0:T(4,128)S(1)}, u32[]{:S(2)}, u32[]{:S(2)}) collective-permute-start(f32[8,4,128]{2,1,0:T(4,128)S(1)} %add.191), channel_id=1, source_target_pairs={{0,128},{32,160},{64,192},{96,224},{128,0},{160,32},{192,64},{224,... | collective-permute-start | bytes 49160 | tf_op jit(solution)/shard_map/ppermute | solution.py:30
  48.1 4.4 %collective-permute-start.6 = (bf16[96,4096]{1,0:T(8,128)(2,1)}, bf16[96,4096]{1,0:T(8,128)(2,1)}, u32[]{:S(2)}, u32[]{:S(2)}) collective-permute-start(bf16[96,4096]{1,0:T(8,128)(2,1)} %convolution_convert_fusion.2), channel_id=1, source_target_pairs={{0,24},{8,0},{16,8},{24,16},{1,25},{9,1},{17,9},{25,17},{2,26},{10... | collective-permute-start | bytes 2359304 | tf_op jit(solution)/shard_map/ppermute | solution.py:26
  52.5 2.4 %collective-permute-start.5 = (bf16[96,4096]{1,0:T(8,128)(2,1)}, bf16[96,4096]{1,0:T(8,128)(2,1)}, u32[]{:S(2)}, u32[]{:S(2)}) collective-permute-start(bf16[96,4096]{1,0:T(8,128)(2,1)} %convolution_convert_fusion.3), channel_id=1, source_target_pairs={{0,16},{8,24},{16,0},{24,8},{1,17},{9,25},{17,1},{25,9},{2,18},{10... | collective-permute-start | bytes 2359304 | tf_op jit(solution)/shard_map/ppermute | solution.py:26
  54.9 2.5 %collective-permute-start.4 = (bf16[96,4096]{1,0:T(8,128)(2,1)}, bf16[96,4096]{1,0:T(8,128)(2,1)}, u32[]{:S(2)}, u32[]{:S(2)}) collective-permute-start(bf16[96,4096]{1,0:T(8,128)(2,1)} %convolution_convert_fusion.4), channel_id=1, source_target_pairs={{0,8},{8,16},{16,24},{24,0},{1,9},{9,17},{17,25},{25,1},{2,10},{10... | collective-permute-start | bytes 2359304 | tf_op jit(solution)/shard_map/ppermute | solution.py:26
  57.5 10.0 %all-to-all-done = bf16[4,32,4096]{2,1,0:T(8,128)(2,1)} async-done(((bf16[4,32,4096]{2,1,0:T(8,128)(2,1)}), bf16[4,32,4096]{2,1,0:T(8,128)(2,1)}, u32[]{:S(2)}, u32[]{:S(2)}) %all-to-all-start) | async-done | bytes 1048608 | tf_op jit(solution)/shard_map/all_to_all | solution.py:17
  67.5 1.4 convert_reduce_fusion
  68.9 1.2 multiply_reduce_fusion.1
  70.1 1.2 add_convert_fusion
  71.4 3.2 %collective-permute-start.7 = (bf16[32,4096]{1,0:T(8,128)(2,1)S(1)}, bf16[32,4096]{1,0:T(8,128)(2,1)}, u32[]{:S(2)}, u32[]{:S(2)}) collective-permute-start(bf16[32,4096]{1,0:T(8,128)(2,1)S(1)} %add_convert_fusion), channel_id=1, source_target_pairs={{0,1},{1,0},{2,3},{3,2},{4,5},{5,4},{6,7},{7,6},{8,9},{9,8},{10,11... | collective-permute-start | bytes 786440 | tf_op jit(solution)/shard_map/ppermute | solution.py:30
  74.6 3.7 %collective-permute-start.8 = (bf16[32,4096]{1,0:T(8,128)(2,1)S(1)}, bf16[32,4096]{1,0:T(8,128)(2,1)}, u32[]{:S(2)}, u32[]{:S(2)}) collective-permute-start(bf16[32,4096]{1,0:T(8,128)(2,1)S(1)} %add_convert_fusion), channel_id=1, source_target_pairs={{0,2},{2,4},{4,6},{6,0},{1,3},{3,5},{5,7},{7,1},{8,10},{10,12},{12... | collective-permute-start | bytes 786440 | tf_op jit(solution)/shard_map/ppermute | solution.py:26
  79.0 7.1 %all-to-all-start.1 = ((f32[32,4,128]{2,1,0:T(4,128)}), f32[32,4,128]{2,1,0:T(4,128)S(1)}, u32[]{:S(2)}, u32[]{:S(2)}) async-start(f32[32,4,128]{2,1,0:T(4,128)} %broadcast_in_dim.4), calls=%async_computation.1 | async-start | bytes 131072 | tf_op jit(solution)/shard_map/all_to_all | solution.py:17
  86.1 1.6 broadcast_in_dim.5
  88.4 11.7 %all-to-all-done.1 = f32[32,4,128]{2,1,0:T(4,128)S(1)} async-done(((f32[32,4,128]{2,1,0:T(4,128)}), f32[32,4,128]{2,1,0:T(4,128)S(1)}, u32[]{:S(2)}, u32[]{:S(2)}) %all-to-all-start.1) | async-done | bytes 65568 | tf_op jit(solution)/shard_map/all_to_all | solution.py:17
  100.1 3.0 %collective-permute-start.10 = (bf16[32,4096]{1,0:T(8,128)(2,1)S(1)}, bf16[32,4096]{1,0:T(8,128)(2,1)}, u32[]{:S(2)}, u32[]{:S(2)}) collective-permute-start(bf16[32,4096]{1,0:T(8,128)(2,1)S(1)} %add_convert_fusion), channel_id=1, source_target_pairs={{0,6},{2,0},{4,2},{6,4},{1,7},{3,1},{5,3},{7,5},{8,14},{10,8},{12,... | collective-permute-start | bytes 786440 | tf_op jit(solution)/shard_map/ppermute | solution.py:26
  103.1 7.9 %collective-permute-start.12 = (bf16[32,4096]{1,0:T(8,128)(2,1)S(1)}, bf16[32,4096]{1,0:T(8,128)(2,1)}, u32[]{:S(2)}, u32[]{:S(2)}) collective-permute-start(bf16[32,4096]{1,0:T(8,128)(2,1)S(1)} %add_convert_fusion), channel_id=1, source_target_pairs={{0,4},{2,6},{4,0},{6,2},{1,5},{3,7},{5,1},{7,3},{8,12},{10,14},{12... | collective-permute-start | bytes 786440 | tf_op jit(solution)/shard_map/ppermute | solution.py:26
  111.0 1.1 copy-done.2
  112.1 2.0 %pack.1 = bf16[24,4,4352]{2,1,0:T(4,128)(2,1)S(1)} custom-call(bf16[96,4096]{1,0:T(8,128)(2,1)S(1)} %copy-done.2, bf16[96,4096]{1,0:T(8,128)(2,1)} %collective-permute-done.4.second, bf16[96,4096]{1,0:T(8,128)(2,1)} %collective-permute-done.5.third, bf16[96,4096]{1,0:T(8,128)(2,1)} %collective-permute-done.6.fourth, bf16[4,256]{1,0:T(4,128)(2,1)S(1)} %pad_maximum_fusion.rider), custom_call_target="tpu_custom_call" | custom-call | flops 1179648 | bytes 3932160 | tf_op jit(solution)/shard_map/pack/pallas_call | solution.py:60
  114.2 0.9 copy-done.1
  115.1 6.1 %all-to-all-start.2 = ((bf16[24,4,4352]{2,1,0:T(4,128)(2,1)}), bf16[24,4,4352]{2,1,0:T(4,128)(2,1)}, u32[]{:S(2)}, u32[]{:S(2)}) async-start(bf16[24,4,4352]{2,1,0:T(4,128)(2,1)} %copy-done.1), calls=%async_computation.2 | async-start | bytes 1671168 | tf_op jit(solution)/shard_map/all_to_all | solution.py:17
  121.2 3.8 %collective-permute-start.9 = (bf16[32,4096]{1,0:T(8,128)(2,1)}, bf16[32,4096]{1,0:T(8,128)(2,1)S(1)}, u32[]{:S(2)}, u32[]{:S(2)}) collective-permute-start(bf16[32,4096]{1,0:T(8,128)(2,1)} %collective-permute-done.8), channel_id=1, source_target_pairs={{0,1},{1,0},{2,3},{3,2},{4,5},{5,4},{6,7},{7,6},{8,9},{9,8},{10,11... | collective-permute-start | bytes 786440 | tf_op jit(solution)/shard_map/ppermute | solution.py:30
  125.0 10.0 %collective-permute-done.10 = bf16[32,4096]{1,0:T(8,128)(2,1)} collective-permute-done((bf16[32,4096]{1,0:T(8,128)(2,1)S(1)}, bf16[32,4096]{1,0:T(8,128)(2,1)}, u32[]{:S(2)}, u32[]{:S(2)}) %collective-permute-start.10) | collective-permute-done | bytes 262176 | tf_op jit(solution)/shard_map/ppermute | solution.py:26
  135.0 2.5 %collective-permute-start.11 = (bf16[32,4096]{1,0:T(8,128)(2,1)}, bf16[32,4096]{1,0:T(8,128)(2,1)S(1)}, u32[]{:S(2)}, u32[]{:S(2)}) collective-permute-start(bf16[32,4096]{1,0:T(8,128)(2,1)} %collective-permute-done.10), channel_id=1, source_target_pairs={{0,1},{1,0},{2,3},{3,2},{4,5},{5,4},{6,7},{7,6},{8,9},{9,8},{10,11... | collective-permute-start | bytes 786440 | tf_op jit(solution)/shard_map/ppermute | solution.py:30
  137.5 5.0 %collective-permute-done.12 = bf16[32,4096]{1,0:T(8,128)(2,1)} collective-permute-done((bf16[32,4096]{1,0:T(8,128)(2,1)S(1)}, bf16[32,4096]{1,0:T(8,128)(2,1)}, u32[]{:S(2)}, u32[]{:S(2)}) %collective-permute-start.12) | collective-permute-done | bytes 262176 | tf_op jit(solution)/shard_map/ppermute | solution.py:26
  142.5 8.8 %collective-permute-start.13 = (bf16[32,4096]{1,0:T(8,128)(2,1)}, bf16[32,4096]{1,0:T(8,128)(2,1)S(1)}, u32[]{:S(2)}, u32[]{:S(2)}) collective-permute-start(bf16[32,4096]{1,0:T(8,128)(2,1)} %collective-permute-done.12), channel_id=1, source_target_pairs={{0,1},{1,0},{2,3},{3,2},{4,5},{5,4},{6,7},{7,6},{8,9},{9,8},{10,11... | collective-permute-start | bytes 786440 | tf_op jit(solution)/shard_map/ppermute | solution.py:30
  151.3 1.7 %constant_dynamic-update-slice_fusion.6 = bf16[256,4096]{1,0:T(8,128)(2,1)} fusion(bf16[256,4096]{1,0:T(8,128)(2,1)} %constant_dynamic-update-slice_fusion.7, bf16[32,4096]{1,0:T(8,128)(2,1)} %collective-permute-done.7, s32[]{:T(128)S(6)} %select_n.85), kind=kLoop, calls=%fused_computation.40 | loop fusion | bytes 524292 | tf_op jit(solution)/shard_map/dynamic_update_slice | solution.py:155
  153.0 1.7 %constant_dynamic-update-slice_fusion.5 = bf16[256,4096]{1,0:T(8,128)(2,1)} fusion(bf16[256,4096]{1,0:T(8,128)(2,1)} %constant_dynamic-update-slice_fusion.6, bf16[32,4096]{1,0:T(8,128)(2,1)} %collective-permute-done.8, s32[]{:T(128)S(6)} %select_n.86), kind=kLoop, calls=%fused_computation.39 | loop fusion | bytes 524292 | tf_op jit(solution)/shard_map/dynamic_update_slice | solution.py:154
  154.7 0.7 constant_dynamic-update-slice_fusion.4
  155.4 1.7 %constant_dynamic-update-slice_fusion.3 = bf16[256,4096]{1,0:T(8,128)(2,1)} fusion(bf16[256,4096]{1,0:T(8,128)(2,1)} %constant_dynamic-update-slice_fusion.4, bf16[32,4096]{1,0:T(8,128)(2,1)} %collective-permute-done.10, s32[]{:T(128)S(6)} %select_n.88), kind=kLoop, calls=%fused_computation.37 | loop fusion | bytes 524292 | tf_op jit(solution)/shard_map/dynamic_update_slice | solution.py:154
  157.1 0.7 constant_dynamic-update-slice_fusion.2
  157.8 1.7 %constant_dynamic-update-slice_fusion.1 = bf16[256,4096]{1,0:T(8,128)(2,1)} fusion(bf16[256,4096]{1,0:T(8,128)(2,1)} %constant_dynamic-update-slice_fusion.2, bf16[32,4096]{1,0:T(8,128)(2,1)} %collective-permute-done.12, s32[]{:T(128)S(6)} %select_n.90), kind=kLoop, calls=%fused_computation.35 | loop fusion | bytes 524292 | tf_op jit(solution)/shard_map/dynamic_update_slice | solution.py:154
  159.5 0.7 constant_dynamic-update-slice_fusion
  160.2 0.8 slice_convert_fusion
  161.6 2.1 %convert_reduce_fusion.1 = f32[4,4096]{1,0:T(4,128)} fusion(bf16[24,4,4352]{2,1,0:T(4,128)(2,1)} %all-to-all-done.2), kind=kLoop, calls=%fused_computation.18 | loop fusion | flops 770048 | bytes 851968 | tf_op jit(solution)/shard_map/reduce_sum | solution.py:21
  (43 shorter events, 2.8 us)
Async XLA Ops:
  0.6 2.5 %copy-start = (bf16[384,4096]{1,0:T(8,128)(2,1)S(1)}, bf16[384,4096]{1,0:T(8,128)(2,1)}, u32[]{:S(2)}) copy-start(bf16[384,4096]{1,0:T(8,128)(2,1)} %param.8) | copy-start | bytes 9437188
  0.6 2.5 %copy-start.5 = (bf16[256,384]{1,0:T(8,128)(2,1)S(1)}, bf16[256,384]{1,0:T(8,128)(2,1)}, u32[]{:S(2)}) copy-start(bf16[256,384]{1,0:T(8,128)(2,1)} %param.7) | copy-start | bytes 589828
  4.8 5.4 %collective-permute-start = (bf16[128,4096]{1,0:T(8,128)(2,1)}, bf16[128,4096]{1,0:T(8,128)(2,1)}, u32[]{:S(2)}, u32[]{:S(2)}) collective-permute-start(bf16[128,4096]{1,0:T(8,128)(2,1)} %convolution_convert_fusion), channel_id=1, source_target_pairs={{0,1},{1,0},{2,3},{3,2},{4,5},{5,4},{6,7},{7,6},{8,9},{9,8},{10,11... | collective-permute-start | bytes 3145736 | tf_op jit(solution)/shard_map/ppermute | solution.py:30
  7.5 1.7 %copy-start.6 = (bf16[4096]{0:T(1024)(128)(2,1)S(1)}, bf16[4096]{0:T(1024)(128)(2,1)}, u32[]{:S(2)}) copy-start(bf16[4096]{0:T(1024)(128)(2,1)} %param.6) | copy-start | bytes 24580
  13.0 54.5 %all-to-all-start = ((bf16[4,32,4096]{2,1,0:T(8,128)(2,1)}), bf16[4,32,4096]{2,1,0:T(8,128)(2,1)}, u32[]{:S(2)}, u32[]{:S(2)}) async-start(bf16[4,32,4096]{2,1,0:T(8,128)(2,1)} %bitcast.17), calls=%async_computation | async-start | bytes 2097152 | tf_op jit(solution)/shard_map/all_to_all | solution.py:17
  26.3 2.2 %copy-start.4 = (bf16[128,4096]{1,0:T(8,128)(2,1)S(1)}, bf16[128,4096]{1,0:T(8,128)(2,1)}, u32[]{:S(2)}) copy-start(bf16[128,4096]{1,0:T(8,128)(2,1)} %convolution_convert_fusion.1) | copy-start | bytes 3145732
  28.5 5.0 %copy-start.3 = (bf16[256,4096]{1,0:T(8,128)(2,1)S(1)}, bf16[256,4096]{1,0:T(8,128)(2,1)}, u32[]{:S(2)}) copy-start(bf16[256,4096]{1,0:T(8,128)(2,1)} %param.5) | copy-start | bytes 6291460
  28.5 5.0 %copy-start.7 = (bf16[256,384]{1,0:T(8,128)(2,1)S(1)}, bf16[256,384]{1,0:T(8,128)(2,1)}, u32[]{:S(2)}) copy-start(bf16[256,384]{1,0:T(8,128)(2,1)} %convolution_convert_fusion.6) | copy-start | bytes 589828
  30.5 8.2 %collective-permute-start.1 = (f32[8,4,128]{2,1,0:T(4,128)S(1)}, f32[8,4,128]{2,1,0:T(4,128)S(1)}, u32[]{:S(2)}, u32[]{:S(2)}) collective-permute-start(f32[8,4,128]{2,1,0:T(4,128)S(1)} %bitcast.19), channel_id=1, source_target_pairs={{0,32},{32,0},{64,96},{96,64},{128,160},{160,128},{192,224},{224,1... | collective-permute-start | bytes 49160 | tf_op jit(solution)/shard_map/ppermute | solution.py:30
  38.7 5.8 %collective-permute-start.2 = (f32[8,4,128]{2,1,0:T(4,128)S(1)}, f32[8,4,128]{2,1,0:T(4,128)S(1)}, u32[]{:S(2)}, u32[]{:S(2)}) collective-permute-start(f32[8,4,128]{2,1,0:T(4,128)S(1)} %add.190), channel_id=1, source_target_pairs={{0,64},{32,96},{64,0},{96,32},{128,192},{160,224},{192,128},{224,1... | collective-permute-start | bytes 49160 | tf_op jit(solution)/shard_map/ppermute | solution.py:30
  44.5 12.9 %collective-permute-start.3 = (f32[8,4,128]{2,1,0:T(4,128)S(1)}, f32[8,4,128]{2,1,0:T(4,128)S(1)}, u32[]{:S(2)}, u32[]{:S(2)}) collective-permute-start(f32[8,4,128]{2,1,0:T(4,128)S(1)} %add.191), channel_id=1, source_target_pairs={{0,128},{32,160},{64,192},{96,224},{128,0},{160,32},{192,64},{224,... | collective-permute-start | bytes 49160 | tf_op jit(solution)/shard_map/ppermute | solution.py:30
  48.1 52.0 %collective-permute-start.6 = (bf16[96,4096]{1,0:T(8,128)(2,1)}, bf16[96,4096]{1,0:T(8,128)(2,1)}, u32[]{:S(2)}, u32[]{:S(2)}) collective-permute-start(bf16[96,4096]{1,0:T(8,128)(2,1)} %convolution_convert_fusion.2), channel_id=1, source_target_pairs={{0,24},{8,0},{16,8},{24,16},{1,25},{9,1},{17,9},{25,17},{2,26},{10... | collective-permute-start | bytes 2359304 | tf_op jit(solution)/shard_map/ppermute | solution.py:26
  52.5 50.6 %collective-permute-start.5 = (bf16[96,4096]{1,0:T(8,128)(2,1)}, bf16[96,4096]{1,0:T(8,128)(2,1)}, u32[]{:S(2)}, u32[]{:S(2)}) collective-permute-start(bf16[96,4096]{1,0:T(8,128)(2,1)} %convolution_convert_fusion.3), channel_id=1, source_target_pairs={{0,16},{8,24},{16,0},{24,8},{1,17},{9,25},{17,1},{25,9},{2,18},{10... | collective-permute-start | bytes 2359304 | tf_op jit(solution)/shard_map/ppermute | solution.py:26
  54.9 56.1 %collective-permute-start.4 = (bf16[96,4096]{1,0:T(8,128)(2,1)}, bf16[96,4096]{1,0:T(8,128)(2,1)}, u32[]{:S(2)}, u32[]{:S(2)}) collective-permute-start(bf16[96,4096]{1,0:T(8,128)(2,1)} %convolution_convert_fusion.4), channel_id=1, source_target_pairs={{0,8},{8,16},{16,24},{24,0},{1,9},{9,17},{17,25},{25,1},{2,10},{10... | collective-permute-start | bytes 2359304 | tf_op jit(solution)/shard_map/ppermute | solution.py:26
  71.4 80.0 %collective-permute-start.7 = (bf16[32,4096]{1,0:T(8,128)(2,1)S(1)}, bf16[32,4096]{1,0:T(8,128)(2,1)}, u32[]{:S(2)}, u32[]{:S(2)}) collective-permute-start(bf16[32,4096]{1,0:T(8,128)(2,1)S(1)} %add_convert_fusion), channel_id=1, source_target_pairs={{0,1},{1,0},{2,3},{3,2},{4,5},{5,4},{6,7},{7,6},{8,9},{9,8},{10,11... | collective-permute-start | bytes 786440 | tf_op jit(solution)/shard_map/ppermute | solution.py:30
  74.6 46.6 %collective-permute-start.8 = (bf16[32,4096]{1,0:T(8,128)(2,1)S(1)}, bf16[32,4096]{1,0:T(8,128)(2,1)}, u32[]{:S(2)}, u32[]{:S(2)}) collective-permute-start(bf16[32,4096]{1,0:T(8,128)(2,1)S(1)} %add_convert_fusion), channel_id=1, source_target_pairs={{0,2},{2,4},{4,6},{6,0},{1,3},{3,5},{5,7},{7,1},{8,10},{10,12},{12... | collective-permute-start | bytes 786440 | tf_op jit(solution)/shard_map/ppermute | solution.py:26
  79.0 21.1 %all-to-all-start.1 = ((f32[32,4,128]{2,1,0:T(4,128)}), f32[32,4,128]{2,1,0:T(4,128)S(1)}, u32[]{:S(2)}, u32[]{:S(2)}) async-start(f32[32,4,128]{2,1,0:T(4,128)} %broadcast_in_dim.4), calls=%async_computation.1 | async-start | bytes 131072 | tf_op jit(solution)/shard_map/all_to_all | solution.py:17
  100.1 34.8 %collective-permute-start.10 = (bf16[32,4096]{1,0:T(8,128)(2,1)S(1)}, bf16[32,4096]{1,0:T(8,128)(2,1)}, u32[]{:S(2)}, u32[]{:S(2)}) collective-permute-start(bf16[32,4096]{1,0:T(8,128)(2,1)S(1)} %add_convert_fusion), channel_id=1, source_target_pairs={{0,6},{2,0},{4,2},{6,4},{1,7},{3,1},{5,3},{7,5},{8,14},{10,8},{12,... | collective-permute-start | bytes 786440 | tf_op jit(solution)/shard_map/ppermute | solution.py:26
  103.1 39.4 %collective-permute-start.12 = (bf16[32,4096]{1,0:T(8,128)(2,1)S(1)}, bf16[32,4096]{1,0:T(8,128)(2,1)}, u32[]{:S(2)}, u32[]{:S(2)}) collective-permute-start(bf16[32,4096]{1,0:T(8,128)(2,1)S(1)} %add_convert_fusion), channel_id=1, source_target_pairs={{0,4},{2,6},{4,0},{6,2},{1,5},{3,7},{5,1},{7,3},{8,12},{10,14},{12... | collective-permute-start | bytes 786440 | tf_op jit(solution)/shard_map/ppermute | solution.py:26
  111.0 1.1 copy-start.2
  114.2 0.9 copy-start.1
  115.1 45.1 %all-to-all-start.2 = ((bf16[24,4,4352]{2,1,0:T(4,128)(2,1)}), bf16[24,4,4352]{2,1,0:T(4,128)(2,1)}, u32[]{:S(2)}, u32[]{:S(2)}) async-start(bf16[24,4,4352]{2,1,0:T(4,128)(2,1)} %copy-done.1), calls=%async_computation.2 | async-start | bytes 1671168 | tf_op jit(solution)/shard_map/all_to_all | solution.py:17
  121.2 33.5 %collective-permute-start.9 = (bf16[32,4096]{1,0:T(8,128)(2,1)}, bf16[32,4096]{1,0:T(8,128)(2,1)S(1)}, u32[]{:S(2)}, u32[]{:S(2)}) collective-permute-start(bf16[32,4096]{1,0:T(8,128)(2,1)} %collective-permute-done.8), channel_id=1, source_target_pairs={{0,1},{1,0},{2,3},{3,2},{4,5},{5,4},{6,7},{7,6},{8,9},{9,8},{10,11... | collective-permute-start | bytes 786440 | tf_op jit(solution)/shard_map/ppermute | solution.py:30
  135.0 22.1 %collective-permute-start.11 = (bf16[32,4096]{1,0:T(8,128)(2,1)}, bf16[32,4096]{1,0:T(8,128)(2,1)S(1)}, u32[]{:S(2)}, u32[]{:S(2)}) collective-permute-start(bf16[32,4096]{1,0:T(8,128)(2,1)} %collective-permute-done.10), channel_id=1, source_target_pairs={{0,1},{1,0},{2,3},{3,2},{4,5},{5,4},{6,7},{7,6},{8,9},{9,8},{10,11... | collective-permute-start | bytes 786440 | tf_op jit(solution)/shard_map/ppermute | solution.py:30
  142.5 17.0 %collective-permute-start.13 = (bf16[32,4096]{1,0:T(8,128)(2,1)}, bf16[32,4096]{1,0:T(8,128)(2,1)S(1)}, u32[]{:S(2)}, u32[]{:S(2)}) collective-permute-start(bf16[32,4096]{1,0:T(8,128)(2,1)} %collective-permute-done.12), channel_id=1, source_target_pairs={{0,1},{1,0},{2,3},{3,2},{4,5},{5,4},{6,7},{7,6},{8,9},{9,8},{10,11... | collective-permute-start | bytes 786440 | tf_op jit(solution)/shard_map/ppermute | solution.py:30

commit v3 on v2

--- a/solution.py
+++ b/solution.py
@@ -70,6 +70,32 @@
     )(*blocks, rider)
 
 
+def rows_kernel(summands, resid, gain, grad_in, rows):
+    summed = [summands[i].astype(F32) for i in range(summands.shape[0])]
+    dnormed = (summed[0] + summed[1]) + (summed[2] + summed[3])
+    resid_f = resid[...].astype(F32)
+    inv = lax.rsqrt(jnp.mean(resid_f * resid_f, axis=-1, keepdims=True) + 1e-05)
+    unit = resid_f * inv
+    dunit = dnormed * gain[...].astype(F32)
+    inner = jnp.mean(dunit * unit, axis=-1, keepdims=True)
+    rows[...] = (grad_in[...].astype(F32) + inv * (dunit - unit * inner)).astype(BF16)
+
+
+def result_rows(summands, resid, gain, grad_in):
+    rows, width = resid.shape
+    return pl.pallas_call(
+        rows_kernel,
+        out_shape=jax.ShapeDtypeStruct((rows, width), BF16),
+        in_specs=[pl.BlockSpec(memory_space=pltpu.VMEM)] * 4,
+        out_specs=pl.BlockSpec(memory_space=pltpu.VMEM),
+        compiler_params=pltpu.CompilerParams(vmem_limit_bytes=10 * 2**20),
+        cost_estimate=pl.CostEstimate(
+            flops=15 * rows * width, bytes_accessed=14 * rows * width, transcendentals=0
+        ),
+        name="result_rows",
+    )(summands, resid, gain, grad_in)
+
+
 def body(resid, gain, grad_q, w_query, grad_in):
     tokens, width = resid.shape
     cols = grad_q.shape[1]
@@ -100,7 +126,7 @@
     kept = lax.optimization_barrier(term(own_start))
     pair = (kept.astype(F32) + got.astype(F32)).astype(BF16)
     pair, inv, ordered = lax.optimization_barrier((pair, inv, ordered))
-    dnormed = total(exchange(pair.reshape(n_zh, own, width), "zh"))
+    summands = exchange(pair.reshape(n_zh, own, width), "zh")
 
     unit = resid.astype(F32) * inv
     part = jnp.sum(sent.astype(F32) * rows_of(unit, other_start, half), axis=0)
@@ -120,22 +146,18 @@
 
     blocks = [block(s) for s in range(n_x)]
     blocks = [b if s == 0 else shifted(b, "x", s) for s, b in enumerate(blocks)]
-    for bit in (2, 4):
-        part = part + swapped(part, "y", bit)
+    part = part + swapped(part, "y", 2)
+    first = own_start + zh * own
+    ready = (blocks[0], rows_of(resid, first, own), rows_of(grad_in, first, own))
+    part, own_block, resid_rows, grad_rows = lax.optimization_barrier((part, *ready))
+    part = part + swapped(part, "y", 4)
     part = lax.dynamic_index_in_dim(part, lax.axis_index("y"), 0, keepdims=False)
 
-    first = own_start + zh * own
-    resid_rows = rows_of(resid, first, own)
-    inv_rows = rows_of(inv, first, own)
-    unit_rows = resid_rows.astype(F32) * inv_rows
-    dunit = dnormed * gain_f
-    inner = jnp.mean(dunit * unit_rows, axis=-1, keepdims=True)
     axes = ("x", "zh", "c")
-    part, inner = lax.optimization_barrier((part, inner))
+    part, summands = lax.optimization_barrier((part, summands))
     part = jnp.broadcast_to(part[None], (lax.axis_size(axes), *part.shape))
     part = total(exchange(part, axes))
-    rows = rows_of(grad_in, first, own).astype(F32) + inv_rows * (dunit - unit_rows * inner)
-    own_block, rows = lax.optimization_barrier((blocks[0], rows.astype(BF16)))
+    rows = result_rows(summands, resid_rows, gain.reshape(1, width), grad_rows)
 
     upper = part.astype(BF16)
     lower = (part - upper.astype(F32)).astype(BF16)

time: 165 us -> 170 us (1.030)
  the two profiles are of different devices: /device:TPU:121 before, /device:TPU:97 now
where the time goes in v3:
time: 170 us; the launch traced here: 169 us
  starting transfers between devices  84.5 us (50%)
  waiting for transfers between devices  36.2 us (21%)
  local copies, waits for them, and re-layouts  19.3 us (11%)
  other arithmetic  12.5 us (7%)
  matrix products  11.3 us (7%)
  Pallas kernels  3.74 us (2%)
    ppermute x8, starting transfers between devices, swapped(): lax.ppermute(block, axis, [(i, i ^ bit) for i in range(lax.axis_size(axis...  33.7 us
    all_to_all x3, starting transfers between devices, exchange(): return lax.all_to_all(blocks, axes, 0, 0, tiled=True)  28.1 us
    all_to_all x3, waiting for transfers between devices, exchange(): return lax.all_to_all(blocks, axes, 0, 0, tiled=True)  23.4 us
    ppermute x6, starting transfers between devices, shifted(): lax.ppermute(block, axis, [(i, (i + shift) % peers) for i in range(peers)])  22.7 us
    ppermute x6, waiting for transfers between devices, shifted(): lax.ppermute(block, axis, [(i, (i + shift) % peers) for i in range(peers)])  12.8 us
    dot_general x4, matrix products, block(): lax.dot_general(columns, normed, (((0,), (0,)), ((), ())), preferred_elem...  6.9 us
    dynamic_update_slice x4, local copies, waits for them, and re-layouts, body(): lax.dynamic_update_slice_in_dim(result, piece, own_start + source, 0)  5.72 us
    unnamed x22, local copies, waits for them, and re-layouts  4.23 us
  transfers between devices with their start and end apart: 17, of which 4 were waited for; matrix products, arithmetic and copies ran while one was open for 17% of the time, Pallas kernels for 2%

profile of v3, /device:TPU:97, one launch (start us, length us, event | category | flops | bytes accessed | tf_op | source)
XLA Modules:
  0.0 168.7 jit_solution(9791412277361326169)
XLA Ops:
  0.7 2.2 %fusion = f32[256]{0:T(256)S(1)} fusion(bf16[256,4096]{1,0:T(8,128)(2,1)} %param.5), kind=kLoop, calls=%fused_computation.9 | loop fusion | flops 3145472 | bytes 2098176 | tf_op jit(solution)/shard_map/reduce_sum | solution.py:113
  3.2 1.7 convolution_convert_fusion.1
  4.8 2.6 %collective-permute-start = (bf16[128,4096]{1,0:T(8,128)(2,1)}, bf16[128,4096]{1,0:T(8,128)(2,1)}, u32[]{:S(2)}, u32[]{:S(2)}) collective-permute-start(bf16[128,4096]{1,0:T(8,128)(2,1)} %convolution_convert_fusion.1), channel_id=1, source_target_pairs={{0,1},{1,0},{2,3},{3,2},{4,5},{5,4},{6,7},{7,6},{8,9},{9,8},{10,11... | collective-permute-start | bytes 3145736 | tf_op jit(solution)/shard_map/ppermute | solution.py:30
  7.5 1.7 %convolution_convert_fusion = bf16[128,4096]{1,0:T(8,128)(2,1)} fusion(bf16[384,4096]{1,0:T(8,128)(2,1)S(1)} %copy-done, bf16[256,384]{1,0:T(8,128)(2,1)S(1)} %copy-done.8, s32[]{:T(128)S(6)} %select_n.76), kind=kOutput, calls=%fused_computation.3 | convolution fusion | flops 403177472 | bytes 4292612 | tf_op jit(solution)/shard_map/dot_general | solution.py:117
  9.3 1.0 convolution_convert_fusion.6
  10.3 1.7 constant_dynamic-slice_fusion.3.resid
  12.0 1.7 constant_dynamic-slice_fusion.2.grad_in
  13.7 2.5 %fusion.3 = bf16[128,4096]{1,0:T(8,128)(2,1)} fusion(bf16[128,4096]{1,0:T(8,128)(2,1)S(1)} %copy-done.6, bf16[128,4096]{1,0:T(8,128)(2,1)} %collective-permute-done), kind=kLoop, calls=%fused_computation.14 | loop fusion | flops 2097152 | bytes 3145728 | tf_op jit(solution)/shard_map/convert_element_type | solution.py:127
  16.1 13.3 %all-to-all-start = ((bf16[4,32,4096]{2,1,0:T(8,128)(2,1)}), bf16[4,32,4096]{2,1,0:T(8,128)(2,1)}, u32[]{:S(2)}, u32[]{:S(2)}) async-start(bf16[4,32,4096]{2,1,0:T(8,128)(2,1)} %bitcast.12), calls=%async_computation | async-start | bytes 2097152 | tf_op jit(solution)/shard_map/all_to_all | solution.py:17
  29.5 2.2 %convert_multiply_fusion.1 = f32[256,4096]{1,0:T(8,128)S(1)} fusion(bf16[256,4096]{1,0:T(8,128)(2,1)} %param.5, f32[256]{0:T(256)S(1)} %add_rsqrt_fusion), kind=kLoop, calls=%fused_computation.1 | loop fusion | flops 2097152 | bytes 6292480 | tf_op jit(solution)/shard_map/mul | solution.py:131
  31.7 2.0 %fusion.4 = (f32[4096]{0:T(1024)S(1)}, f32[4096]{0:T(1024)S(1)}) fusion(bf16[128,4096]{1,0:T(8,128)(2,1)S(1)} %copy-done.7, f32[256,4096]{1,0:T(8,128)S(1)} %convert_multiply_fusion.1, s32[]{:T(128)S(6)} %select_n.76, s32[]{:T(128)S(6)} %select_n.75, bf16[128,4096]{1,0:T(8,128)(2,1)} %convolution_convert_fusion.1), kind=kLoop, calls=%fused_computation.15 | loop fusion | flops 3137536 | bytes 6324232 | tf_op jit(solution)/shard_map/reduce_sum | solution.py:133
  33.7 2.3 %collective-permute-start.1 = (f32[8,4,128]{2,1,0:T(4,128)S(1)}, f32[8,4,128]{2,1,0:T(4,128)S(1)}, u32[]{:S(2)}, u32[]{:S(2)}) collective-permute-start(f32[8,4,128]{2,1,0:T(4,128)S(1)} %bitcast.14), channel_id=1, source_target_pairs={{0,32},{32,0},{64,96},{96,64},{128,160},{160,128},{192,224},{224,1... | collective-permute-start | bytes 49160 | tf_op jit(solution)/shard_map/ppermute | solution.py:30
  36.0 1.7 %convolution_convert_fusion.5.first = bf16[96,4096]{1,0:T(8,128)(2,1)} fusion(bf16[256,384]{1,0:T(8,128)(2,1)S(1)} %copy-done.10, bf16[256,4096]{1,0:T(8,128)(2,1)S(1)} %copy-done.5, f32[4096]{0:T(1024)S(1)} %convert_element_type.69, f32[256]{0:T(256)S(1)} %add_rsqrt_fusion), kind=kOutput, calls=%fused_computation.8 | convolution fusion | flops 205914112 | bytes 2966528 | tf_op jit(solution)/shard_map/dot_general | solution.py:142
  37.7 1.7 %convolution_convert_fusion.2 = bf16[96,4096]{1,0:T(8,128)(2,1)} fusion(bf16[256,384]{1,0:T(8,128)(2,1)S(1)} %copy-done.10, bf16[256,4096]{1,0:T(8,128)(2,1)S(1)} %copy-done.5, f32[4096]{0:T(1024)S(1)} %convert_element_type.69, f32[256]{0:T(256)S(1)} %add_rsqrt_fusion), kind=kOutput, calls=%fused_computation.5 | convolution fusion | flops 205914112 | bytes 2966528 | tf_op jit(solution)/shard_map/dot_general | solution.py:142
  39.5 2.4 %collective-permute-start.2 = (f32[8,4,128]{2,1,0:T(4,128)S(1)}, f32[8,4,128]{2,1,0:T(4,128)S(1)}, u32[]{:S(2)}, u32[]{:S(2)}) collective-permute-start(f32[8,4,128]{2,1,0:T(4,128)S(1)} %add.184), channel_id=1, source_target_pairs={{0,64},{32,96},{64,0},{96,32},{128,192},{160,224},{192,128},{224,1... | collective-permute-start | bytes 49160 | tf_op jit(solution)/shard_map/ppermute | solution.py:30
  41.9 1.8 %convolution_convert_fusion.3 = bf16[96,4096]{1,0:T(8,128)(2,1)} fusion(bf16[256,384]{1,0:T(8,128)(2,1)S(1)} %copy-done.10, bf16[256,4096]{1,0:T(8,128)(2,1)S(1)} %copy-done.5, f32[4096]{0:T(1024)S(1)} %convert_element_type.69, f32[256]{0:T(256)S(1)} %add_rsqrt_fusion), kind=kOutput, calls=%fused_computation.6 | convolution fusion | flops 205914112 | bytes 2966528 | tf_op jit(solution)/shard_map/dot_general | solution.py:142
  43.6 4.4 %collective-permute-start.5 = (bf16[96,4096]{1,0:T(8,128)(2,1)}, bf16[96,4096]{1,0:T(8,128)(2,1)}, u32[]{:S(2)}, u32[]{:S(2)}) collective-permute-start(bf16[96,4096]{1,0:T(8,128)(2,1)} %convolution_convert_fusion.2), channel_id=1, source_target_pairs={{0,24},{8,0},{16,8},{24,16},{1,25},{9,1},{17,9},{25,17},{2,26},{10... | collective-permute-start | bytes 2359304 | tf_op jit(solution)/shard_map/ppermute | solution.py:26
  48.0 2.4 %collective-permute-start.4 = (bf16[96,4096]{1,0:T(8,128)(2,1)}, bf16[96,4096]{1,0:T(8,128)(2,1)}, u32[]{:S(2)}, u32[]{:S(2)}) collective-permute-start(bf16[96,4096]{1,0:T(8,128)(2,1)} %convolution_convert_fusion.3), channel_id=1, source_target_pairs={{0,16},{8,24},{16,0},{24,8},{1,17},{9,25},{17,1},{25,9},{2,18},{10... | collective-permute-start | bytes 2359304 | tf_op jit(solution)/shard_map/ppermute | solution.py:26
  50.5 4.4 %collective-permute-start.6 = (f32[8,4,128]{2,1,0:T(4,128)S(1)}, f32[8,4,128]{2,1,0:T(4,128)S(1)}, u32[]{:S(2)}, u32[]{:S(2)}) collective-permute-start(f32[8,4,128]{2,1,0:T(4,128)S(1)} %add.185), channel_id=1, source_target_pairs={{0,128},{32,160},{64,192},{96,224},{128,0},{160,32},{192,64},{224,... | collective-permute-start | bytes 49160 | tf_op jit(solution)/shard_map/ppermute | solution.py:30
  54.9 1.7 %convolution_convert_fusion.4 = bf16[96,4096]{1,0:T(8,128)(2,1)} fusion(bf16[256,384]{1,0:T(8,128)(2,1)S(1)} %copy-done.10, bf16[256,4096]{1,0:T(8,128)(2,1)S(1)} %copy-done.5, f32[4096]{0:T(1024)S(1)} %convert_element_type.69, f32[256]{0:T(256)S(1)} %add_rsqrt_fusion), kind=kOutput, calls=%fused_computation.7 | convolution fusion | flops 205914112 | bytes 2966528 | tf_op jit(solution)/shard_map/dot_general | solution.py:142
  56.6 2.5 %collective-permute-start.3 = (bf16[96,4096]{1,0:T(8,128)(2,1)}, bf16[96,4096]{1,0:T(8,128)(2,1)}, u32[]{:S(2)}, u32[]{:S(2)}) collective-permute-start(bf16[96,4096]{1,0:T(8,128)(2,1)} %convolution_convert_fusion.4), channel_id=1, source_target_pairs={{0,8},{8,16},{16,24},{24,0},{1,9},{9,17},{17,25},{25,1},{2,10},{10... | collective-permute-start | bytes 2359304 | tf_op jit(solution)/shard_map/ppermute | solution.py:26
  59.2 11.7 %all-to-all-done.summands = bf16[4,32,4096]{2,1,0:T(8,128)(2,1)} async-done(((bf16[4,32,4096]{2,1,0:T(8,128)(2,1)}), bf16[4,32,4096]{2,1,0:T(8,128)(2,1)}, u32[]{:S(2)}, u32[]{:S(2)}) %all-to-all-start) | async-done | bytes 1048608 | tf_op jit(solution)/shard_map/all_to_all | solution.py:17
  70.9 0.9 copy-done.2
  71.9 0.9 copy-done.3
  72.8 1.7 %result_rows.1 = bf16[32,4096]{1,0:T(8,128)(2,1)S(1)} custom-call(bf16[4,32,4096]{2,1,0:T(8,128)(2,1)} %all-to-all-done.summands, bf16[32,4096]{1,0:T(8,128)(2,1)S(1)} %copy-done.2, bf16[1,4096]{1,0:T(2,128)(2,1)S(1)} %reshape.93.gain, bf16[32,4096]{1,0:T(8,128)(2,1)S(1)} %copy-done.3), custom_call_target="tpu_custom_call" | custom-call | flops 1966080 | bytes 1835008 | tf_op jit(solution)/shard_map/result_rows/pallas_call | solution.py:86
  74.5 3.0 %collective-permute-start.7 = (bf16[32,4096]{1,0:T(8,128)(2,1)S(1)}, bf16[32,4096]{1,0:T(8,128)(2,1)}, u32[]{:S(2)}, u32[]{:S(2)}) collective-permute-start(bf16[32,4096]{1,0:T(8,128)(2,1)S(1)} %result_rows.1), channel_id=1, source_target_pairs={{0,1},{1,0},{2,3},{3,2},{4,5},{5,4},{6,7},{7,6},{8,9},{9,8},{10,11... | collective-permute-start | bytes 786440 | tf_op jit(solution)/shard_map/ppermute | solution.py:30
  77.5 3.7 %collective-permute-start.8 = (bf16[32,4096]{1,0:T(8,128)(2,1)S(1)}, bf16[32,4096]{1,0:T(8,128)(2,1)}, u32[]{:S(2)}, u32[]{:S(2)}) collective-permute-start(bf16[32,4096]{1,0:T(8,128)(2,1)S(1)} %result_rows.1), channel_id=1, source_target_pairs={{0,2},{2,4},{4,6},{6,0},{1,3},{3,5},{5,7},{7,1},{8,10},{10,12},{12... | collective-permute-start | bytes 786440 | tf_op jit(solution)/shard_map/ppermute | solution.py:26
  81.9 7.1 %all-to-all-start.1 = ((f32[32,4,128]{2,1,0:T(4,128)}), f32[32,4,128]{2,1,0:T(4,128)S(1)}, u32[]{:S(2)}, u32[]{:S(2)}) async-start(f32[32,4,128]{2,1,0:T(4,128)} %broadcast_in_dim.4), calls=%async_computation.1 | async-start | bytes 131072 | tf_op jit(solution)/shard_map/all_to_all | solution.py:17
  89.0 1.6 broadcast_in_dim.5
  91.3 11.7 %all-to-all-done.1 = f32[32,4,128]{2,1,0:T(4,128)S(1)} async-done(((f32[32,4,128]{2,1,0:T(4,128)}), f32[32,4,128]{2,1,0:T(4,128)S(1)}, u32[]{:S(2)}, u32[]{:S(2)}) %all-to-all-start.1) | async-done | bytes 65568 | tf_op jit(solution)/shard_map/all_to_all | solution.py:17
  103.0 1.9 %collective-permute-start.10 = (bf16[32,4096]{1,0:T(8,128)(2,1)S(1)}, bf16[32,4096]{1,0:T(8,128)(2,1)}, u32[]{:S(2)}, u32[]{:S(2)}) collective-permute-start(bf16[32,4096]{1,0:T(8,128)(2,1)S(1)} %result_rows.1), channel_id=1, source_target_pairs={{0,6},{2,0},{4,2},{6,4},{1,7},{3,1},{5,3},{7,5},{8,14},{10,8},{12,... | collective-permute-start | bytes 786440 | tf_op jit(solution)/shard_map/ppermute | solution.py:26
  104.9 7.7 %collective-permute-start.12 = (bf16[32,4096]{1,0:T(8,128)(2,1)S(1)}, bf16[32,4096]{1,0:T(8,128)(2,1)}, u32[]{:S(2)}, u32[]{:S(2)}) collective-permute-start(bf16[32,4096]{1,0:T(8,128)(2,1)S(1)} %result_rows.1), channel_id=1, source_target_pairs={{0,4},{2,6},{4,0},{6,2},{1,5},{3,7},{5,1},{7,3},{8,12},{10,14},{12... | collective-permute-start | bytes 786440 | tf_op jit(solution)/shard_map/ppermute | solution.py:26
  112.7 1.1 copy-done.4
  113.8 2.0 %pack.1 = bf16[24,4,4352]{2,1,0:T(4,128)(2,1)S(1)} custom-call(bf16[96,4096]{1,0:T(8,128)(2,1)S(1)} %copy-done.4, bf16[96,4096]{1,0:T(8,128)(2,1)} %collective-permute-done.3.second, bf16[96,4096]{1,0:T(8,128)(2,1)} %collective-permute-done.4.third, bf16[96,4096]{1,0:T(8,128)(2,1)} %collective-permute-done.5.fourth, bf16[4,256]{1,0:T(4,128)(2,1)S(1)} %pad_maximum_fusion.rider), custom_call_target="tpu_custom_call" | custom-call | flops 1179648 | bytes 3932160 | tf_op jit(solution)/shard_map/pack/pallas_call | solution.py:60
  115.9 0.9 copy-done.1
  116.8 7.6 %all-to-all-start.2 = ((bf16[24,4,4352]{2,1,0:T(4,128)(2,1)}), bf16[24,4,4352]{2,1,0:T(4,128)(2,1)}, u32[]{:S(2)}, u32[]{:S(2)}) async-start(bf16[24,4,4352]{2,1,0:T(4,128)(2,1)} %copy-done.1), calls=%async_computation.2 | async-start | bytes 1671168 | tf_op jit(solution)/shard_map/all_to_all | solution.py:17
  124.5 5.0 %collective-permute-start.9 = (bf16[32,4096]{1,0:T(8,128)(2,1)}, bf16[32,4096]{1,0:T(8,128)(2,1)S(1)}, u32[]{:S(2)}, u32[]{:S(2)}) collective-permute-start(bf16[32,4096]{1,0:T(8,128)(2,1)} %collective-permute-done.8), channel_id=1, source_target_pairs={{0,1},{1,0},{2,3},{3,2},{4,5},{5,4},{6,7},{7,6},{8,9},{9,8},{10,11... | collective-permute-start | bytes 786440 | tf_op jit(solution)/shard_map/ppermute | solution.py:30
  129.5 10.6 %collective-permute-done.10 = bf16[32,4096]{1,0:T(8,128)(2,1)} collective-permute-done((bf16[32,4096]{1,0:T(8,128)(2,1)S(1)}, bf16[32,4096]{1,0:T(8,128)(2,1)}, u32[]{:S(2)}, u32[]{:S(2)}) %collective-permute-start.10) | collective-permute-done | bytes 262176 | tf_op jit(solution)/shard_map/ppermute | solution.py:26
  140.1 2.4 %collective-permute-start.11 = (bf16[32,4096]{1,0:T(8,128)(2,1)}, bf16[32,4096]{1,0:T(8,128)(2,1)S(1)}, u32[]{:S(2)}, u32[]{:S(2)}) collective-permute-start(bf16[32,4096]{1,0:T(8,128)(2,1)} %collective-permute-done.10), channel_id=1, source_target_pairs={{0,1},{1,0},{2,3},{3,2},{4,5},{5,4},{6,7},{7,6},{8,9},{9,8},{10,11... | collective-permute-start | bytes 786440 | tf_op jit(solution)/shard_map/ppermute | solution.py:30
  142.4 2.2 %collective-permute-done.12 = bf16[32,4096]{1,0:T(8,128)(2,1)} collective-permute-done((bf16[32,4096]{1,0:T(8,128)(2,1)S(1)}, bf16[32,4096]{1,0:T(8,128)(2,1)}, u32[]{:S(2)}, u32[]{:S(2)}) %collective-permute-start.12) | collective-permute-done | bytes 262176 | tf_op jit(solution)/shard_map/ppermute | solution.py:26
  144.6 11.7 %collective-permute-start.13 = (bf16[32,4096]{1,0:T(8,128)(2,1)}, bf16[32,4096]{1,0:T(8,128)(2,1)S(1)}, u32[]{:S(2)}, u32[]{:S(2)}) collective-permute-start(bf16[32,4096]{1,0:T(8,128)(2,1)} %collective-permute-done.12), channel_id=1, source_target_pairs={{0,1},{1,0},{2,3},{3,2},{4,5},{5,4},{6,7},{7,6},{8,9},{9,8},{10,11... | collective-permute-start | bytes 786440 | tf_op jit(solution)/shard_map/ppermute | solution.py:30
  156.3 1.7 constant_dynamic-update-slice_fusion.6
  158.0 1.7 constant_dynamic-update-slice_fusion.5
  159.7 0.7 constant_dynamic-update-slice_fusion.4
  160.4 1.7 constant_dynamic-update-slice_fusion.3
  162.8 1.7 constant_dynamic-update-slice_fusion.1
  165.2 0.8 slice_convert_fusion
  166.6 2.1 %convert_reduce_fusion = f32[4,4096]{1,0:T(4,128)} fusion(bf16[24,4,4352]{2,1,0:T(4,128)(2,1)} %all-to-all-done.2), kind=kLoop, calls=%fused_computation.17 | loop fusion | flops 770048 | bytes 851968 | tf_op jit(solution)/shard_map/reduce_sum | solution.py:21
  (48 shorter events, 3.9 us)
Async XLA Ops:
  0.6 2.5 %copy-start = (bf16[384,4096]{1,0:T(8,128)(2,1)S(1)}, bf16[384,4096]{1,0:T(8,128)(2,1)}, u32[]{:S(2)}) copy-start(bf16[384,4096]{1,0:T(8,128)(2,1)} %param.8) | copy-start | bytes 9437188
  0.6 2.5 %copy-start.8 = (bf16[256,384]{1,0:T(8,128)(2,1)S(1)}, bf16[256,384]{1,0:T(8,128)(2,1)}, u32[]{:S(2)}) copy-start(bf16[256,384]{1,0:T(8,128)(2,1)} %param.7) | copy-start | bytes 589828
  3.2 4.3 %copy-start.9 = (bf16[4096]{0:T(1024)(128)(2,1)S(1)}, bf16[4096]{0:T(1024)(128)(2,1)}, u32[]{:S(2)}) copy-start(bf16[4096]{0:T(1024)(128)(2,1)} %param.6) | copy-start | bytes 24580
  4.8 8.8 %collective-permute-start = (bf16[128,4096]{1,0:T(8,128)(2,1)}, bf16[128,4096]{1,0:T(8,128)(2,1)}, u32[]{:S(2)}, u32[]{:S(2)}) collective-permute-start(bf16[128,4096]{1,0:T(8,128)(2,1)} %convolution_convert_fusion.1), channel_id=1, source_target_pairs={{0,1},{1,0},{2,3},{3,2},{4,5},{5,4},{6,7},{7,6},{8,9},{9,8},{10,11... | collective-permute-start | bytes 3145736 | tf_op jit(solution)/shard_map/ppermute | solution.py:30
  9.3 4.4 %copy-start.6 = (bf16[128,4096]{1,0:T(8,128)(2,1)S(1)}, bf16[128,4096]{1,0:T(8,128)(2,1)}, u32[]{:S(2)}) copy-start(bf16[128,4096]{1,0:T(8,128)(2,1)} %convolution_convert_fusion) | copy-start | bytes 3145732
  16.1 54.8 %all-to-all-start = ((bf16[4,32,4096]{2,1,0:T(8,128)(2,1)}), bf16[4,32,4096]{2,1,0:T(8,128)(2,1)}, u32[]{:S(2)}, u32[]{:S(2)}) async-start(bf16[4,32,4096]{2,1,0:T(8,128)(2,1)} %bitcast.12), calls=%async_computation | async-start | bytes 2097152 | tf_op jit(solution)/shard_map/all_to_all | solution.py:17
  29.4 2.2 %copy-start.7 = (bf16[128,4096]{1,0:T(8,128)(2,1)S(1)}, bf16[128,4096]{1,0:T(8,128)(2,1)}, u32[]{:S(2)}) copy-start(bf16[128,4096]{1,0:T(8,128)(2,1)} %convolution_convert_fusion) | copy-start | bytes 3145732
  31.7 4.3 %copy-start.5 = (bf16[256,4096]{1,0:T(8,128)(2,1)S(1)}, bf16[256,4096]{1,0:T(8,128)(2,1)}, u32[]{:S(2)}) copy-start(bf16[256,4096]{1,0:T(8,128)(2,1)} %param.5) | copy-start | bytes 6291460
  31.7 4.3 %copy-start.10 = (bf16[256,384]{1,0:T(8,128)(2,1)S(1)}, bf16[256,384]{1,0:T(8,128)(2,1)}, u32[]{:S(2)}) copy-start(bf16[256,384]{1,0:T(8,128)(2,1)} %convolution_convert_fusion.6) | copy-start | bytes 589828
  33.7 5.8 %collective-permute-start.1 = (f32[8,4,128]{2,1,0:T(4,128)S(1)}, f32[8,4,128]{2,1,0:T(4,128)S(1)}, u32[]{:S(2)}, u32[]{:S(2)}) collective-permute-start(f32[8,4,128]{2,1,0:T(4,128)S(1)} %bitcast.14), channel_id=1, source_target_pairs={{0,32},{32,0},{64,96},{96,64},{128,160},{160,128},{192,224},{224,1... | collective-permute-start | bytes 49160 | tf_op jit(solution)/shard_map/ppermute | solution.py:30
  39.5 11.0 %collective-permute-start.2 = (f32[8,4,128]{2,1,0:T(4,128)S(1)}, f32[8,4,128]{2,1,0:T(4,128)S(1)}, u32[]{:S(2)}, u32[]{:S(2)}) collective-permute-start(f32[8,4,128]{2,1,0:T(4,128)S(1)} %add.184), channel_id=1, source_target_pairs={{0,64},{32,96},{64,0},{96,32},{128,192},{160,224},{192,128},{224,1... | collective-permute-start | bytes 49160 | tf_op jit(solution)/shard_map/ppermute | solution.py:30
  43.6 59.3 %collective-permute-start.5 = (bf16[96,4096]{1,0:T(8,128)(2,1)}, bf16[96,4096]{1,0:T(8,128)(2,1)}, u32[]{:S(2)}, u32[]{:S(2)}) collective-permute-start(bf16[96,4096]{1,0:T(8,128)(2,1)} %convolution_convert_fusion.2), channel_id=1, source_target_pairs={{0,24},{8,0},{16,8},{24,16},{1,25},{9,1},{17,9},{25,17},{2,26},{10... | collective-permute-start | bytes 2359304 | tf_op jit(solution)/shard_map/ppermute | solution.py:26
  48.0 56.9 %collective-permute-start.4 = (bf16[96,4096]{1,0:T(8,128)(2,1)}, bf16[96,4096]{1,0:T(8,128)(2,1)}, u32[]{:S(2)}, u32[]{:S(2)}) collective-permute-start(bf16[96,4096]{1,0:T(8,128)(2,1)} %convolution_convert_fusion.3), channel_id=1, source_target_pairs={{0,16},{8,24},{16,0},{24,8},{1,17},{9,25},{17,1},{25,9},{2,18},{10... | collective-permute-start | bytes 2359304 | tf_op jit(solution)/shard_map/ppermute | solution.py:26
  50.5 8.7 %collective-permute-start.6 = (f32[8,4,128]{2,1,0:T(4,128)S(1)}, f32[8,4,128]{2,1,0:T(4,128)S(1)}, u32[]{:S(2)}, u32[]{:S(2)}) collective-permute-start(f32[8,4,128]{2,1,0:T(4,128)S(1)} %add.185), channel_id=1, source_target_pairs={{0,128},{32,160},{64,192},{96,224},{128,0},{160,32},{192,64},{224,... | collective-permute-start | bytes 49160 | tf_op jit(solution)/shard_map/ppermute | solution.py:30
  56.6 56.0 %collective-permute-start.3 = (bf16[96,4096]{1,0:T(8,128)(2,1)}, bf16[96,4096]{1,0:T(8,128)(2,1)}, u32[]{:S(2)}, u32[]{:S(2)}) collective-permute-start(bf16[96,4096]{1,0:T(8,128)(2,1)} %convolution_convert_fusion.4), channel_id=1, source_target_pairs={{0,8},{8,16},{16,24},{24,0},{1,9},{9,17},{17,25},{25,1},{2,10},{10... | collective-permute-start | bytes 2359304 | tf_op jit(solution)/shard_map/ppermute | solution.py:26
  70.9 1.0 copy-start.2
  71.9 0.9 copy-start.3
  74.5 81.8 %collective-permute-start.7 = (bf16[32,4096]{1,0:T(8,128)(2,1)S(1)}, bf16[32,4096]{1,0:T(8,128)(2,1)}, u32[]{:S(2)}, u32[]{:S(2)}) collective-permute-start(bf16[32,4096]{1,0:T(8,128)(2,1)S(1)} %result_rows.1), channel_id=1, source_target_pairs={{0,1},{1,0},{2,3},{3,2},{4,5},{5,4},{6,7},{7,6},{8,9},{9,8},{10,11... | collective-permute-start | bytes 786440 | tf_op jit(solution)/shard_map/ppermute | solution.py:30
  77.5 47.0 %collective-permute-start.8 = (bf16[32,4096]{1,0:T(8,128)(2,1)S(1)}, bf16[32,4096]{1,0:T(8,128)(2,1)}, u32[]{:S(2)}, u32[]{:S(2)}) collective-permute-start(bf16[32,4096]{1,0:T(8,128)(2,1)S(1)} %result_rows.1), channel_id=1, source_target_pairs={{0,2},{2,4},{4,6},{6,0},{1,3},{3,5},{5,7},{7,1},{8,10},{10,12},{12... | collective-permute-start | bytes 786440 | tf_op jit(solution)/shard_map/ppermute | solution.py:26
  81.9 21.1 %all-to-all-start.1 = ((f32[32,4,128]{2,1,0:T(4,128)}), f32[32,4,128]{2,1,0:T(4,128)S(1)}, u32[]{:S(2)}, u32[]{:S(2)}) async-start(f32[32,4,128]{2,1,0:T(4,128)} %broadcast_in_dim.4), calls=%async_computation.1 | async-start | bytes 131072 | tf_op jit(solution)/shard_map/all_to_all | solution.py:17
  103.0 37.1 %collective-permute-start.10 = (bf16[32,4096]{1,0:T(8,128)(2,1)S(1)}, bf16[32,4096]{1,0:T(8,128)(2,1)}, u32[]{:S(2)}, u32[]{:S(2)}) collective-permute-start(bf16[32,4096]{1,0:T(8,128)(2,1)S(1)} %result_rows.1), channel_id=1, source_target_pairs={{0,6},{2,0},{4,2},{6,4},{1,7},{3,1},{5,3},{7,5},{8,14},{10,8},{12,... | collective-permute-start | bytes 786440 | tf_op jit(solution)/shard_map/ppermute | solution.py:26
  104.9 39.7 %collective-permute-start.12 = (bf16[32,4096]{1,0:T(8,128)(2,1)S(1)}, bf16[32,4096]{1,0:T(8,128)(2,1)}, u32[]{:S(2)}, u32[]{:S(2)}) collective-permute-start(bf16[32,4096]{1,0:T(8,128)(2,1)S(1)} %result_rows.1), channel_id=1, source_target_pairs={{0,4},{2,6},{4,0},{6,2},{1,5},{3,7},{5,1},{7,3},{8,12},{10,14},{12... | collective-permute-start | bytes 786440 | tf_op jit(solution)/shard_map/ppermute | solution.py:26
  112.7 1.1 copy-start.4
  115.9 0.9 copy-start.1
  116.8 48.4 %all-to-all-start.2 = ((bf16[24,4,4352]{2,1,0:T(4,128)(2,1)}), bf16[24,4,4352]{2,1,0:T(4,128)(2,1)}, u32[]{:S(2)}, u32[]{:S(2)}) async-start(bf16[24,4,4352]{2,1,0:T(4,128)(2,1)} %copy-done.1), calls=%async_computation.2 | async-start | bytes 1671168 | tf_op jit(solution)/shard_map/all_to_all | solution.py:17
  124.5 35.2 %collective-permute-start.9 = (bf16[32,4096]{1,0:T(8,128)(2,1)}, bf16[32,4096]{1,0:T(8,128)(2,1)S(1)}, u32[]{:S(2)}, u32[]{:S(2)}) collective-permute-start(bf16[32,4096]{1,0:T(8,128)(2,1)} %collective-permute-done.8), channel_id=1, source_target_pairs={{0,1},{1,0},{2,3},{3,2},{4,5},{5,4},{6,7},{7,6},{8,9},{9,8},{10,11... | collective-permute-start | bytes 786440 | tf_op jit(solution)/shard_map/ppermute | solution.py:30
  140.1 22.0 %collective-permute-start.11 = (bf16[32,4096]{1,0:T(8,128)(2,1)}, bf16[32,4096]{1,0:T(8,128)(2,1)S(1)}, u32[]{:S(2)}, u32[]{:S(2)}) collective-permute-start(bf16[32,4096]{1,0:T(8,128)(2,1)} %collective-permute-done.10), channel_id=1, source_target_pairs={{0,1},{1,0},{2,3},{3,2},{4,5},{5,4},{6,7},{7,6},{8,9},{9,8},{10,11... | collective-permute-start | bytes 786440 | tf_op jit(solution)/shard_map/ppermute | solution.py:30
  144.6 19.8 %collective-permute-start.13 = (bf16[32,4096]{1,0:T(8,128)(2,1)}, bf16[32,4096]{1,0:T(8,128)(2,1)S(1)}, u32[]{:S(2)}, u32[]{:S(2)}) collective-permute-start(bf16[32,4096]{1,0:T(8,128)(2,1)} %collective-permute-done.12), channel_id=1, source_target_pairs={{0,1},{1,0},{2,3},{3,2},{4,5},{5,4},{6,7},{7,6},{8,9},{9,8},{10,11... | collective-permute-start | bytes 786440 | tf_op jit(solution)/shard_map/ppermute | solution.py:30

commit v4 on v3

--- a/solution.py
+++ b/solution.py
@@ -70,30 +70,74 @@
     )(*blocks, rider)
 
 
-def rows_kernel(summands, resid, gain, grad_in, rows):
+def sums_kernel(last, weight_grad, gain_grad):
+    width = weight_grad.shape[1]
+    summed = last[0].astype(F32)
+    for one in range(1, last.shape[0]):
+        summed = summed + last[one].astype(F32)
+    weight_grad[...] = summed[:, :width]
+    extra = summed.shape[1] - width
+    for row in range(summed.shape[0]):
+        gain_grad[:, row * extra : (row + 1) * extra] = summed[row : row + 1, width:]
+
+
+def last_sums(last, width):
+    peers, rows, lanes = last.shape
+    return pl.pallas_call(
+        sums_kernel,
+        out_shape=(
+            jax.ShapeDtypeStruct((rows, width), F32),
+            jax.ShapeDtypeStruct((1, rows * (lanes - width)), F32),
+        ),
+        in_specs=[pl.BlockSpec(memory_space=pltpu.VMEM)],
+        out_specs=[pl.BlockSpec(memory_space=pltpu.VMEM)] * 2,
+        compiler_params=pltpu.CompilerParams(vmem_limit_bytes=10 * 2**20),
+        cost_estimate=pl.CostEstimate(
+            flops=peers * rows * lanes, bytes_accessed=2 * peers * rows * lanes, transcendentals=0
+        ),
+        name="last_sums",
+    )(last)
+
+
+def rows_kernel(first, summands, gain, resid, grad_in, rows, held, sems):
+    place = pl.ds(pl.multiple_of(first[0], 32), rows.shape[0])
+    copies = [
+        pltpu.make_async_copy(array.at[place, :], held.at[i], sems.at[i])
+        for i, array in enumerate((resid, grad_in))
+    ]
+    for copy in copies:
+        copy.start()
     summed = [summands[i].astype(F32) for i in range(summands.shape[0])]
-    dnormed = (summed[0] + summed[1]) + (summed[2] + summed[3])
-    resid_f = resid[...].astype(F32)
+    dunit = ((summed[0] + summed[1]) + (summed[2] + summed[3])) * gain[...].astype(F32)
+    copies[0].wait()
+    resid_f = held[0].astype(F32)
     inv = lax.rsqrt(jnp.mean(resid_f * resid_f, axis=-1, keepdims=True) + 1e-05)
     unit = resid_f * inv
-    dunit = dnormed * gain[...].astype(F32)
     inner = jnp.mean(dunit * unit, axis=-1, keepdims=True)
-    rows[...] = (grad_in[...].astype(F32) + inv * (dunit - unit * inner)).astype(BF16)
-
-
-def result_rows(summands, resid, gain, grad_in):
-    rows, width = resid.shape
+    copies[1].wait()
+    rows[...] = (held[1].astype(F32) + inv * (dunit - unit * inner)).astype(BF16)
+
+
+def result_rows(first, summands, gain, resid, grad_in):
+    _, rows, width = summands.shape
     return pl.pallas_call(
         rows_kernel,
         out_shape=jax.ShapeDtypeStruct((rows, width), BF16),
-        in_specs=[pl.BlockSpec(memory_space=pltpu.VMEM)] * 4,
+        in_specs=[
+            pl.BlockSpec(memory_space=pltpu.SMEM),
+            pl.BlockSpec(memory_space=pltpu.VMEM),
+            pl.BlockSpec(memory_space=pltpu.VMEM),
+            pl.BlockSpec(memory_space=pltpu.HBM),
+            pl.BlockSpec(memory_space=pltpu.HBM),
+        ],
         out_specs=pl.BlockSpec(memory_space=pltpu.VMEM),
-        compiler_params=pltpu.CompilerParams(vmem_limit_bytes=10 * 2**20),
+        scratch_shapes=[pltpu.VMEM((2, rows, width), BF16), pltpu.SemaphoreType.DMA((2,))],
+        compiler_params=pltpu.CompilerParams(vmem_limit_bytes=125 * 2**19),
         cost_estimate=pl.CostEstimate(
             flops=15 * rows * width, bytes_accessed=14 * rows * width, transcendentals=0
         ),
         name="result_rows",
-    )(summands, resid, gain, grad_in)
+    )(first, summands, gain, resid, grad_in)
 
 
 def body(resid, gain, grad_q, w_query, grad_in):
@@ -131,8 +175,10 @@
     unit = resid.astype(F32) * inv
     part = jnp.sum(sent.astype(F32) * rows_of(unit, other_start, half), axis=0)
     part = part + jnp.sum(kept.astype(F32) * rows_of(unit, own_start, half), axis=0)
-    part, inv_x = lax.optimization_barrier((part.reshape(n_y, -1, 128), inv))
-    part = part + swapped(part, "y", 1)
+    part, inv_x = lax.optimization_barrier((part.reshape(-1, 128), inv))
+    part = part + swapped(part, "x", 1)
+    part, inv_x = lax.optimization_barrier((part, inv_x))
+    part_x = swapped(part, "x", 2)
 
     normed = (resid.astype(F32) * inv_x * gain_f).astype(BF16)
     share = cols // n_x
@@ -146,27 +192,19 @@
 
     blocks = [block(s) for s in range(n_x)]
     blocks = [b if s == 0 else shifted(b, "x", s) for s, b in enumerate(blocks)]
-    part = part + swapped(part, "y", 2)
-    first = own_start + zh * own
-    ready = (blocks[0], rows_of(resid, first, own), rows_of(grad_in, first, own))
-    part, own_block, resid_rows, grad_rows = lax.optimization_barrier((part, *ready))
-    part = part + swapped(part, "y", 4)
-    part = lax.dynamic_index_in_dim(part, lax.axis_index("y"), 0, keepdims=False)
-
-    axes = ("x", "zh", "c")
+    first = (own_start + zh * own).astype(jnp.int32).reshape(1)
+    ready = (part + part_x, blocks[0], first, gain.reshape(1, width))
+    part, own_block, first, gain_row = lax.optimization_barrier(ready)
+
     part, summands = lax.optimization_barrier((part, summands))
-    part = jnp.broadcast_to(part[None], (lax.axis_size(axes), *part.shape))
-    part = total(exchange(part, axes))
-    rows = result_rows(summands, resid_rows, gain.reshape(1, width), grad_rows)
-
-    upper = part.astype(BF16)
-    lower = (part - upper.astype(F32)).astype(BF16)
-    packed = pack([own_block, *blocks[1:]], jnp.concatenate([upper, lower], axis=1))
+    part = jnp.broadcast_to(part[None], (lax.axis_size(TP), *part.shape))
+    part = total(exchange(part, TP))
+    rows = result_rows(first, summands, gain_row, resid, grad_in)
+
+    mine = share // (n_y * n_zl)
+    packed = pack([own_block, *blocks[1:]], part.astype(BF16).reshape(mine, -1))
     last = exchange(packed, ("zl", "y"))
-    weight_grad = total(last[:, :, :width])
-    parts = last[:, :, width:].astype(F32)
-    parts = (parts[:, :, :128] + parts[:, :, 128:]).reshape(n_zl, n_y, -1, 128)
-    gain_grad = jnp.sum(parts, axis=0).reshape(-1)
+    weight_grad, gain_grad = last_sums(last, width)
 
     result = jnp.zeros((tokens, width), BF16)
     for shift in (0, 1, n_zh - 1, 2):
@@ -175,7 +213,7 @@
         source = lax.rem(zh + n_zh - shift, n_zh) * own
         result = lax.dynamic_update_slice_in_dim(result, piece, own_start + source, 0)
         result = lax.dynamic_update_slice_in_dim(result, other, other_start + source, 0)
-    return weight_grad, gain_grad, result
+    return weight_grad, gain_grad.reshape(-1), result
 
 
 def solution(mesh):

time: 170 us -> 192 us (1.13)
  the two profiles are of different devices: /device:TPU:97 before, /device:TPU:120 now
where the time goes in v4:
time: 192 us; the launch traced here: 191 us
  waiting for transfers between devices  78.4 us (41%)
  starting transfers between devices  72.4 us (38%)
  matrix products  14.3 us (7%)
  local copies, waits for them, and re-layouts  10.3 us (5%)
  other arithmetic  7.47 us (4%)
  Pallas kernels  6.79 us (4%)
    ppermute x6, starting transfers between devices, shifted(): lax.ppermute(block, axis, [(i, (i + shift) % peers) for i in range(peers)])  29 us
    ppermute x7, waiting for transfers between devices, swapped(): lax.ppermute(block, axis, [(i, i ^ bit) for i in range(lax.axis_size(axis...  28.4 us
    ppermute x6, waiting for transfers between devices, shifted(): lax.ppermute(block, axis, [(i, (i + shift) % peers) for i in range(peers)])  26.9 us
    all_to_all x3, starting transfers between devices, exchange(): return lax.all_to_all(blocks, axes, 0, 0, tiled=True)  26.6 us
    all_to_all x3, waiting for transfers between devices, exchange(): return lax.all_to_all(blocks, axes, 0, 0, tiled=True)  23.1 us
    ppermute x7, starting transfers between devices, swapped(): lax.ppermute(block, axis, [(i, i ^ bit) for i in range(lax.axis_size(axis...  16.9 us
    dot_general x2, matrix products, term(): return jnp.dot(rows, w_query, preferred_element_type=F32).astype(BF16)  7.16 us
    dot_general x4, matrix products, block(): lax.dot_general(columns, normed, (((0,), (0,)), ((), ())), preferred_elem...  6.85 us
  transfers between devices with their start and end apart: 16, of which 5 were waited for; matrix products, arithmetic and copies ran while one was open for 12% of the time, Pallas kernels for 3%

profile of v4, /device:TPU:120, one launch (start us, length us, event | category | flops | bytes accessed | tf_op | source)
XLA Modules:
  0.0 190.6 jit_solution(17085960178933074475)
XLA Ops:
  0.6 0.0 copy-start
  0.6 2.1 %fusion = f32[256]{0:T(256)S(1)} fusion(bf16[256,4096]{1,0:T(8,128)(2,1)} %resid.1), kind=kLoop, calls=%fused_computation.9 | loop fusion | flops 3145472 | bytes 2098176 | tf_op jit(solution)/shard_map/reduce_sum | solution.py:157
  2.8 3.6 %convolution_convert_fusion.1 = bf16[128,4096]{1,0:T(8,128)(2,1)} fusion(bf16[384,4096]{1,0:T(8,128)(2,1)} %param.8, bf16[256,384]{1,0:T(8,128)(2,1)S(1)} %copy-done, s32[]{:T(128)S(6)} %select_n.67), kind=kOutput, calls=%fused_computation.4 | convolution fusion | flops 403177472 | bytes 4292612 | tf_op jit(solution)/shard_map/dot_general | solution.py:161
  6.4 1.9 %collective-permute-start = (bf16[128,4096]{1,0:T(8,128)(2,1)}, bf16[128,4096]{1,0:T(8,128)(2,1)}, u32[]{:S(2)}, u32[]{:S(2)}) collective-permute-start(bf16[128,4096]{1,0:T(8,128)(2,1)} %convolution_convert_fusion.1), channel_id=1, source_target_pairs={{0,1},{1,0},{2,3},{3,2},{4,5},{5,4},{6,7},{7,6},{8,9},{9,8},{10,11... | collective-permute-start | bytes 3145736 | tf_op jit(solution)/shard_map/ppermute | solution.py:30
  8.3 3.6 %convolution_convert_fusion = bf16[128,4096]{1,0:T(8,128)(2,1)} fusion(bf16[384,4096]{1,0:T(8,128)(2,1)} %param.8, bf16[256,384]{1,0:T(8,128)(2,1)S(1)} %copy-done, s32[]{:T(128)S(6)} %select_n.68), kind=kOutput, calls=%fused_computation.3 | convolution fusion | flops 403177472 | bytes 4292612 | tf_op jit(solution)/shard_map/dot_general | solution.py:161
  11.9 0.3 convolution_convert_fusion.6
  12.2 2.9 %fusion.3 = bf16[128,4096]{1,0:T(8,128)(2,1)} fusion(bf16[128,4096]{1,0:T(8,128)(2,1)} %convolution_convert_fusion, bf16[128,4096]{1,0:T(8,128)(2,1)} %collective-permute-done), kind=kLoop, calls=%fused_computation.14 | loop fusion | flops 2097152 | bytes 3145728 | tf_op jit(solution)/shard_map/convert_element_type | solution.py:171
  15.2 13.6 %all-to-all-start = ((bf16[4,32,4096]{2,1,0:T(8,128)(2,1)}), bf16[4,32,4096]{2,1,0:T(8,128)(2,1)}, u32[]{:S(2)}, u32[]{:S(2)}) async-start(bf16[4,32,4096]{2,1,0:T(8,128)(2,1)} %bitcast.11), calls=%async_computation | async-start | bytes 2097152 | tf_op jit(solution)/shard_map/all_to_all | solution.py:17
  28.8 0.5 convert_multiply_fusion.1
  29.3 0.7 copy-done.3
  30.0 1.8 fusion.4
  31.9 3.4 %collective-permute-start.1 = (f32[32,128]{1,0:T(8,128)S(1)}, f32[32,128]{1,0:T(8,128)S(1)}, u32[]{:S(2)}, u32[]{:S(2)}) collective-permute-start(f32[32,128]{1,0:T(8,128)S(1)} %add_bitcast_fusion), channel_id=1, source_target_pairs={{0,8},{8,0},{16,24},{24,16},{1,9},{9,1},{17,25},{25,17},{2,10},{10... | collective-permute-start | bytes 49160 | tf_op jit(solution)/shard_map/ppermute | solution.py:30
  35.3 2.2 %collective-permute-done.1 = f32[32,128]{1,0:T(8,128)S(1)} collective-permute-done((f32[32,128]{1,0:T(8,128)S(1)}, f32[32,128]{1,0:T(8,128)S(1)}, u32[]{:S(2)}, u32[]{:S(2)}) %collective-permute-start.1) | collective-permute-done | bytes 16416 | tf_op jit(solution)/shard_map/ppermute | solution.py:30
  37.5 1.8 convolution_convert_fusion.2
  39.2 1.7 convolution_convert_fusion.3
  40.9 4.7 %collective-permute-start.5 = (bf16[96,4096]{1,0:T(8,128)(2,1)}, bf16[96,4096]{1,0:T(8,128)(2,1)S(1)}, u32[]{:S(2)}, u32[]{:S(2)}) collective-permute-start(bf16[96,4096]{1,0:T(8,128)(2,1)} %convolution_convert_fusion.2), channel_id=1, source_target_pairs={{0,24},{8,0},{16,8},{24,16},{1,25},{9,1},{17,9},{25,17},{2,26},{10... | collective-permute-start | bytes 2359304 | tf_op jit(solution)/shard_map/ppermute | solution.py:26
  45.6 2.7 %collective-permute-start.4 = (bf16[96,4096]{1,0:T(8,128)(2,1)}, bf16[96,4096]{1,0:T(8,128)(2,1)}, u32[]{:S(2)}, u32[]{:S(2)}) collective-permute-start(bf16[96,4096]{1,0:T(8,128)(2,1)} %convolution_convert_fusion.3), channel_id=1, source_target_pairs={{0,16},{8,24},{16,0},{24,8},{1,17},{9,25},{17,1},{25,9},{2,18},{10... | collective-permute-start | bytes 2359304 | tf_op jit(solution)/shard_map/ppermute | solution.py:26
  48.3 1.7 convolution_convert_fusion.4
  50.0 2.8 %collective-permute-start.3 = (bf16[96,4096]{1,0:T(8,128)(2,1)}, bf16[96,4096]{1,0:T(8,128)(2,1)}, u32[]{:S(2)}, u32[]{:S(2)}) collective-permute-start(bf16[96,4096]{1,0:T(8,128)(2,1)} %convolution_convert_fusion.4), channel_id=1, source_target_pairs={{0,8},{8,16},{16,24},{24,0},{1,9},{9,17},{17,25},{25,1},{2,10},{10... | collective-permute-start | bytes 2359304 | tf_op jit(solution)/shard_map/ppermute | solution.py:26
  52.8 0.6 reshape.94.gain
  53.4 3.8 %collective-permute-start.2 = (f32[32,128]{1,0:T(8,128)S(1)}, f32[32,128]{1,0:T(8,128)S(1)}, u32[]{:S(2)}, u32[]{:S(2)}) collective-permute-start(f32[32,128]{1,0:T(8,128)S(1)} %add.170), channel_id=1, source_target_pairs={{0,16},{8,24},{16,0},{24,8},{1,17},{9,25},{17,1},{25,9},{2,18},{10... | collective-permute-start | bytes 49160 | tf_op jit(solution)/shard_map/ppermute | solution.py:30
  57.2 1.7 convolution_convert_fusion.5.first
  58.9 26.2 %collective-permute-done.2 = f32[32,128]{1,0:T(8,128)S(1)} collective-permute-done((f32[32,128]{1,0:T(8,128)S(1)}, f32[32,128]{1,0:T(8,128)S(1)}, u32[]{:S(2)}, u32[]{:S(2)}) %collective-permute-start.2) | collective-permute-done | bytes 16416 | tf_op jit(solution)/shard_map/ppermute | solution.py:30
  85.1 3.3 %result_rows.1 = bf16[32,4096]{1,0:T(8,128)(2,1)} custom-call(s32[1]{0:T(128)} %bitcast.4.first, bf16[4,32,4096]{2,1,0:T(8,128)(2,1)} %all-to-all-done.summands, bf16[1,4096]{1,0:T(2,128)(2,1)} %reshape.94.gain, bf16[256,4096]{1,0:T(8,128)(2,1)} %resid.1, bf16[256,4096]{1,0:T(8,128)(2,1)} %grad_in.1), custom_call_target="tpu_custom_call" | custom-call | flops 1966080 | bytes 1835008 | tf_op jit(solution)/shard_map/result_rows/pallas_call | solution.py:123
  88.4 2.1 %collective-permute-start.6 = (bf16[32,4096]{1,0:T(8,128)(2,1)}, bf16[32,4096]{1,0:T(8,128)(2,1)S(1)}, u32[]{:S(2)}, u32[]{:S(2)}) collective-permute-start(bf16[32,4096]{1,0:T(8,128)(2,1)} %result_rows.1), channel_id=1, source_target_pairs={{0,1},{1,0},{2,3},{3,2},{4,5},{5,4},{6,7},{7,6},{8,9},{9,8},{10,11... | collective-permute-start | bytes 786440 | tf_op jit(solution)/shard_map/ppermute | solution.py:30
  90.5 6.7 %collective-permute-start.7 = (bf16[32,4096]{1,0:T(8,128)(2,1)}, bf16[32,4096]{1,0:T(8,128)(2,1)S(1)}, u32[]{:S(2)}, u32[]{:S(2)}) collective-permute-start(bf16[32,4096]{1,0:T(8,128)(2,1)} %result_rows.1), channel_id=1, source_target_pairs={{0,2},{2,4},{4,6},{6,0},{1,3},{3,5},{5,7},{7,1},{8,10},{10,12},{12... | collective-permute-start | bytes 786440 | tf_op jit(solution)/shard_map/ppermute | solution.py:26
  97.1 0.7 broadcast_in_dim.4
  97.8 5.1 %all-to-all-start.1 = ((f32[8,32,128]{2,1,0:T(8,128)}), f32[8,32,128]{2,1,0:T(8,128)S(1)}, u32[]{:S(2)}, u32[]{:S(2)}) async-start(f32[8,32,128]{2,1,0:T(8,128)} %broadcast_in_dim.4), calls=%async_computation.1 | async-start | bytes 262144 | tf_op jit(solution)/shard_map/all_to_all | solution.py:17
  102.9 6.9 %collective-permute-start.9 = (bf16[32,4096]{1,0:T(8,128)(2,1)}, bf16[32,4096]{1,0:T(8,128)(2,1)S(1)}, u32[]{:S(2)}, u32[]{:S(2)}) collective-permute-start(bf16[32,4096]{1,0:T(8,128)(2,1)} %result_rows.1), channel_id=1, source_target_pairs={{0,6},{2,0},{4,2},{6,4},{1,7},{3,1},{5,3},{7,5},{8,14},{10,8},{12,... | collective-permute-start | bytes 786440 | tf_op jit(solution)/shard_map/ppermute | solution.py:26
  109.9 5.2 %collective-permute-start.11 = (bf16[32,4096]{1,0:T(8,128)(2,1)}, bf16[32,4096]{1,0:T(8,128)(2,1)S(1)}, u32[]{:S(2)}, u32[]{:S(2)}) collective-permute-start(bf16[32,4096]{1,0:T(8,128)(2,1)} %result_rows.1), channel_id=1, source_target_pairs={{0,4},{2,6},{4,0},{6,2},{1,5},{3,7},{5,1},{7,3},{8,12},{10,14},{12... | collective-permute-start | bytes 786440 | tf_op jit(solution)/shard_map/ppermute | solution.py:26
  115.1 1.6 broadcast_in_dim.5
  116.7 0.7 constant_dynamic-update-slice_fusion.7
  117.4 1.9 %collective-permute-start.8 = (bf16[32,4096]{1,0:T(8,128)(2,1)S(1)}, bf16[32,4096]{1,0:T(8,128)(2,1)}, u32[]{:S(2)}, u32[]{:S(2)}) collective-permute-start(bf16[32,4096]{1,0:T(8,128)(2,1)S(1)} %collective-permute-done.7), channel_id=1, source_target_pairs={{0,1},{1,0},{2,3},{3,2},{4,5},{5,4},{6,7},{7,6},{8,9},{9,8},{10,11... | collective-permute-start | bytes 786440 | tf_op jit(solution)/shard_map/ppermute | solution.py:30
  119.4 9.7 %collective-permute-done.9 = bf16[32,4096]{1,0:T(8,128)(2,1)S(1)} collective-permute-done((bf16[32,4096]{1,0:T(8,128)(2,1)}, bf16[32,4096]{1,0:T(8,128)(2,1)S(1)}, u32[]{:S(2)}, u32[]{:S(2)}) %collective-permute-start.9) | collective-permute-done | bytes 262176 | tf_op jit(solution)/shard_map/ppermute | solution.py:26
  129.1 1.9 %collective-permute-start.10 = (bf16[32,4096]{1,0:T(8,128)(2,1)S(1)}, bf16[32,4096]{1,0:T(8,128)(2,1)S(1)}, u32[]{:S(2)}, u32[]{:S(2)}) collective-permute-start(bf16[32,4096]{1,0:T(8,128)(2,1)S(1)} %collective-permute-done.9), channel_id=1, source_target_pairs={{0,1},{1,0},{2,3},{3,2},{4,5},{5,4},{6,7},{7,6},{8,9},{9,8},{10,11... | collective-permute-start | bytes 786440 | tf_op jit(solution)/shard_map/ppermute | solution.py:30
  131.0 17.2 %collective-permute-done.11 = bf16[32,4096]{1,0:T(8,128)(2,1)S(1)} collective-permute-done((bf16[32,4096]{1,0:T(8,128)(2,1)}, bf16[32,4096]{1,0:T(8,128)(2,1)S(1)}, u32[]{:S(2)}, u32[]{:S(2)}) %collective-permute-start.11) | collective-permute-done | bytes 262176 | tf_op jit(solution)/shard_map/ppermute | solution.py:26
  148.1 1.9 %collective-permute-start.12 = (bf16[32,4096]{1,0:T(8,128)(2,1)S(1)}, bf16[32,4096]{1,0:T(8,128)(2,1)S(1)}, u32[]{:S(2)}, u32[]{:S(2)}) collective-permute-start(bf16[32,4096]{1,0:T(8,128)(2,1)S(1)} %collective-permute-done.11), channel_id=1, source_target_pairs={{0,1},{1,0},{2,3},{3,2},{4,5},{5,4},{6,7},{7,6},{8,9},{9,8},{10,11... | collective-permute-start | bytes 786440 | tf_op jit(solution)/shard_map/ppermute | solution.py:30
  150.1 2.8 %pack.1 = bf16[24,4,5120]{2,1,0:T(4,128)(2,1)} custom-call(bf16[96,4096]{1,0:T(8,128)(2,1)S(1)} %copy-done.1, bf16[96,4096]{1,0:T(8,128)(2,1)} %collective-permute-done.3.second, bf16[96,4096]{1,0:T(8,128)(2,1)} %collective-permute-done.4.third, bf16[96,4096]{1,0:T(8,128)(2,1)S(1)} %collective-permute-done.5.fourth, ...), custom_call_target="tpu_custom_call" | custom-call | flops 1179648 | bytes 3932160 | tf_op jit(solution)/shard_map/pack/pallas_call | solution.py:60
  152.8 7.8 %all-to-all-start.2 = ((bf16[24,4,5120]{2,1,0:T(4,128)(2,1)}), bf16[24,4,5120]{2,1,0:T(4,128)(2,1)S(1)}, u32[]{:S(2)}, u32[]{:S(2)}) async-start(bf16[24,4,5120]{2,1,0:T(4,128)(2,1)} %pack.1), calls=%async_computation.2 | async-start | bytes 1966080 | tf_op jit(solution)/shard_map/all_to_all | solution.py:17
  160.7 0.7 constant_dynamic-update-slice_fusion.6
  161.4 0.7 constant_dynamic-update-slice_fusion.5
  162.1 1.7 constant_dynamic-update-slice_fusion.4
  163.8 0.7 constant_dynamic-update-slice_fusion.3
  164.5 0.7 constant_dynamic-update-slice_fusion.2
  165.2 0.7 constant_dynamic-update-slice_fusion.1
  166.0 0.7 constant_dynamic-update-slice_fusion
  166.7 23.1 %all-to-all-done.2.last = bf16[24,4,5120]{2,1,0:T(4,128)(2,1)S(1)} async-done(((bf16[24,4,5120]{2,1,0:T(4,128)(2,1)}), bf16[24,4,5120]{2,1,0:T(4,128)(2,1)S(1)}, u32[]{:S(2)}, u32[]{:S(2)}) %all-to-all-start.2) | async-done | bytes 983072 | tf_op jit(solution)/shard_map/all_to_all | solution.py:17
  189.8 0.8 last_sums.1
  (29 shorter events, 0.1 us)
Async XLA Ops:
  0.6 2.2 %copy-start = (bf16[256,384]{1,0:T(8,128)(2,1)S(1)}, bf16[256,384]{1,0:T(8,128)(2,1)}, u32[]{:S(2)}) copy-start(bf16[256,384]{1,0:T(8,128)(2,1)} %param.7) | copy-start | bytes 589828
  6.4 5.9 %collective-permute-start = (bf16[128,4096]{1,0:T(8,128)(2,1)}, bf16[128,4096]{1,0:T(8,128)(2,1)}, u32[]{:S(2)}, u32[]{:S(2)}) collective-permute-start(bf16[128,4096]{1,0:T(8,128)(2,1)} %convolution_convert_fusion.1), channel_id=1, source_target_pairs={{0,1},{1,0},{2,3},{3,2},{4,5},{5,4},{6,7},{7,6},{8,9},{9,8},{10,11... | collective-permute-start | bytes 3145736 | tf_op jit(solution)/shard_map/ppermute | solution.py:30
  12.2 16.6 %copy-start.2 = (bf16[256,4096]{1,0:T(8,128)(2,1)S(1)}, bf16[256,4096]{1,0:T(8,128)(2,1)}, u32[]{:S(2)}) copy-start(bf16[256,4096]{1,0:T(8,128)(2,1)} %resid.1) | copy-start | bytes 6291460
  15.2 69.9 %all-to-all-start = ((bf16[4,32,4096]{2,1,0:T(8,128)(2,1)}), bf16[4,32,4096]{2,1,0:T(8,128)(2,1)}, u32[]{:S(2)}, u32[]{:S(2)}) async-start(bf16[4,32,4096]{2,1,0:T(8,128)(2,1)} %bitcast.11), calls=%async_computation | async-start | bytes 2097152 | tf_op jit(solution)/shard_map/all_to_all | solution.py:17
  28.8 1.2 copy-start.3
  30.0 5.3 %copy-start.5 = (bf16[4096]{0:T(1024)(128)(2,1)S(1)}, bf16[4096]{0:T(1024)(128)(2,1)}, u32[]{:S(2)}) copy-start(bf16[4096]{0:T(1024)(128)(2,1)} %param.6) | copy-start | bytes 24580
  31.9 5.6 %collective-permute-start.1 = (f32[32,128]{1,0:T(8,128)S(1)}, f32[32,128]{1,0:T(8,128)S(1)}, u32[]{:S(2)}, u32[]{:S(2)}) collective-permute-start(f32[32,128]{1,0:T(8,128)S(1)} %add_bitcast_fusion), channel_id=1, source_target_pairs={{0,8},{8,0},{16,24},{24,16},{1,9},{9,1},{17,25},{25,17},{2,10},{10... | collective-permute-start | bytes 49160 | tf_op jit(solution)/shard_map/ppermute | solution.py:30
  40.9 62.0 %collective-permute-start.5 = (bf16[96,4096]{1,0:T(8,128)(2,1)}, bf16[96,4096]{1,0:T(8,128)(2,1)S(1)}, u32[]{:S(2)}, u32[]{:S(2)}) collective-permute-start(bf16[96,4096]{1,0:T(8,128)(2,1)} %convolution_convert_fusion.2), channel_id=1, source_target_pairs={{0,24},{8,0},{16,8},{24,16},{1,25},{9,1},{17,9},{25,17},{2,26},{10... | collective-permute-start | bytes 2359304 | tf_op jit(solution)/shard_map/ppermute | solution.py:26
  45.6 64.3 %collective-permute-start.4 = (bf16[96,4096]{1,0:T(8,128)(2,1)}, bf16[96,4096]{1,0:T(8,128)(2,1)}, u32[]{:S(2)}, u32[]{:S(2)}) collective-permute-start(bf16[96,4096]{1,0:T(8,128)(2,1)} %convolution_convert_fusion.3), channel_id=1, source_target_pairs={{0,16},{8,24},{16,0},{24,8},{1,17},{9,25},{17,1},{25,9},{2,18},{10... | collective-permute-start | bytes 2359304 | tf_op jit(solution)/shard_map/ppermute | solution.py:26
  50.0 100.1 %collective-permute-start.3 = (bf16[96,4096]{1,0:T(8,128)(2,1)}, bf16[96,4096]{1,0:T(8,128)(2,1)}, u32[]{:S(2)}, u32[]{:S(2)}) collective-permute-start(bf16[96,4096]{1,0:T(8,128)(2,1)} %convolution_convert_fusion.4), channel_id=1, source_target_pairs={{0,8},{8,16},{16,24},{24,0},{1,9},{9,17},{17,25},{25,1},{2,10},{10... | collective-permute-start | bytes 2359304 | tf_op jit(solution)/shard_map/ppermute | solution.py:26
  53.4 31.7 %collective-permute-start.2 = (f32[32,128]{1,0:T(8,128)S(1)}, f32[32,128]{1,0:T(8,128)S(1)}, u32[]{:S(2)}, u32[]{:S(2)}) collective-permute-start(f32[32,128]{1,0:T(8,128)S(1)} %add.170), channel_id=1, source_target_pairs={{0,16},{8,24},{16,0},{24,8},{1,17},{9,25},{17,1},{25,9},{2,18},{10... | collective-permute-start | bytes 49160 | tf_op jit(solution)/shard_map/ppermute | solution.py:30
  88.4 28.3 %copy-start.4 = (bf16[32,4096]{1,0:T(8,128)(2,1)S(1)}, bf16[32,4096]{1,0:T(8,128)(2,1)}, u32[]{:S(2)}) copy-start(bf16[32,4096]{1,0:T(8,128)(2,1)} %result_rows.1) | copy-start | bytes 786436
  88.4 61.7 %copy-start.1 = (bf16[96,4096]{1,0:T(8,128)(2,1)S(1)}, bf16[96,4096]{1,0:T(8,128)(2,1)}, u32[]{:S(2)}) copy-start(bf16[96,4096]{1,0:T(8,128)(2,1)} %convolution_convert_fusion.5.first) | copy-start | bytes 2359300
  88.4 72.3 %collective-permute-start.6 = (bf16[32,4096]{1,0:T(8,128)(2,1)}, bf16[32,4096]{1,0:T(8,128)(2,1)S(1)}, u32[]{:S(2)}, u32[]{:S(2)}) collective-permute-start(bf16[32,4096]{1,0:T(8,128)(2,1)} %result_rows.1), channel_id=1, source_target_pairs={{0,1},{1,0},{2,3},{3,2},{4,5},{5,4},{6,7},{7,6},{8,9},{9,8},{10,11... | collective-permute-start | bytes 786440 | tf_op jit(solution)/shard_map/ppermute | solution.py:30
  90.5 27.0 %collective-permute-start.7 = (bf16[32,4096]{1,0:T(8,128)(2,1)}, bf16[32,4096]{1,0:T(8,128)(2,1)S(1)}, u32[]{:S(2)}, u32[]{:S(2)}) collective-permute-start(bf16[32,4096]{1,0:T(8,128)(2,1)} %result_rows.1), channel_id=1, source_target_pairs={{0,2},{2,4},{4,6},{6,0},{1,3},{3,5},{5,7},{7,1},{8,10},{10,12},{12... | collective-permute-start | bytes 786440 | tf_op jit(solution)/shard_map/ppermute | solution.py:26
  97.8 19.6 %all-to-all-start.1 = ((f32[8,32,128]{2,1,0:T(8,128)}), f32[8,32,128]{2,1,0:T(8,128)S(1)}, u32[]{:S(2)}, u32[]{:S(2)}) async-start(f32[8,32,128]{2,1,0:T(8,128)} %broadcast_in_dim.4), calls=%async_computation.1 | async-start | bytes 262144 | tf_op jit(solution)/shard_map/all_to_all | solution.py:17
  102.9 26.1 %collective-permute-start.9 = (bf16[32,4096]{1,0:T(8,128)(2,1)}, bf16[32,4096]{1,0:T(8,128)(2,1)S(1)}, u32[]{:S(2)}, u32[]{:S(2)}) collective-permute-start(bf16[32,4096]{1,0:T(8,128)(2,1)} %result_rows.1), channel_id=1, source_target_pairs={{0,6},{2,0},{4,2},{6,4},{1,7},{3,1},{5,3},{7,5},{8,14},{10,8},{12,... | collective-permute-start | bytes 786440 | tf_op jit(solution)/shard_map/ppermute | solution.py:26
  109.9 38.3 %collective-permute-start.11 = (bf16[32,4096]{1,0:T(8,128)(2,1)}, bf16[32,4096]{1,0:T(8,128)(2,1)S(1)}, u32[]{:S(2)}, u32[]{:S(2)}) collective-permute-start(bf16[32,4096]{1,0:T(8,128)(2,1)} %result_rows.1), channel_id=1, source_target_pairs={{0,4},{2,6},{4,0},{6,2},{1,5},{3,7},{5,1},{7,3},{8,12},{10,14},{12... | collective-permute-start | bytes 786440 | tf_op jit(solution)/shard_map/ppermute | solution.py:26
  117.4 44.7 %collective-permute-start.8 = (bf16[32,4096]{1,0:T(8,128)(2,1)S(1)}, bf16[32,4096]{1,0:T(8,128)(2,1)}, u32[]{:S(2)}, u32[]{:S(2)}) collective-permute-start(bf16[32,4096]{1,0:T(8,128)(2,1)S(1)} %collective-permute-done.7), channel_id=1, source_target_pairs={{0,1},{1,0},{2,3},{3,2},{4,5},{5,4},{6,7},{7,6},{8,9},{9,8},{10,11... | collective-permute-start | bytes 786440 | tf_op jit(solution)/shard_map/ppermute | solution.py:30
  129.1 35.5 %collective-permute-start.10 = (bf16[32,4096]{1,0:T(8,128)(2,1)S(1)}, bf16[32,4096]{1,0:T(8,128)(2,1)S(1)}, u32[]{:S(2)}, u32[]{:S(2)}) collective-permute-start(bf16[32,4096]{1,0:T(8,128)(2,1)S(1)} %collective-permute-done.9), channel_id=1, source_target_pairs={{0,1},{1,0},{2,3},{3,2},{4,5},{5,4},{6,7},{7,6},{8,9},{9,8},{10,11... | collective-permute-start | bytes 786440 | tf_op jit(solution)/shard_map/ppermute | solution.py:30
  148.1 17.8 %collective-permute-start.12 = (bf16[32,4096]{1,0:T(8,128)(2,1)S(1)}, bf16[32,4096]{1,0:T(8,128)(2,1)S(1)}, u32[]{:S(2)}, u32[]{:S(2)}) collective-permute-start(bf16[32,4096]{1,0:T(8,128)(2,1)S(1)} %collective-permute-done.11), channel_id=1, source_target_pairs={{0,1},{1,0},{2,3},{3,2},{4,5},{5,4},{6,7},{7,6},{8,9},{9,8},{10,11... | collective-permute-start | bytes 786440 | tf_op jit(solution)/shard_map/ppermute | solution.py:30
  152.8 37.0 %all-to-all-start.2 = ((bf16[24,4,5120]{2,1,0:T(4,128)(2,1)}), bf16[24,4,5120]{2,1,0:T(4,128)(2,1)S(1)}, u32[]{:S(2)}, u32[]{:S(2)}) async-start(bf16[24,4,5120]{2,1,0:T(4,128)(2,1)} %pack.1), calls=%async_computation.2 | async-start | bytes 1966080 | tf_op jit(solution)/shard_map/all_to_all | solution.py:17

commit v5 on v4

--- a/solution.py
+++ b/solution.py
@@ -99,45 +99,29 @@
     )(last)
 
 
-def rows_kernel(first, summands, gain, resid, grad_in, rows, held, sems):
-    place = pl.ds(pl.multiple_of(first[0], 32), rows.shape[0])
-    copies = [
-        pltpu.make_async_copy(array.at[place, :], held.at[i], sems.at[i])
-        for i, array in enumerate((resid, grad_in))
-    ]
-    for copy in copies:
-        copy.start()
+def rows_kernel(summands, gain, slices, rows):
     summed = [summands[i].astype(F32) for i in range(summands.shape[0])]
     dunit = ((summed[0] + summed[1]) + (summed[2] + summed[3])) * gain[...].astype(F32)
-    copies[0].wait()
-    resid_f = held[0].astype(F32)
+    resid_f = slices[0].astype(F32)
     inv = lax.rsqrt(jnp.mean(resid_f * resid_f, axis=-1, keepdims=True) + 1e-05)
     unit = resid_f * inv
     inner = jnp.mean(dunit * unit, axis=-1, keepdims=True)
-    copies[1].wait()
-    rows[...] = (held[1].astype(F32) + inv * (dunit - unit * inner)).astype(BF16)
-
-
-def result_rows(first, summands, gain, resid, grad_in):
-    _, rows, width = summands.shape
+    rows[...] = (slices[1].astype(F32) + inv * (dunit - unit * inner)).astype(BF16)
+
+
+def result_rows(summands, gain, slices):
+    _, rows, width = slices.shape
     return pl.pallas_call(
         rows_kernel,
         out_shape=jax.ShapeDtypeStruct((rows, width), BF16),
-        in_specs=[
-            pl.BlockSpec(memory_space=pltpu.SMEM),
-            pl.BlockSpec(memory_space=pltpu.VMEM),
-            pl.BlockSpec(memory_space=pltpu.VMEM),
-            pl.BlockSpec(memory_space=pltpu.HBM),
-            pl.BlockSpec(memory_space=pltpu.HBM),
-        ],
+        in_specs=[pl.BlockSpec(memory_space=pltpu.VMEM)] * 3,
         out_specs=pl.BlockSpec(memory_space=pltpu.VMEM),
-        scratch_shapes=[pltpu.VMEM((2, rows, width), BF16), pltpu.SemaphoreType.DMA((2,))],
-        compiler_params=pltpu.CompilerParams(vmem_limit_bytes=125 * 2**19),
+        compiler_params=pltpu.CompilerParams(vmem_limit_bytes=10 * 2**20),
         cost_estimate=pl.CostEstimate(
             flops=15 * rows * width, bytes_accessed=14 * rows * width, transcendentals=0
         ),
         name="result_rows",
-    )(first, summands, gain, resid, grad_in)
+    )(summands, gain, slices)
 
 
 def body(resid, gain, grad_q, w_query, grad_in):
@@ -161,21 +145,22 @@
         return jnp.dot(rows, w_query, preferred_element_type=F32).astype(BF16)
 
     inv, grad_q = lax.optimization_barrier((inverse(resid), grad_q))
-    ordered = jnp.dot(grad_q, owner_columns(cols, lax.axis_index("x")), preferred_element_type=F32)
-    ordered = ordered.astype(BF16)
 
     other_start, own_start = (1 - core) * half, core * half
     sent = term(other_start)
     got = swapped(sent, "c", 1)
     kept = lax.optimization_barrier(term(own_start))
     pair = (kept.astype(F32) + got.astype(F32)).astype(BF16)
-    pair, inv, ordered = lax.optimization_barrier((pair, inv, ordered))
+    held = (pair, inv, grad_q, resid, grad_in)
+    pair, inv, grad_q, resid_x, grad_in = lax.optimization_barrier(held)
     summands = exchange(pair.reshape(n_zh, own, width), "zh")
 
     unit = resid.astype(F32) * inv
     part = jnp.sum(sent.astype(F32) * rows_of(unit, other_start, half), axis=0)
     part = part + jnp.sum(kept.astype(F32) * rows_of(unit, own_start, half), axis=0)
     part, inv_x = lax.optimization_barrier((part.reshape(-1, 128), inv))
+    ordered = jnp.dot(grad_q, owner_columns(cols, lax.axis_index("x")), preferred_element_type=F32)
+    ordered = lax.optimization_barrier(ordered.astype(BF16))
     part = part + swapped(part, "x", 1)
     part, inv_x = lax.optimization_barrier((part, inv_x))
     part_x = swapped(part, "x", 2)
@@ -192,25 +177,31 @@
 
     blocks = [block(s) for s in range(n_x)]
     blocks = [b if s == 0 else shifted(b, "x", s) for s, b in enumerate(blocks)]
-    first = (own_start + zh * own).astype(jnp.int32).reshape(1)
-    ready = (part + part_x, blocks[0], first, gain.reshape(1, width))
-    part, own_block, first, gain_row = lax.optimization_barrier(ready)
+    first = own_start + zh * own
+    slices = jnp.stack([rows_of(resid_x, first, own), rows_of(grad_in, first, own)])
+    ready = (part + part_x, blocks[0], gain.reshape(1, width), slices)
+    part, own_block, gain_row, slices = lax.optimization_barrier(ready)
 
     part, summands = lax.optimization_barrier((part, summands))
     part = jnp.broadcast_to(part[None], (lax.axis_size(TP), *part.shape))
     part = total(exchange(part, TP))
-    rows = result_rows(first, summands, gain_row, resid, grad_in)
+    rows = result_rows(summands, gain_row, slices)
 
     mine = share // (n_y * n_zl)
     packed = pack([own_block, *blocks[1:]], part.astype(BF16).reshape(mine, -1))
     last = exchange(packed, ("zl", "y"))
     weight_grad, gain_grad = last_sums(last, width)
 
+    before, after = shifted(rows, "zh", 1), shifted(rows, "zh", n_zh - 1)
+    upper, lower = before[: own // 2], after[own // 2 :]
+    upper, lower = shifted(upper, "zh", 1), shifted(lower, "zh", n_zh - 1)
+    pieces = (
+        (0, 0, rows), (1, 0, before), (n_zh - 1, 0, after), (2, 0, upper), (2, own // 2, lower)
+    )
     result = jnp.zeros((tokens, width), BF16)
-    for shift in (0, 1, n_zh - 1, 2):
-        piece = rows if shift == 0 else shifted(rows, "zh", shift)
+    for shift, offset, piece in pieces:
         other = swapped(piece, "c", 1)
-        source = lax.rem(zh + n_zh - shift, n_zh) * own
+        source = lax.rem(zh + n_zh - shift, n_zh) * own + offset
         result = lax.dynamic_update_slice_in_dim(result, piece, own_start + source, 0)
         result = lax.dynamic_update_slice_in_dim(result, other, other_start + source, 0)
     return weight_grad, gain_grad.reshape(-1), result

time: 192 us -> 171 us (0.89)
  waiting for transfers between devices: 78.4 us -> 40.6 us
  local copies, waits for them, and re-layouts: 10.3 us -> 23.1 us
  starting transfers between devices: 72.4 us -> 80 us
  matrix products: 14.3 us -> 10.6 us
    ppermute x7 -> x8, waiting for transfers between devices: 28.4 us -> 1.16 us  [swapped(): lax.ppermute(block, axis, [(i, i ^ bit) for i in range(lax.axis_size(axis...]
    ppermute x6 -> x7, waiting for transfers between devices: 26.9 us -> 6.14 us  [shifted(): lax.ppermute(block, axis, [(i, (i + shift) % peers) for i in range(peers)])]
    all_to_all x3, waiting for transfers between devices: 23.1 us -> 33.3 us  [exchange(): return lax.all_to_all(blocks, axes, 0, 0, tiled=True)]
    dynamic_update_slice x4 -> x5, local copies, waits for them, and re-layouts: 2.88 us -> 7.2 us  [body(): lax.dynamic_update_slice_in_dim(result, piece, own_start + source, 0)]
    ppermute x7 -> x8, starting transfers between devices: 16.9 us -> 20.9 us  [swapped(): lax.ppermute(block, axis, [(i, i ^ bit) for i in range(lax.axis_size(axis...]
    all_to_all x3, starting transfers between devices: 26.6 us -> 30.5 us  [exchange(): return lax.all_to_all(blocks, axes, 0, 0, tiled=True)]
    dot_general x2, matrix products: 7.16 us -> 3.4 us  [term(): return jnp.dot(rows, w_query, preferred_element_type=F32).astype(BF16)]
    unnamed x12 -> x18, local copies, waits for them, and re-layouts: 0.72 us -> 4.07 us
  transfers between devices with their start and end apart: 16 -> 18, of which waited for: 5 -> 5; matrix products, arithmetic and copies ran while one was open for 12% -> 17% of each run, Pallas kernels for 3% -> 2%
where the time goes in v5:
time: 171 us; the launch traced here: 169 us
  starting transfers between devices  80 us (47%)
  waiting for transfers between devices  40.6 us (24%)
  local copies, waits for them, and re-layouts  23.1 us (14%)
  matrix products  10.6 us (6%)
  other arithmetic  8.28 us (5%)
  Pallas kernels  5.7 us (3%)
    all_to_all x3, waiting for transfers between devices, exchange(): return lax.all_to_all(blocks, axes, 0, 0, tiled=True)  33.3 us
    all_to_all x3, starting transfers between devices, exchange(): return lax.all_to_all(blocks, axes, 0, 0, tiled=True)  30.5 us
    ppermute x7, starting transfers between devices, shifted(): lax.ppermute(block, axis, [(i, (i + shift) % peers) for i in range(peers)])  28.7 us
    ppermute x8, starting transfers between devices, swapped(): lax.ppermute(block, axis, [(i, i ^ bit) for i in range(lax.axis_size(axis...  20.9 us
    dynamic_update_slice x5, local copies, waits for them, and re-layouts, body(): lax.dynamic_update_slice_in_dim(result, piece, own_start + source, 0)  7.2 us
    dot_general x4, matrix products, block(): lax.dot_general(columns, normed, (((0,), (0,)), ((), ())), preferred_elem...  6.88 us
    ppermute x7, waiting for transfers between devices, shifted(): lax.ppermute(block, axis, [(i, (i + shift) % peers) for i in range(peers)])  6.14 us
    dynamic_update_slice x5, local copies, waits for them, and re-layouts, body(): lax.dynamic_update_slice_in_dim(result, other, other_start + source, 0)  5.4 us
  transfers between devices with their start and end apart: 18, of which 5 were waited for; matrix products, arithmetic and copies ran while one was open for 17% of the time, Pallas kernels for 2%

profile of v5, /device:TPU:120, one launch (start us, length us, event | category | flops | bytes accessed | tf_op | source)
XLA Modules:
  0.0 169.3 jit_solution(1203194888527274655)
XLA Ops:
  0.7 2.2 %fusion = f32[256]{0:T(256)S(1)} fusion(bf16[256,4096]{1,0:T(8,128)(2,1)} %param.5), kind=kLoop, calls=%fused_computation.9 | loop fusion | flops 3145472 | bytes 2098176 | tf_op jit(solution)/shard_map/reduce_sum | solution.py:141
  3.2 1.7 %convolution_convert_fusion.1 = bf16[128,4096]{1,0:T(8,128)(2,1)} fusion(bf16[384,4096]{1,0:T(8,128)(2,1)S(1)} %copy-done, bf16[256,384]{1,0:T(8,128)(2,1)S(1)} %copy-done.7, s32[]{:T(128)S(6)} %select_n.77), kind=kOutput, calls=%fused_computation.4 | convolution fusion | flops 403177472 | bytes 4292612 | tf_op jit(solution)/shard_map/dot_general | solution.py:145
  4.9 1.9 %collective-permute-start = (bf16[128,4096]{1,0:T(8,128)(2,1)}, bf16[128,4096]{1,0:T(8,128)(2,1)}, u32[]{:S(2)}, u32[]{:S(2)}) collective-permute-start(bf16[128,4096]{1,0:T(8,128)(2,1)} %convolution_convert_fusion.1), channel_id=1, source_target_pairs={{0,1},{1,0},{2,3},{3,2},{4,5},{5,4},{6,7},{7,6},{8,9},{9,8},{10,11... | collective-permute-start | bytes 3145736 | tf_op jit(solution)/shard_map/ppermute | solution.py:30
  6.9 1.7 %convolution_convert_fusion = bf16[128,4096]{1,0:T(8,128)(2,1)} fusion(bf16[384,4096]{1,0:T(8,128)(2,1)S(1)} %copy-done, bf16[256,384]{1,0:T(8,128)(2,1)S(1)} %copy-done.7, s32[]{:T(128)S(6)} %select_n.78), kind=kOutput, calls=%fused_computation.3 | convolution fusion | flops 403177472 | bytes 4292612 | tf_op jit(solution)/shard_map/dot_general | solution.py:145
  8.6 1.1 collective-permute-done
  9.8 2.8 %fusion.3 = bf16[128,4096]{1,0:T(8,128)(2,1)} fusion(bf16[128,4096]{1,0:T(8,128)(2,1)} %convolution_convert_fusion, bf16[128,4096]{1,0:T(8,128)(2,1)} %collective-permute-done), kind=kLoop, calls=%fused_computation.14 | loop fusion | flops 2097152 | bytes 3145728 | tf_op jit(solution)/shard_map/convert_element_type | solution.py:153
  13.8 1.8 %fusion.4 = (f32[4096]{0:T(1024)S(1)}, f32[4096]{0:T(1024)S(1)}) fusion(bf16[128,4096]{1,0:T(8,128)(2,1)S(1)} %copy-done.6, f32[256,4096]{1,0:T(8,128)S(1)} %convert_multiply_fusion.1, s32[]{:T(128)S(6)} %select_n.78, s32[]{:T(128)S(6)} %select_n.77, bf16[128,4096]{1,0:T(8,128)(2,1)} %convolution_convert_fusion.1), kind=kLoop, calls=%fused_computation.15 | loop fusion | flops 3137536 | bytes 6324232 | tf_op jit(solution)/shard_map/reduce_sum | solution.py:160
  15.6 13.6 %all-to-all-start = ((bf16[4,32,4096]{2,1,0:T(8,128)(2,1)}), bf16[4,32,4096]{2,1,0:T(8,128)(2,1)}, u32[]{:S(2)}, u32[]{:S(2)}) async-start(bf16[4,32,4096]{2,1,0:T(8,128)(2,1)} %bitcast.14), calls=%async_computation | async-start | bytes 2097152 | tf_op jit(solution)/shard_map/all_to_all | solution.py:17
  29.2 3.5 %collective-permute-start.1 = (f32[32,128]{1,0:T(8,128)S(1)}, f32[32,128]{1,0:T(8,128)S(1)}, u32[]{:S(2)}, u32[]{:S(2)}) collective-permute-start(f32[32,128]{1,0:T(8,128)S(1)} %add_bitcast_fusion), channel_id=1, source_target_pairs={{0,8},{8,0},{16,24},{24,16},{1,9},{9,1},{17,25},{25,17},{2,10},{10... | collective-permute-start | bytes 49160 | tf_op jit(solution)/shard_map/ppermute | solution.py:30
  32.7 1.1 dynamic-slice_bitcast_fusion
  35.0 4.9 %collective-permute-start.2 = (f32[32,128]{1,0:T(8,128)S(1)}, f32[32,128]{1,0:T(8,128)S(1)}, u32[]{:S(2)}, u32[]{:S(2)}) collective-permute-start(f32[32,128]{1,0:T(8,128)S(1)} %add.184), channel_id=1, source_target_pairs={{0,16},{8,24},{16,0},{24,8},{1,17},{9,25},{17,1},{25,9},{2,18},{10... | collective-permute-start | bytes 49160 | tf_op jit(solution)/shard_map/ppermute | solution.py:30
  39.9 1.7 %convolution_convert_fusion.5.first = bf16[96,4096]{1,0:T(8,128)(2,1)} fusion(bf16[256,384]{1,0:T(8,128)(2,1)S(1)} %convolution_convert_fusion.6, bf16[256,4096]{1,0:T(8,128)(2,1)S(1)} %copy-done.5, f32[4096]{0:T(1024)S(1)} %convert_element_type.61, f32[256]{0:T(256)S(1)} %add_rsqrt_fusion), kind=kOutput, calls=%fused_computation.8 | convolution fusion | flops 205914112 | bytes 2966528 | tf_op jit(solution)/shard_map/dot_general | solution.py:173
  41.6 1.7 %convolution_convert_fusion.4 = bf16[96,4096]{1,0:T(8,128)(2,1)} fusion(bf16[256,384]{1,0:T(8,128)(2,1)S(1)} %convolution_convert_fusion.6, bf16[256,4096]{1,0:T(8,128)(2,1)S(1)} %copy-done.5, f32[4096]{0:T(1024)S(1)} %convert_element_type.61, f32[256]{0:T(256)S(1)} %add_rsqrt_fusion), kind=kOutput, calls=%fused_computation.7 | convolution fusion | flops 205914112 | bytes 2966528 | tf_op jit(solution)/shard_map/dot_general | solution.py:173
  43.3 1.7 %convolution_convert_fusion.3 = bf16[96,4096]{1,0:T(8,128)(2,1)} fusion(bf16[256,384]{1,0:T(8,128)(2,1)S(1)} %convolution_convert_fusion.6, bf16[256,4096]{1,0:T(8,128)(2,1)S(1)} %copy-done.5, f32[4096]{0:T(1024)S(1)} %convert_element_type.61, f32[256]{0:T(256)S(1)} %add_rsqrt_fusion), kind=kOutput, calls=%fused_computation.6 | convolution fusion | flops 205914112 | bytes 2966528 | tf_op jit(solution)/shard_map/dot_general | solution.py:173
  45.1 1.7 %convolution_convert_fusion.2 = bf16[96,4096]{1,0:T(8,128)(2,1)} fusion(bf16[256,384]{1,0:T(8,128)(2,1)S(1)} %convolution_convert_fusion.6, bf16[256,4096]{1,0:T(8,128)(2,1)S(1)} %copy-done.5, f32[4096]{0:T(1024)S(1)} %convert_element_type.61, f32[256]{0:T(256)S(1)} %add_rsqrt_fusion), kind=kOutput, calls=%fused_computation.5 | convolution fusion | flops 205914112 | bytes 2966528 | tf_op jit(solution)/shard_map/dot_general | solution.py:173
  46.8 2.5 %collective-permute-start.3 = (bf16[96,4096]{1,0:T(8,128)(2,1)}, bf16[96,4096]{1,0:T(8,128)(2,1)}, u32[]{:S(2)}, u32[]{:S(2)}) collective-permute-start(bf16[96,4096]{1,0:T(8,128)(2,1)} %convolution_convert_fusion.4), channel_id=1, source_target_pairs={{0,8},{8,16},{16,24},{24,0},{1,9},{9,17},{17,25},{25,1},{2,10},{10... | collective-permute-start | bytes 2359304 | tf_op jit(solution)/shard_map/ppermute | solution.py:26
  49.3 3.9 %collective-permute-start.4 = (bf16[96,4096]{1,0:T(8,128)(2,1)}, bf16[96,4096]{1,0:T(8,128)(2,1)}, u32[]{:S(2)}, u32[]{:S(2)}) collective-permute-start(bf16[96,4096]{1,0:T(8,128)(2,1)} %convolution_convert_fusion.3), channel_id=1, source_target_pairs={{0,16},{8,24},{16,0},{24,8},{1,17},{9,25},{17,1},{25,9},{2,18},{10... | collective-permute-start | bytes 2359304 | tf_op jit(solution)/shard_map/ppermute | solution.py:26
  53.3 17.8 %all-to-all-done.summands = bf16[4,32,4096]{2,1,0:T(8,128)(2,1)} async-done(((bf16[4,32,4096]{2,1,0:T(8,128)(2,1)}), bf16[4,32,4096]{2,1,0:T(8,128)(2,1)}, u32[]{:S(2)}, u32[]{:S(2)}) %all-to-all-start) | async-done | bytes 1048608 | tf_op jit(solution)/shard_map/all_to_all | solution.py:17
  71.1 1.0 copy-done.2
  72.1 1.7 %result_rows.1 = bf16[32,4096]{1,0:T(8,128)(2,1)S(1)} custom-call(bf16[4,32,4096]{2,1,0:T(8,128)(2,1)} %all-to-all-done.summands, bf16[1,4096]{1,0:T(2,128)(2,1)S(1)} %reshape.90.gain, bf16[2,32,4096]{2,1,0:T(8,128)(2,1)S(1)} %copy-done.2), custom_call_target="tpu_custom_call" | custom-call | flops 1966080 | bytes 1835008 | tf_op jit(solution)/shard_map/result_rows/pallas_call | solution.py:114
  73.8 1.9 %collective-permute-start.6 = (bf16[32,4096]{1,0:T(8,128)(2,1)S(1)}, bf16[32,4096]{1,0:T(8,128)(2,1)}, u32[]{:S(2)}, u32[]{:S(2)}) collective-permute-start(bf16[32,4096]{1,0:T(8,128)(2,1)S(1)} %result_rows.1), channel_id=1, source_target_pairs={{0,1},{1,0},{2,3},{3,2},{4,5},{5,4},{6,7},{7,6},{8,9},{9,8},{10,11... | collective-permute-start | bytes 786440 | tf_op jit(solution)/shard_map/ppermute | solution.py:30
  75.8 4.0 %collective-permute-start.7 = (bf16[32,4096]{1,0:T(8,128)(2,1)S(1)}, bf16[32,4096]{1,0:T(8,128)(2,1)}, u32[]{:S(2)}, u32[]{:S(2)}) collective-permute-start(bf16[32,4096]{1,0:T(8,128)(2,1)S(1)} %result_rows.1), channel_id=1, source_target_pairs={{0,2},{2,4},{4,6},{6,0},{1,3},{3,5},{5,7},{7,1},{8,10},{10,12},{12... | collective-permute-start | bytes 786440 | tf_op jit(solution)/shard_map/ppermute | solution.py:26
  79.8 4.8 %collective-permute-start.9 = (bf16[32,4096]{1,0:T(8,128)(2,1)S(1)}, bf16[32,4096]{1,0:T(8,128)(2,1)}, u32[]{:S(2)}, u32[]{:S(2)}) collective-permute-start(bf16[32,4096]{1,0:T(8,128)(2,1)S(1)} %result_rows.1), channel_id=1, source_target_pairs={{0,6},{2,0},{4,2},{6,4},{1,7},{3,1},{5,3},{7,5},{8,14},{10,8},{12,... | collective-permute-start | bytes 786440 | tf_op jit(solution)/shard_map/ppermute | solution.py:26
  85.3 3.4 %all-to-all-start.1 = ((f32[8,32,128]{2,1,0:T(8,128)}), f32[8,32,128]{2,1,0:T(8,128)S(1)}, u32[]{:S(2)}, u32[]{:S(2)}) async-start(f32[8,32,128]{2,1,0:T(8,128)} %broadcast_in_dim.4), calls=%async_computation.1 | async-start | bytes 262144 | tf_op jit(solution)/shard_map/all_to_all | solution.py:17
  88.7 1.6 broadcast_in_dim.5
  91.0 2.5 %collective-permute-done.7 = bf16[32,4096]{1,0:T(8,128)(2,1)} collective-permute-done((bf16[32,4096]{1,0:T(8,128)(2,1)S(1)}, bf16[32,4096]{1,0:T(8,128)(2,1)}, u32[]{:S(2)}, u32[]{:S(2)}) %collective-permute-start.7) | collective-permute-done | bytes 262176 | tf_op jit(solution)/shard_map/ppermute | solution.py:26
  93.5 4.6 %collective-permute-start.5 = (bf16[96,4096]{1,0:T(8,128)(2,1)}, bf16[96,4096]{1,0:T(8,128)(2,1)}, u32[]{:S(2)}, u32[]{:S(2)}) collective-permute-start(bf16[96,4096]{1,0:T(8,128)(2,1)} %convolution_convert_fusion.2), channel_id=1, source_target_pairs={{0,24},{8,0},{16,8},{24,16},{1,25},{9,1},{17,9},{25,17},{2,26},{10... | collective-permute-start | bytes 2359304 | tf_op jit(solution)/shard_map/ppermute | solution.py:26
  98.0 1.6 slice.28
  99.6 3.6 %collective-permute-done.9 = bf16[32,4096]{1,0:T(8,128)(2,1)} collective-permute-done((bf16[32,4096]{1,0:T(8,128)(2,1)S(1)}, bf16[32,4096]{1,0:T(8,128)(2,1)}, u32[]{:S(2)}, u32[]{:S(2)}) %collective-permute-start.9) | collective-permute-done | bytes 262176 | tf_op jit(solution)/shard_map/ppermute | solution.py:26
  103.2 3.8 %collective-permute-start.11 = (bf16[16,4096]{1,0:T(8,128)(2,1)}, bf16[16,4096]{1,0:T(8,128)(2,1)}, u32[]{:S(2)}, u32[]{:S(2)}) collective-permute-start(bf16[16,4096]{1,0:T(8,128)(2,1)} %slice.28), channel_id=1, source_target_pairs={{0,2},{2,4},{4,6},{6,0},{1,3},{3,5},{5,7},{7,1},{8,10},{10,12},{12... | collective-permute-start | bytes 393224 | tf_op jit(solution)/shard_map/ppermute | solution.py:26
  107.1 1.6 slice.29
  108.6 5.0 %collective-permute-start.13 = (bf16[16,4096]{1,0:T(8,128)(2,1)}, bf16[16,4096]{1,0:T(8,128)(2,1)}, u32[]{:S(2)}, u32[]{:S(2)}) collective-permute-start(bf16[16,4096]{1,0:T(8,128)(2,1)} %slice.29), channel_id=1, source_target_pairs={{0,6},{2,0},{4,2},{6,4},{1,7},{3,1},{5,3},{7,5},{8,14},{10,8},{12,... | collective-permute-start | bytes 393224 | tf_op jit(solution)/shard_map/ppermute | solution.py:26
  113.6 1.7 constant_dynamic-update-slice_fusion.8
  115.3 1.9 %collective-permute-start.8 = (bf16[32,4096]{1,0:T(8,128)(2,1)}, bf16[32,4096]{1,0:T(8,128)(2,1)S(1)}, u32[]{:S(2)}, u32[]{:S(2)}) collective-permute-start(bf16[32,4096]{1,0:T(8,128)(2,1)} %collective-permute-done.7), channel_id=1, source_target_pairs={{0,1},{1,0},{2,3},{3,2},{4,5},{5,4},{6,7},{7,6},{8,9},{9,8},{10,11... | collective-permute-start | bytes 786440 | tf_op jit(solution)/shard_map/ppermute | solution.py:30
  117.2 1.7 constant_dynamic-update-slice_fusion.7
  118.9 2.4 %collective-permute-start.10 = (bf16[32,4096]{1,0:T(8,128)(2,1)}, bf16[32,4096]{1,0:T(8,128)(2,1)}, u32[]{:S(2)}, u32[]{:S(2)}) collective-permute-start(bf16[32,4096]{1,0:T(8,128)(2,1)} %collective-permute-done.9), channel_id=1, source_target_pairs={{0,1},{1,0},{2,3},{3,2},{4,5},{5,4},{6,7},{7,6},{8,9},{9,8},{10,11... | collective-permute-start | bytes 786440 | tf_op jit(solution)/shard_map/ppermute | solution.py:30
  121.4 1.1 copy-done.3
  122.5 2.0 %pack.1 = bf16[24,4,5120]{2,1,0:T(4,128)(2,1)S(1)} custom-call(bf16[96,4096]{1,0:T(8,128)(2,1)S(1)} %copy-done.3, bf16[96,4096]{1,0:T(8,128)(2,1)} %collective-permute-done.3.second, bf16[96,4096]{1,0:T(8,128)(2,1)} %collective-permute-done.4.third, bf16[96,4096]{1,0:T(8,128)(2,1)} %collective-permute-done.5.fourth, ...), custom_call_target="tpu_custom_call" | custom-call | flops 1179648 | bytes 3932160 | tf_op jit(solution)/shard_map/pack/pallas_call | solution.py:60
  124.6 0.9 copy-done.1
  125.5 13.4 %all-to-all-start.2 = ((bf16[24,4,5120]{2,1,0:T(4,128)(2,1)}), bf16[24,4,5120]{2,1,0:T(4,128)(2,1)}, u32[]{:S(2)}, u32[]{:S(2)}) async-start(bf16[24,4,5120]{2,1,0:T(4,128)(2,1)} %copy-done.1), calls=%async_computation.2 | async-start | bytes 1966080 | tf_op jit(solution)/shard_map/all_to_all | solution.py:17
  139.0 1.9 %collective-permute-start.12 = (bf16[16,4096]{1,0:T(8,128)(2,1)}, bf16[16,4096]{1,0:T(8,128)(2,1)S(1)}, u32[]{:S(2)}, u32[]{:S(2)}) collective-permute-start(bf16[16,4096]{1,0:T(8,128)(2,1)} %collective-permute-done.11), channel_id=1, source_target_pairs={{0,1},{1,0},{2,3},{3,2},{4,5},{5,4},{6,7},{7,6},{8,9},{9,8},{10,11... | collective-permute-start | bytes 393224 | tf_op jit(solution)/shard_map/ppermute | solution.py:30
  140.9 2.4 %collective-permute-start.14 = (bf16[16,4096]{1,0:T(8,128)(2,1)}, bf16[16,4096]{1,0:T(8,128)(2,1)S(1)}, u32[]{:S(2)}, u32[]{:S(2)}) collective-permute-start(bf16[16,4096]{1,0:T(8,128)(2,1)} %collective-permute-done.13), channel_id=1, source_target_pairs={{0,1},{1,0},{2,3},{3,2},{4,5},{5,4},{6,7},{7,6},{8,9},{9,8},{10,11... | collective-permute-start | bytes 393224 | tf_op jit(solution)/shard_map/ppermute | solution.py:30
  144.1 1.7 constant_dynamic-update-slice_fusion.5
  145.7 1.7 constant_dynamic-update-slice_fusion.4
  147.4 1.6 constant_dynamic-update-slice_fusion.3
  149.6 1.6 constant_dynamic-update-slice_fusion.1
  151.9 15.4 %all-to-all-done.2.last = bf16[24,4,5120]{2,1,0:T(4,128)(2,1)} async-done(((bf16[24,4,5120]{2,1,0:T(4,128)(2,1)}), bf16[24,4,5120]{2,1,0:T(4,128)(2,1)}, u32[]{:S(2)}, u32[]{:S(2)}) %all-to-all-start.2) | async-done | bytes 983072 | tf_op jit(solution)/shard_map/all_to_all | solution.py:17
  167.3 2.0 %last_sums.1 = (f32[4,4096]{1,0:T(4,128)}, f32[1,4096]{1,0:T(1,128)}) custom-call(bf16[24,4,5120]{2,1,0:T(4,128)(2,1)} %all-to-all-done.2.last), custom_call_target="tpu_custom_call" | custom-call | flops 491520 | bytes 983040 | tf_op jit(solution)/shard_map/last_sums/pallas_call | solution.py:86
  (45 shorter events, 6.2 us)
Async XLA Ops:
  0.6 2.5 %copy-start = (bf16[384,4096]{1,0:T(8,128)(2,1)S(1)}, bf16[384,4096]{1,0:T(8,128)(2,1)}, u32[]{:S(2)}) copy-start(bf16[384,4096]{1,0:T(8,128)(2,1)} %param.8) | copy-start | bytes 9437188
  0.6 2.5 %copy-start.7 = (bf16[256,384]{1,0:T(8,128)(2,1)S(1)}, bf16[256,384]{1,0:T(8,128)(2,1)}, u32[]{:S(2)}) copy-start(bf16[256,384]{1,0:T(8,128)(2,1)} %param.7) | copy-start | bytes 589828
  3.2 3.6 %copy-start.8 = (bf16[4096]{0:T(1024)(128)(2,1)S(1)}, bf16[4096]{0:T(1024)(128)(2,1)}, u32[]{:S(2)}) copy-start(bf16[4096]{0:T(1024)(128)(2,1)} %param.6) | copy-start | bytes 24580
  4.9 4.9 %collective-permute-start = (bf16[128,4096]{1,0:T(8,128)(2,1)}, bf16[128,4096]{1,0:T(8,128)(2,1)}, u32[]{:S(2)}, u32[]{:S(2)}) collective-permute-start(bf16[128,4096]{1,0:T(8,128)(2,1)} %convolution_convert_fusion.1), channel_id=1, source_target_pairs={{0,1},{1,0},{2,3},{3,2},{4,5},{5,4},{6,7},{7,6},{8,9},{9,8},{10,11... | collective-permute-start | bytes 3145736 | tf_op jit(solution)/shard_map/ppermute | solution.py:30
  8.6 4.0 %copy-start.4 = (bf16[256,4096]{1,0:T(8,128)(2,1)S(1)}, bf16[256,4096]{1,0:T(8,128)(2,1)}, u32[]{:S(2)}) copy-start(bf16[256,4096]{1,0:T(8,128)(2,1)} %param.5) | copy-start | bytes 6291460
  12.5 1.2 copy-start.6
  15.6 55.5 %all-to-all-start = ((bf16[4,32,4096]{2,1,0:T(8,128)(2,1)}), bf16[4,32,4096]{2,1,0:T(8,128)(2,1)}, u32[]{:S(2)}, u32[]{:S(2)}) async-start(bf16[4,32,4096]{2,1,0:T(8,128)(2,1)} %bitcast.14), calls=%async_computation | async-start | bytes 2097152 | tf_op jit(solution)/shard_map/all_to_all | solution.py:17
  29.2 10.7 %copy-start.5 = (bf16[256,4096]{1,0:T(8,128)(2,1)S(1)}, bf16[256,4096]{1,0:T(8,128)(2,1)}, u32[]{:S(2)}) copy-start(bf16[256,4096]{1,0:T(8,128)(2,1)} %param.5) | copy-start | bytes 6291460
  29.2 5.8 %collective-permute-start.1 = (f32[32,128]{1,0:T(8,128)S(1)}, f32[32,128]{1,0:T(8,128)S(1)}, u32[]{:S(2)}, u32[]{:S(2)}) collective-permute-start(f32[32,128]{1,0:T(8,128)S(1)} %add_bitcast_fusion), channel_id=1, source_target_pairs={{0,8},{8,0},{16,24},{24,16},{1,9},{9,1},{17,25},{25,17},{2,10},{10... | collective-permute-start | bytes 49160 | tf_op jit(solution)/shard_map/ppermute | solution.py:30
  35.0 18.2 %collective-permute-start.2 = (f32[32,128]{1,0:T(8,128)S(1)}, f32[32,128]{1,0:T(8,128)S(1)}, u32[]{:S(2)}, u32[]{:S(2)}) collective-permute-start(f32[32,128]{1,0:T(8,128)S(1)} %add.184), channel_id=1, source_target_pairs={{0,16},{8,24},{16,0},{24,8},{1,17},{9,25},{17,1},{25,9},{2,18},{10... | collective-permute-start | bytes 49160 | tf_op jit(solution)/shard_map/ppermute | solution.py:30
  46.8 68.5 %collective-permute-start.3 = (bf16[96,4096]{1,0:T(8,128)(2,1)}, bf16[96,4096]{1,0:T(8,128)(2,1)}, u32[]{:S(2)}, u32[]{:S(2)}) collective-permute-start(bf16[96,4096]{1,0:T(8,128)(2,1)} %convolution_convert_fusion.4), channel_id=1, source_target_pairs={{0,8},{8,16},{16,24},{24,0},{1,9},{9,17},{17,25},{25,1},{2,10},{10... | collective-permute-start | bytes 2359304 | tf_op jit(solution)/shard_map/ppermute | solution.py:26
  49.3 69.6 %collective-permute-start.4 = (bf16[96,4096]{1,0:T(8,128)(2,1)}, bf16[96,4096]{1,0:T(8,128)(2,1)}, u32[]{:S(2)}, u32[]{:S(2)}) collective-permute-start(bf16[96,4096]{1,0:T(8,128)(2,1)} %convolution_convert_fusion.3), channel_id=1, source_target_pairs={{0,16},{8,24},{16,0},{24,8},{1,17},{9,25},{17,1},{25,9},{2,18},{10... | collective-permute-start | bytes 2359304 | tf_op jit(solution)/shard_map/ppermute | solution.py:26
  71.1 1.0 copy-start.2
  73.8 34.8 %collective-permute-start.6 = (bf16[32,4096]{1,0:T(8,128)(2,1)S(1)}, bf16[32,4096]{1,0:T(8,128)(2,1)}, u32[]{:S(2)}, u32[]{:S(2)}) collective-permute-start(bf16[32,4096]{1,0:T(8,128)(2,1)S(1)} %result_rows.1), channel_id=1, source_target_pairs={{0,1},{1,0},{2,3},{3,2},{4,5},{5,4},{6,7},{7,6},{8,9},{9,8},{10,11... | collective-permute-start | bytes 786440 | tf_op jit(solution)/shard_map/ppermute | solution.py:30
  75.8 17.7 %collective-permute-start.7 = (bf16[32,4096]{1,0:T(8,128)(2,1)S(1)}, bf16[32,4096]{1,0:T(8,128)(2,1)}, u32[]{:S(2)}, u32[]{:S(2)}) collective-permute-start(bf16[32,4096]{1,0:T(8,128)(2,1)S(1)} %result_rows.1), channel_id=1, source_target_pairs={{0,2},{2,4},{4,6},{6,0},{1,3},{3,5},{5,7},{7,1},{8,10},{10,12},{12... | collective-permute-start | bytes 786440 | tf_op jit(solution)/shard_map/ppermute | solution.py:26
  79.8 23.4 %collective-permute-start.9 = (bf16[32,4096]{1,0:T(8,128)(2,1)S(1)}, bf16[32,4096]{1,0:T(8,128)(2,1)}, u32[]{:S(2)}, u32[]{:S(2)}) collective-permute-start(bf16[32,4096]{1,0:T(8,128)(2,1)S(1)} %result_rows.1), channel_id=1, source_target_pairs={{0,6},{2,0},{4,2},{6,4},{1,7},{3,1},{5,3},{7,5},{8,14},{10,8},{12,... | collective-permute-start | bytes 786440 | tf_op jit(solution)/shard_map/ppermute | solution.py:26
  85.3 33.6 %all-to-all-start.1 = ((f32[8,32,128]{2,1,0:T(8,128)}), f32[8,32,128]{2,1,0:T(8,128)S(1)}, u32[]{:S(2)}, u32[]{:S(2)}) async-start(f32[8,32,128]{2,1,0:T(8,128)} %broadcast_in_dim.4), calls=%async_computation.1 | async-start | bytes 262144 | tf_op jit(solution)/shard_map/all_to_all | solution.py:17
  93.5 27.9 %collective-permute-start.5 = (bf16[96,4096]{1,0:T(8,128)(2,1)}, bf16[96,4096]{1,0:T(8,128)(2,1)}, u32[]{:S(2)}, u32[]{:S(2)}) collective-permute-start(bf16[96,4096]{1,0:T(8,128)(2,1)} %convolution_convert_fusion.2), channel_id=1, source_target_pairs={{0,24},{8,0},{16,8},{24,16},{1,25},{9,1},{17,9},{25,17},{2,26},{10... | collective-permute-start | bytes 2359304 | tf_op jit(solution)/shard_map/ppermute | solution.py:26
  103.2 35.7 %collective-permute-start.11 = (bf16[16,4096]{1,0:T(8,128)(2,1)}, bf16[16,4096]{1,0:T(8,128)(2,1)}, u32[]{:S(2)}, u32[]{:S(2)}) collective-permute-start(bf16[16,4096]{1,0:T(8,128)(2,1)} %slice.28), channel_id=1, source_target_pairs={{0,2},{2,4},{4,6},{6,0},{1,3},{3,5},{5,7},{7,1},{8,10},{10,12},{12... | collective-permute-start | bytes 393224 | tf_op jit(solution)/shard_map/ppermute | solution.py:26
  108.6 32.3 %collective-permute-start.13 = (bf16[16,4096]{1,0:T(8,128)(2,1)}, bf16[16,4096]{1,0:T(8,128)(2,1)}, u32[]{:S(2)}, u32[]{:S(2)}) collective-permute-start(bf16[16,4096]{1,0:T(8,128)(2,1)} %slice.29), channel_id=1, source_target_pairs={{0,6},{2,0},{4,2},{6,4},{1,7},{3,1},{5,3},{7,5},{8,14},{10,8},{12,... | collective-permute-start | bytes 393224 | tf_op jit(solution)/shard_map/ppermute | solution.py:26
  115.3 28.0 %collective-permute-start.8 = (bf16[32,4096]{1,0:T(8,128)(2,1)}, bf16[32,4096]{1,0:T(8,128)(2,1)S(1)}, u32[]{:S(2)}, u32[]{:S(2)}) collective-permute-start(bf16[32,4096]{1,0:T(8,128)(2,1)} %collective-permute-done.7), channel_id=1, source_target_pairs={{0,1},{1,0},{2,3},{3,2},{4,5},{5,4},{6,7},{7,6},{8,9},{9,8},{10,11... | collective-permute-start | bytes 786440 | tf_op jit(solution)/shard_map/ppermute | solution.py:30
  118.9 26.8 %collective-permute-start.10 = (bf16[32,4096]{1,0:T(8,128)(2,1)}, bf16[32,4096]{1,0:T(8,128)(2,1)}, u32[]{:S(2)}, u32[]{:S(2)}) collective-permute-start(bf16[32,4096]{1,0:T(8,128)(2,1)} %collective-permute-done.9), channel_id=1, source_target_pairs={{0,1},{1,0},{2,3},{3,2},{4,5},{5,4},{6,7},{7,6},{8,9},{9,8},{10,11... | collective-permute-start | bytes 786440 | tf_op jit(solution)/shard_map/ppermute | solution.py:30
  121.4 1.1 copy-start.3
  124.5 0.9 copy-start.1
  125.5 41.8 %all-to-all-start.2 = ((bf16[24,4,5120]{2,1,0:T(4,128)(2,1)}), bf16[24,4,5120]{2,1,0:T(4,128)(2,1)}, u32[]{:S(2)}, u32[]{:S(2)}) async-start(bf16[24,4,5120]{2,1,0:T(4,128)(2,1)} %copy-done.1), calls=%async_computation.2 | async-start | bytes 1966080 | tf_op jit(solution)/shard_map/all_to_all | solution.py:17
  139.0 10.0 %collective-permute-start.12 = (bf16[16,4096]{1,0:T(8,128)(2,1)}, bf16[16,4096]{1,0:T(8,128)(2,1)S(1)}, u32[]{:S(2)}, u32[]{:S(2)}) collective-permute-start(bf16[16,4096]{1,0:T(8,128)(2,1)} %collective-permute-done.11), channel_id=1, source_target_pairs={{0,1},{1,0},{2,3},{3,2},{4,5},{5,4},{6,7},{7,6},{8,9},{9,8},{10,11... | collective-permute-start | bytes 393224 | tf_op jit(solution)/shard_map/ppermute | solution.py:30
  140.9 10.3 %collective-permute-start.14 = (bf16[16,4096]{1,0:T(8,128)(2,1)}, bf16[16,4096]{1,0:T(8,128)(2,1)S(1)}, u32[]{:S(2)}, u32[]{:S(2)}) collective-permute-start(bf16[16,4096]{1,0:T(8,128)(2,1)} %collective-permute-done.13), channel_id=1, source_target_pairs={{0,1},{1,0},{2,3},{3,2},{4,5},{5,4},{6,7},{7,6},{8,9},{9,8},{10,11... | collective-permute-start | bytes 393224 | tf_op jit(solution)/shard_map/ppermute | solution.py:30

commit v6 on v5

--- a/solution.py
+++ b/solution.py
@@ -192,16 +192,11 @@
     last = exchange(packed, ("zl", "y"))
     weight_grad, gain_grad = last_sums(last, width)
 
-    before, after = shifted(rows, "zh", 1), shifted(rows, "zh", n_zh - 1)
-    upper, lower = before[: own // 2], after[own // 2 :]
-    upper, lower = shifted(upper, "zh", 1), shifted(lower, "zh", n_zh - 1)
-    pieces = (
-        (0, 0, rows), (1, 0, before), (n_zh - 1, 0, after), (2, 0, upper), (2, own // 2, lower)
-    )
     result = jnp.zeros((tokens, width), BF16)
-    for shift, offset, piece in pieces:
+    for shift in (0, 1, n_zh - 1, 2):
+        piece = rows if shift == 0 else shifted(rows, "zh", shift)
         other = swapped(piece, "c", 1)
-        source = lax.rem(zh + n_zh - shift, n_zh) * own + offset
+        source = lax.rem(zh + n_zh - shift, n_zh) * own
         result = lax.dynamic_update_slice_in_dim(result, piece, own_start + source, 0)
         result = lax.dynamic_update_slice_in_dim(result, other, other_start + source, 0)
     return weight_grad, gain_grad.reshape(-1), result

time: 171 us -> 192 us (1.12)
  the two profiles are of different devices: /device:TPU:120 before, /device:TPU:122 now
where the time goes in v6:
time: 192 us; the launch traced here: 191 us
  waiting for transfers between devices  73 us (38%)
  starting transfers between devices  70.7 us (37%)
  local copies, waits for them, and re-layouts  19.8 us (10%)
  matrix products  12.2 us (6%)
  other arithmetic  8.27 us (4%)
  Pallas kernels  5.7 us (3%)
    all_to_all x3, waiting for transfers between devices, exchange(): return lax.all_to_all(blocks, axes, 0, 0, tiled=True)  35.3 us
    ppermute x6, starting transfers between devices, shifted(): lax.ppermute(block, axis, [(i, (i + shift) % peers) for i in range(peers)])  29.5 us
    ppermute x7, waiting for transfers between devices, swapped(): lax.ppermute(block, axis, [(i, i ^ bit) for i in range(lax.axis_size(axis...  28.2 us
    all_to_all x3, starting transfers between devices, exchange(): return lax.all_to_all(blocks, axes, 0, 0, tiled=True)  26.5 us
    ppermute x7, starting transfers between devices, swapped(): lax.ppermute(block, axis, [(i, i ^ bit) for i in range(lax.axis_size(axis...  14.7 us
    ppermute x6, waiting for transfers between devices, shifted(): lax.ppermute(block, axis, [(i, (i + shift) % peers) for i in range(peers)])  9.48 us
    dot_general x4, matrix products, block(): lax.dot_general(columns, normed, (((0,), (0,)), ((), ())), preferred_elem...  8.48 us
    dynamic_update_slice x4, local copies, waits for them, and re-layouts, body(): lax.dynamic_update_slice_in_dim(result, other, other_start + source, 0)  6.68 us
  transfers between devices with their start and end apart: 16, of which 6 were waited for; matrix products, arithmetic and copies ran while one was open for 14% of the time, Pallas kernels for 2%

profile of v6, /device:TPU:122, one launch (start us, length us, event | category | flops | bytes accessed | tf_op | source)
XLA Modules:
  0.0 190.7 jit_solution(1342624160711250395)
XLA Ops:
  0.7 2.2 %fusion = f32[256]{0:T(256)S(1)} fusion(bf16[256,4096]{1,0:T(8,128)(2,1)} %param.5), kind=kLoop, calls=%fused_computation.9 | loop fusion | flops 3145472 | bytes 2098176 | tf_op jit(solution)/shard_map/reduce_sum | solution.py:141
  3.2 1.7 convolution_convert_fusion.1
  4.9 1.9 %collective-permute-start = (bf16[128,4096]{1,0:T(8,128)(2,1)}, bf16[128,4096]{1,0:T(8,128)(2,1)}, u32[]{:S(2)}, u32[]{:S(2)}) collective-permute-start(bf16[128,4096]{1,0:T(8,128)(2,1)} %convolution_convert_fusion.1), channel_id=1, source_target_pairs={{0,1},{1,0},{2,3},{3,2},{4,5},{5,4},{6,7},{7,6},{8,9},{9,8},{10,11... | collective-permute-start | bytes 3145736 | tf_op jit(solution)/shard_map/ppermute | solution.py:30
  6.9 1.7 convolution_convert_fusion
  8.6 1.2 collective-permute-done
  9.7 2.8 %fusion.3 = bf16[128,4096]{1,0:T(8,128)(2,1)} fusion(bf16[128,4096]{1,0:T(8,128)(2,1)} %convolution_convert_fusion, bf16[128,4096]{1,0:T(8,128)(2,1)} %collective-permute-done), kind=kLoop, calls=%fused_computation.14 | loop fusion | flops 2097152 | bytes 3145728 | tf_op jit(solution)/shard_map/convert_element_type | solution.py:153
  13.8 1.8 fusion.4
  15.6 13.6 %all-to-all-start = ((bf16[4,32,4096]{2,1,0:T(8,128)(2,1)}), bf16[4,32,4096]{2,1,0:T(8,128)(2,1)}, u32[]{:S(2)}, u32[]{:S(2)}) async-start(bf16[4,32,4096]{2,1,0:T(8,128)(2,1)} %bitcast.14), calls=%async_computation | async-start | bytes 2097152 | tf_op jit(solution)/shard_map/all_to_all | solution.py:17
  29.2 2.4 %collective-permute-start.1 = (f32[32,128]{1,0:T(8,128)S(1)}, f32[32,128]{1,0:T(8,128)S(1)}, u32[]{:S(2)}, u32[]{:S(2)}) collective-permute-start(f32[32,128]{1,0:T(8,128)S(1)} %add_bitcast_fusion), channel_id=1, source_target_pairs={{0,8},{8,0},{16,24},{24,16},{1,9},{9,1},{17,25},{25,17},{2,10},{10... | collective-permute-start | bytes 49160 | tf_op jit(solution)/shard_map/ppermute | solution.py:30
  31.6 1.1 dynamic-slice_bitcast_fusion
  33.0 1.8 collective-permute-done.1
  34.8 3.3 %convolution_convert_fusion.4 = bf16[96,4096]{1,0:T(8,128)(2,1)} fusion(bf16[256,384]{1,0:T(8,128)(2,1)S(1)} %convolution_convert_fusion.6, bf16[256,4096]{1,0:T(8,128)(2,1)} %param.5, f32[4096]{0:T(1024)S(1)} %convert_element_type.61, f32[256]{0:T(256)S(1)} %add_rsqrt_fusion), kind=kOutput, calls=%fused_computation.7 | convolution fusion | flops 205914112 | bytes 2966528 | tf_op jit(solution)/shard_map/dot_general | solution.py:173
  38.1 3.4 %collective-permute-start.3 = (bf16[96,4096]{1,0:T(8,128)(2,1)}, bf16[96,4096]{1,0:T(8,128)(2,1)}, u32[]{:S(2)}, u32[]{:S(2)}) collective-permute-start(bf16[96,4096]{1,0:T(8,128)(2,1)} %convolution_convert_fusion.4), channel_id=1, source_target_pairs={{0,8},{8,16},{16,24},{24,0},{1,9},{9,17},{17,25},{25,1},{2,10},{10... | collective-permute-start | bytes 2359304 | tf_op jit(solution)/shard_map/ppermute | solution.py:26
  41.5 1.8 convolution_convert_fusion.3
  43.3 3.0 %collective-permute-start.4 = (bf16[96,4096]{1,0:T(8,128)(2,1)}, bf16[96,4096]{1,0:T(8,128)(2,1)}, u32[]{:S(2)}, u32[]{:S(2)}) collective-permute-start(bf16[96,4096]{1,0:T(8,128)(2,1)} %convolution_convert_fusion.3), channel_id=1, source_target_pairs={{0,16},{8,24},{16,0},{24,8},{1,17},{9,25},{17,1},{25,9},{2,18},{10... | collective-permute-start | bytes 2359304 | tf_op jit(solution)/shard_map/ppermute | solution.py:26
  46.3 1.7 convolution_convert_fusion.2
  48.0 4.1 %collective-permute-start.5 = (bf16[96,4096]{1,0:T(8,128)(2,1)}, bf16[96,4096]{1,0:T(8,128)(2,1)}, u32[]{:S(2)}, u32[]{:S(2)}) collective-permute-start(bf16[96,4096]{1,0:T(8,128)(2,1)} %convolution_convert_fusion.2), channel_id=1, source_target_pairs={{0,24},{8,0},{16,8},{24,16},{1,25},{9,1},{17,9},{25,17},{2,26},{10... | collective-permute-start | bytes 2359304 | tf_op jit(solution)/shard_map/ppermute | solution.py:26
  52.1 0.8 pad_maximum_fusion.slices
  52.9 2.2 %collective-permute-start.2 = (f32[32,128]{1,0:T(8,128)S(1)}, f32[32,128]{1,0:T(8,128)S(1)}, u32[]{:S(2)}, u32[]{:S(2)}) collective-permute-start(f32[32,128]{1,0:T(8,128)S(1)} %add.168), channel_id=1, source_target_pairs={{0,16},{8,24},{16,0},{24,8},{1,17},{9,25},{17,1},{25,9},{2,18},{10... | collective-permute-start | bytes 49160 | tf_op jit(solution)/shard_map/ppermute | solution.py:30
  55.1 1.7 convolution_convert_fusion.5.first
  56.8 25.3 %collective-permute-done.2 = f32[32,128]{1,0:T(8,128)S(1)} collective-permute-done((f32[32,128]{1,0:T(8,128)S(1)}, f32[32,128]{1,0:T(8,128)S(1)}, u32[]{:S(2)}, u32[]{:S(2)}) %collective-permute-start.2) | collective-permute-done | bytes 16416 | tf_op jit(solution)/shard_map/ppermute | solution.py:30
  82.1 1.0 copy-done.2
  83.2 1.7 result_rows.1
  84.9 1.9 %collective-permute-start.6 = (bf16[32,4096]{1,0:T(8,128)(2,1)S(1)}, bf16[32,4096]{1,0:T(8,128)(2,1)}, u32[]{:S(2)}, u32[]{:S(2)}) collective-permute-start(bf16[32,4096]{1,0:T(8,128)(2,1)S(1)} %result_rows.1), channel_id=1, source_target_pairs={{0,1},{1,0},{2,3},{3,2},{4,5},{5,4},{6,7},{7,6},{8,9},{9,8},{10,11... | collective-permute-start | bytes 786440 | tf_op jit(solution)/shard_map/ppermute | solution.py:30
  86.8 6.9 %collective-permute-start.7 = (bf16[32,4096]{1,0:T(8,128)(2,1)S(1)}, bf16[32,4096]{1,0:T(8,128)(2,1)}, u32[]{:S(2)}, u32[]{:S(2)}) collective-permute-start(bf16[32,4096]{1,0:T(8,128)(2,1)S(1)} %result_rows.1), channel_id=1, source_target_pairs={{0,2},{2,4},{4,6},{6,0},{1,3},{3,5},{5,7},{7,1},{8,10},{10,12},{12... | collective-permute-start | bytes 786440 | tf_op jit(solution)/shard_map/ppermute | solution.py:26
  94.4 4.9 %all-to-all-start.1 = ((f32[8,32,128]{2,1,0:T(8,128)}), f32[8,32,128]{2,1,0:T(8,128)S(1)}, u32[]{:S(2)}, u32[]{:S(2)}) async-start(f32[8,32,128]{2,1,0:T(8,128)} %broadcast_in_dim.4), calls=%async_computation.1 | async-start | bytes 262144 | tf_op jit(solution)/shard_map/all_to_all | solution.py:17
  99.3 6.9 %collective-permute-start.9 = (bf16[32,4096]{1,0:T(8,128)(2,1)S(1)}, bf16[32,4096]{1,0:T(8,128)(2,1)}, u32[]{:S(2)}, u32[]{:S(2)}) collective-permute-start(bf16[32,4096]{1,0:T(8,128)(2,1)S(1)} %result_rows.1), channel_id=1, source_target_pairs={{0,6},{2,0},{4,2},{6,4},{1,7},{3,1},{5,3},{7,5},{8,14},{10,8},{12,... | collective-permute-start | bytes 786440 | tf_op jit(solution)/shard_map/ppermute | solution.py:26
  106.2 5.2 %collective-permute-start.11 = (bf16[32,4096]{1,0:T(8,128)(2,1)S(1)}, bf16[32,4096]{1,0:T(8,128)(2,1)}, u32[]{:S(2)}, u32[]{:S(2)}) collective-permute-start(bf16[32,4096]{1,0:T(8,128)(2,1)S(1)} %result_rows.1), channel_id=1, source_target_pairs={{0,4},{2,6},{4,0},{6,2},{1,5},{3,7},{5,1},{7,3},{8,12},{10,14},{12... | collective-permute-start | bytes 786440 | tf_op jit(solution)/shard_map/ppermute | solution.py:26
  111.5 1.6 broadcast_in_dim.5
  113.0 0.7 constant_dynamic-update-slice_fusion.7
  113.7 17.8 %all-to-all-done.1 = f32[8,32,128]{2,1,0:T(8,128)S(1)} async-done(((f32[8,32,128]{2,1,0:T(8,128)}), f32[8,32,128]{2,1,0:T(8,128)S(1)}, u32[]{:S(2)}, u32[]{:S(2)}) %all-to-all-start.1) | async-done | bytes 131104 | tf_op jit(solution)/shard_map/all_to_all | solution.py:17
  131.6 1.9 %collective-permute-start.8 = (bf16[32,4096]{1,0:T(8,128)(2,1)}, bf16[32,4096]{1,0:T(8,128)(2,1)}, u32[]{:S(2)}, u32[]{:S(2)}) collective-permute-start(bf16[32,4096]{1,0:T(8,128)(2,1)} %collective-permute-done.7), channel_id=1, source_target_pairs={{0,1},{1,0},{2,3},{3,2},{4,5},{5,4},{6,7},{7,6},{8,9},{9,8},{10,11... | collective-permute-start | bytes 786440 | tf_op jit(solution)/shard_map/ppermute | solution.py:30
  133.5 2.4 %collective-permute-start.10 = (bf16[32,4096]{1,0:T(8,128)(2,1)}, bf16[32,4096]{1,0:T(8,128)(2,1)}, u32[]{:S(2)}, u32[]{:S(2)}) collective-permute-start(bf16[32,4096]{1,0:T(8,128)(2,1)} %collective-permute-done.9), channel_id=1, source_target_pairs={{0,1},{1,0},{2,3},{3,2},{4,5},{5,4},{6,7},{7,6},{8,9},{9,8},{10,11... | collective-permute-start | bytes 786440 | tf_op jit(solution)/shard_map/ppermute | solution.py:30
  135.9 9.5 %collective-permute-done.11 = bf16[32,4096]{1,0:T(8,128)(2,1)} collective-permute-done((bf16[32,4096]{1,0:T(8,128)(2,1)S(1)}, bf16[32,4096]{1,0:T(8,128)(2,1)}, u32[]{:S(2)}, u32[]{:S(2)}) %collective-permute-start.11) | collective-permute-done | bytes 262176 | tf_op jit(solution)/shard_map/ppermute | solution.py:26
  145.4 1.9 %collective-permute-start.12 = (bf16[32,4096]{1,0:T(8,128)(2,1)}, bf16[32,4096]{1,0:T(8,128)(2,1)}, u32[]{:S(2)}, u32[]{:S(2)}) collective-permute-start(bf16[32,4096]{1,0:T(8,128)(2,1)} %collective-permute-done.11), channel_id=1, source_target_pairs={{0,1},{1,0},{2,3},{3,2},{4,5},{5,4},{6,7},{7,6},{8,9},{9,8},{10,11... | collective-permute-start | bytes 786440 | tf_op jit(solution)/shard_map/ppermute | solution.py:30
  147.3 1.1 copy-done.3
  148.5 2.0 %pack.1 = bf16[24,4,5120]{2,1,0:T(4,128)(2,1)S(1)} custom-call(bf16[96,4096]{1,0:T(8,128)(2,1)S(1)} %copy-done.3, bf16[96,4096]{1,0:T(8,128)(2,1)} %collective-permute-done.3.second, bf16[96,4096]{1,0:T(8,128)(2,1)} %collective-permute-done.4.third, bf16[96,4096]{1,0:T(8,128)(2,1)} %collective-permute-done.5.fourth, ...), custom_call_target="tpu_custom_call" | custom-call | flops 1179648 | bytes 3932160 | tf_op jit(solution)/shard_map/pack/pallas_call | solution.py:60
  150.5 1.0 copy-done.1
  151.5 8.0 %all-to-all-start.2 = ((bf16[24,4,5120]{2,1,0:T(4,128)(2,1)}), bf16[24,4,5120]{2,1,0:T(4,128)(2,1)}, u32[]{:S(2)}, u32[]{:S(2)}) async-start(bf16[24,4,5120]{2,1,0:T(4,128)(2,1)} %copy-done.1), calls=%async_computation.2 | async-start | bytes 1966080 | tf_op jit(solution)/shard_map/all_to_all | solution.py:17
  159.6 1.7 constant_dynamic-update-slice_fusion.6
  161.2 1.7 constant_dynamic-update-slice_fusion.5
  162.9 1.7 constant_dynamic-update-slice_fusion.4
  164.6 1.7 constant_dynamic-update-slice_fusion.3
  166.2 1.7 constant_dynamic-update-slice_fusion.2
  167.9 1.7 constant_dynamic-update-slice_fusion.1
  169.6 1.7 constant_dynamic-update-slice_fusion
  171.3 17.5 %all-to-all-done.2.last = bf16[24,4,5120]{2,1,0:T(4,128)(2,1)} async-done(((bf16[24,4,5120]{2,1,0:T(4,128)(2,1)}), bf16[24,4,5120]{2,1,0:T(4,128)(2,1)}, u32[]{:S(2)}, u32[]{:S(2)}) %all-to-all-start.2) | async-done | bytes 983072 | tf_op jit(solution)/shard_map/all_to_all | solution.py:17
  188.8 2.0 %last_sums.1 = (f32[4,4096]{1,0:T(4,128)}, f32[1,4096]{1,0:T(1,128)}) custom-call(bf16[24,4,5120]{2,1,0:T(4,128)(2,1)} %all-to-all-done.2.last), custom_call_target="tpu_custom_call" | custom-call | flops 491520 | bytes 983040 | tf_op jit(solution)/shard_map/last_sums/pallas_call | solution.py:86
  (37 shorter events, 2.6 us)
Async XLA Ops:
  0.6 2.5 %copy-start = (bf16[384,4096]{1,0:T(8,128)(2,1)S(1)}, bf16[384,4096]{1,0:T(8,128)(2,1)}, u32[]{:S(2)}) copy-start(bf16[384,4096]{1,0:T(8,128)(2,1)} %param.8) | copy-start | bytes 9437188
  0.6 2.5 %copy-start.7 = (bf16[256,384]{1,0:T(8,128)(2,1)S(1)}, bf16[256,384]{1,0:T(8,128)(2,1)}, u32[]{:S(2)}) copy-start(bf16[256,384]{1,0:T(8,128)(2,1)} %param.7) | copy-start | bytes 589828
  3.2 3.6 %copy-start.8 = (bf16[4096]{0:T(1024)(128)(2,1)S(1)}, bf16[4096]{0:T(1024)(128)(2,1)}, u32[]{:S(2)}) copy-start(bf16[4096]{0:T(1024)(128)(2,1)} %param.6) | copy-start | bytes 24580
  4.9 4.9 %collective-permute-start = (bf16[128,4096]{1,0:T(8,128)(2,1)}, bf16[128,4096]{1,0:T(8,128)(2,1)}, u32[]{:S(2)}, u32[]{:S(2)}) collective-permute-start(bf16[128,4096]{1,0:T(8,128)(2,1)} %convolution_convert_fusion.1), channel_id=1, source_target_pairs={{0,1},{1,0},{2,3},{3,2},{4,5},{5,4},{6,7},{7,6},{8,9},{9,8},{10,11... | collective-permute-start | bytes 3145736 | tf_op jit(solution)/shard_map/ppermute | solution.py:30
  8.6 4.0 %copy-start.4 = (bf16[256,4096]{1,0:T(8,128)(2,1)S(1)}, bf16[256,4096]{1,0:T(8,128)(2,1)}, u32[]{:S(2)}) copy-start(bf16[256,4096]{1,0:T(8,128)(2,1)} %param.5) | copy-start | bytes 6291460
  12.5 1.2 copy-start.6
  15.6 66.5 %all-to-all-start = ((bf16[4,32,4096]{2,1,0:T(8,128)(2,1)}), bf16[4,32,4096]{2,1,0:T(8,128)(2,1)}, u32[]{:S(2)}, u32[]{:S(2)}) async-start(bf16[4,32,4096]{2,1,0:T(8,128)(2,1)} %bitcast.14), calls=%async_computation | async-start | bytes 2097152 | tf_op jit(solution)/shard_map/all_to_all | solution.py:17
  29.2 5.6 %collective-permute-start.1 = (f32[32,128]{1,0:T(8,128)S(1)}, f32[32,128]{1,0:T(8,128)S(1)}, u32[]{:S(2)}, u32[]{:S(2)}) collective-permute-start(f32[32,128]{1,0:T(8,128)S(1)} %add_bitcast_fusion), channel_id=1, source_target_pairs={{0,8},{8,0},{16,24},{24,16},{1,9},{9,1},{17,25},{25,17},{2,10},{10... | collective-permute-start | bytes 49160 | tf_op jit(solution)/shard_map/ppermute | solution.py:30
  33.0 8.5 %copy-start.5 = (bf16[256,4096]{1,0:T(8,128)(2,1)S(1)}, bf16[256,4096]{1,0:T(8,128)(2,1)}, u32[]{:S(2)}) copy-start(bf16[256,4096]{1,0:T(8,128)(2,1)} %param.5) | copy-start | bytes 6291460
  38.1 61.2 %collective-permute-start.3 = (bf16[96,4096]{1,0:T(8,128)(2,1)}, bf16[96,4096]{1,0:T(8,128)(2,1)}, u32[]{:S(2)}, u32[]{:S(2)}) collective-permute-start(bf16[96,4096]{1,0:T(8,128)(2,1)} %convolution_convert_fusion.4), channel_id=1, source_target_pairs={{0,8},{8,16},{16,24},{24,0},{1,9},{9,17},{17,25},{25,1},{2,10},{10... | collective-permute-start | bytes 2359304 | tf_op jit(solution)/shard_map/ppermute | solution.py:26
  43.3 63.0 %collective-permute-start.4 = (bf16[96,4096]{1,0:T(8,128)(2,1)}, bf16[96,4096]{1,0:T(8,128)(2,1)}, u32[]{:S(2)}, u32[]{:S(2)}) collective-permute-start(bf16[96,4096]{1,0:T(8,128)(2,1)} %convolution_convert_fusion.3), channel_id=1, source_target_pairs={{0,16},{8,24},{16,0},{24,8},{1,17},{9,25},{17,1},{25,9},{2,18},{10... | collective-permute-start | bytes 2359304 | tf_op jit(solution)/shard_map/ppermute | solution.py:26
  48.0 99.3 %collective-permute-start.5 = (bf16[96,4096]{1,0:T(8,128)(2,1)}, bf16[96,4096]{1,0:T(8,128)(2,1)}, u32[]{:S(2)}, u32[]{:S(2)}) collective-permute-start(bf16[96,4096]{1,0:T(8,128)(2,1)} %convolution_convert_fusion.2), channel_id=1, source_target_pairs={{0,24},{8,0},{16,8},{24,16},{1,25},{9,1},{17,9},{25,17},{2,26},{10... | collective-permute-start | bytes 2359304 | tf_op jit(solution)/shard_map/ppermute | solution.py:26
  52.9 29.2 %collective-permute-start.2 = (f32[32,128]{1,0:T(8,128)S(1)}, f32[32,128]{1,0:T(8,128)S(1)}, u32[]{:S(2)}, u32[]{:S(2)}) collective-permute-start(f32[32,128]{1,0:T(8,128)S(1)} %add.168), channel_id=1, source_target_pairs={{0,16},{8,24},{16,0},{24,8},{1,17},{9,25},{17,1},{25,9},{2,18},{10... | collective-permute-start | bytes 49160 | tf_op jit(solution)/shard_map/ppermute | solution.py:30
  82.1 1.0 copy-start.2
  84.9 74.7 %collective-permute-start.6 = (bf16[32,4096]{1,0:T(8,128)(2,1)S(1)}, bf16[32,4096]{1,0:T(8,128)(2,1)}, u32[]{:S(2)}, u32[]{:S(2)}) collective-permute-start(bf16[32,4096]{1,0:T(8,128)(2,1)S(1)} %result_rows.1), channel_id=1, source_target_pairs={{0,1},{1,0},{2,3},{3,2},{4,5},{5,4},{6,7},{7,6},{8,9},{9,8},{10,11... | collective-permute-start | bytes 786440 | tf_op jit(solution)/shard_map/ppermute | solution.py:30
  86.8 44.8 %collective-permute-start.7 = (bf16[32,4096]{1,0:T(8,128)(2,1)S(1)}, bf16[32,4096]{1,0:T(8,128)(2,1)}, u32[]{:S(2)}, u32[]{:S(2)}) collective-permute-start(bf16[32,4096]{1,0:T(8,128)(2,1)S(1)} %result_rows.1), channel_id=1, source_target_pairs={{0,2},{2,4},{4,6},{6,0},{1,3},{3,5},{5,7},{7,1},{8,10},{10,12},{12... | collective-permute-start | bytes 786440 | tf_op jit(solution)/shard_map/ppermute | solution.py:26
  94.4 37.1 %all-to-all-start.1 = ((f32[8,32,128]{2,1,0:T(8,128)}), f32[8,32,128]{2,1,0:T(8,128)S(1)}, u32[]{:S(2)}, u32[]{:S(2)}) async-start(f32[8,32,128]{2,1,0:T(8,128)} %broadcast_in_dim.4), calls=%async_computation.1 | async-start | bytes 262144 | tf_op jit(solution)/shard_map/all_to_all | solution.py:17
  99.3 34.2 %collective-permute-start.9 = (bf16[32,4096]{1,0:T(8,128)(2,1)S(1)}, bf16[32,4096]{1,0:T(8,128)(2,1)}, u32[]{:S(2)}, u32[]{:S(2)}) collective-permute-start(bf16[32,4096]{1,0:T(8,128)(2,1)S(1)} %result_rows.1), channel_id=1, source_target_pairs={{0,6},{2,0},{4,2},{6,4},{1,7},{3,1},{5,3},{7,5},{8,14},{10,8},{12,... | collective-permute-start | bytes 786440 | tf_op jit(solution)/shard_map/ppermute | solution.py:26
  106.2 39.2 %collective-permute-start.11 = (bf16[32,4096]{1,0:T(8,128)(2,1)S(1)}, bf16[32,4096]{1,0:T(8,128)(2,1)}, u32[]{:S(2)}, u32[]{:S(2)}) collective-permute-start(bf16[32,4096]{1,0:T(8,128)(2,1)S(1)} %result_rows.1), channel_id=1, source_target_pairs={{0,4},{2,6},{4,0},{6,2},{1,5},{3,7},{5,1},{7,3},{8,12},{10,14},{12... | collective-permute-start | bytes 786440 | tf_op jit(solution)/shard_map/ppermute | solution.py:26
  131.6 31.3 %collective-permute-start.8 = (bf16[32,4096]{1,0:T(8,128)(2,1)}, bf16[32,4096]{1,0:T(8,128)(2,1)}, u32[]{:S(2)}, u32[]{:S(2)}) collective-permute-start(bf16[32,4096]{1,0:T(8,128)(2,1)} %collective-permute-done.7), channel_id=1, source_target_pairs={{0,1},{1,0},{2,3},{3,2},{4,5},{5,4},{6,7},{7,6},{8,9},{9,8},{10,11... | collective-permute-start | bytes 786440 | tf_op jit(solution)/shard_map/ppermute | solution.py:30
  133.5 32.7 %collective-permute-start.10 = (bf16[32,4096]{1,0:T(8,128)(2,1)}, bf16[32,4096]{1,0:T(8,128)(2,1)}, u32[]{:S(2)}, u32[]{:S(2)}) collective-permute-start(bf16[32,4096]{1,0:T(8,128)(2,1)} %collective-permute-done.9), channel_id=1, source_target_pairs={{0,1},{1,0},{2,3},{3,2},{4,5},{5,4},{6,7},{7,6},{8,9},{9,8},{10,11... | collective-permute-start | bytes 786440 | tf_op jit(solution)/shard_map/ppermute | solution.py:30
  145.4 24.2 %collective-permute-start.12 = (bf16[32,4096]{1,0:T(8,128)(2,1)}, bf16[32,4096]{1,0:T(8,128)(2,1)}, u32[]{:S(2)}, u32[]{:S(2)}) collective-permute-start(bf16[32,4096]{1,0:T(8,128)(2,1)} %collective-permute-done.11), channel_id=1, source_target_pairs={{0,1},{1,0},{2,3},{3,2},{4,5},{5,4},{6,7},{7,6},{8,9},{9,8},{10,11... | collective-permute-start | bytes 786440 | tf_op jit(solution)/shard_map/ppermute | solution.py:30
  147.3 1.1 copy-start.3
  150.5 1.0 copy-start.1
  151.5 37.3 %all-to-all-start.2 = ((bf16[24,4,5120]{2,1,0:T(4,128)(2,1)}), bf16[24,4,5120]{2,1,0:T(4,128)(2,1)}, u32[]{:S(2)}, u32[]{:S(2)}) async-start(bf16[24,4,5120]{2,1,0:T(4,128)(2,1)} %copy-done.1), calls=%async_computation.2 | async-start | bytes 1966080 | tf_op jit(solution)/shard_map/all_to_all | solution.py:17

commit v7 on v6

--- a/solution.py
+++ b/solution.py
@@ -192,9 +192,13 @@
     last = exchange(packed, ("zl", "y"))
     weight_grad, gain_grad = last_sums(last, width)
 
+    before, after = shifted(rows, "zh", 1), shifted(rows, "zh", n_zh - 1)
+    upper, lower = before[: own // 2], after[own // 2 :]
+    upper, lower = shifted(upper, "zh", 1), shifted(lower, "zh", n_zh - 1)
     result = jnp.zeros((tokens, width), BF16)
-    for shift in (0, 1, n_zh - 1, 2):
-        piece = rows if shift == 0 else shifted(rows, "zh", shift)
+    for shift, piece in (
+        (0, rows), (1, before), (n_zh - 1, after), (2, jnp.concatenate([upper, lower], axis=0))
+    ):
         other = swapped(piece, "c", 1)
         source = lax.rem(zh + n_zh - shift, n_zh) * own
         result = lax.dynamic_update_slice_in_dim(result, piece, own_start + source, 0)

time: 192 us -> 171 us (0.89)
  the two profiles are of different devices: /device:TPU:122 before, /device:TPU:120 now
where the time goes in v7:
time: 171 us; the launch traced here: 169 us
  starting transfers between devices  77.6 us (45%)
  waiting for transfers between devices  44.2 us (26%)
  local copies, waits for them, and re-layouts  22 us (13%)
  matrix products  10.6 us (6%)
  other arithmetic  8.28 us (5%)
  Pallas kernels  5.7 us (3%)
    all_to_all x3, waiting for transfers between devices, exchange(): return lax.all_to_all(blocks, axes, 0, 0, tiled=True)  36.9 us
    all_to_all x3, starting transfers between devices, exchange(): return lax.all_to_all(blocks, axes, 0, 0, tiled=True)  30.5 us
    ppermute x7, starting transfers between devices, shifted(): lax.ppermute(block, axis, [(i, (i + shift) % peers) for i in range(peers)])  28.6 us
    ppermute x7, starting transfers between devices, swapped(): lax.ppermute(block, axis, [(i, i ^ bit) for i in range(lax.axis_size(axis...  18.5 us
    dot_general x4, matrix products, block(): lax.dot_general(columns, normed, (((0,), (0,)), ((), ())), preferred_elem...  6.9 us
    ppermute x7, waiting for transfers between devices, shifted(): lax.ppermute(block, axis, [(i, (i + shift) % peers) for i in range(peers)])  6.14 us
    unnamed x19, local copies, waits for them, and re-layouts  5 us
    dynamic_update_slice x4, local copies, waits for them, and re-layouts, body(): lax.dynamic_update_slice_in_dim(result, other, other_start + source, 0)  4.79 us
  transfers between devices with their start and end apart: 17, of which 5 were waited for; matrix products, arithmetic and copies ran while one was open for 16% of the time, Pallas kernels for 2%

profile of v7, /device:TPU:120, one launch (start us, length us, event | category | flops | bytes accessed | tf_op | source)
XLA Modules:
  0.0 169.3 jit_solution(8019984939743638487)
XLA Ops:
  0.7 2.2 %fusion = f32[256]{0:T(256)S(1)} fusion(bf16[256,4096]{1,0:T(8,128)(2,1)} %param.5), kind=kLoop, calls=%fused_computation.9 | loop fusion | flops 3145472 | bytes 2098176 | tf_op jit(solution)/shard_map/reduce_sum | solution.py:141
  3.2 1.7 %convolution_convert_fusion.1 = bf16[128,4096]{1,0:T(8,128)(2,1)} fusion(bf16[384,4096]{1,0:T(8,128)(2,1)S(1)} %copy-done, bf16[256,384]{1,0:T(8,128)(2,1)S(1)} %copy-done.7, s32[]{:T(128)S(6)} %select_n.71), kind=kOutput, calls=%fused_computation.4 | convolution fusion | flops 403177472 | bytes 4292612 | tf_op jit(solution)/shard_map/dot_general | solution.py:145
  4.9 1.9 %collective-permute-start = (bf16[128,4096]{1,0:T(8,128)(2,1)}, bf16[128,4096]{1,0:T(8,128)(2,1)}, u32[]{:S(2)}, u32[]{:S(2)}) collective-permute-start(bf16[128,4096]{1,0:T(8,128)(2,1)} %convolution_convert_fusion.1), channel_id=1, source_target_pairs={{0,1},{1,0},{2,3},{3,2},{4,5},{5,4},{6,7},{7,6},{8,9},{9,8},{10,11... | collective-permute-start | bytes 3145736 | tf_op jit(solution)/shard_map/ppermute | solution.py:30
  6.9 1.7 convolution_convert_fusion
  8.6 1.2 collective-permute-done
  9.8 2.8 %fusion.3 = bf16[128,4096]{1,0:T(8,128)(2,1)} fusion(bf16[128,4096]{1,0:T(8,128)(2,1)} %convolution_convert_fusion, bf16[128,4096]{1,0:T(8,128)(2,1)} %collective-permute-done), kind=kLoop, calls=%fused_computation.14 | loop fusion | flops 2097152 | bytes 3145728 | tf_op jit(solution)/shard_map/convert_element_type | solution.py:153
  13.8 1.8 %fusion.4 = (f32[4096]{0:T(1024)S(1)}, f32[4096]{0:T(1024)S(1)}) fusion(bf16[128,4096]{1,0:T(8,128)(2,1)S(1)} %copy-done.6, f32[256,4096]{1,0:T(8,128)S(1)} %convert_multiply_fusion.1, s32[]{:T(128)S(6)} %select_n.72, s32[]{:T(128)S(6)} %select_n.71, bf16[128,4096]{1,0:T(8,128)(2,1)} %convolution_convert_fusion.1), kind=kLoop, calls=%fused_computation.15 | loop fusion | flops 3137536 | bytes 6324232 | tf_op jit(solution)/shard_map/reduce_sum | solution.py:160
  15.6 13.6 %all-to-all-start = ((bf16[4,32,4096]{2,1,0:T(8,128)(2,1)}), bf16[4,32,4096]{2,1,0:T(8,128)(2,1)}, u32[]{:S(2)}, u32[]{:S(2)}) async-start(bf16[4,32,4096]{2,1,0:T(8,128)(2,1)} %bitcast.14), calls=%async_computation | async-start | bytes 2097152 | tf_op jit(solution)/shard_map/all_to_all | solution.py:17
  29.2 3.5 %collective-permute-start.1 = (f32[32,128]{1,0:T(8,128)S(1)}, f32[32,128]{1,0:T(8,128)S(1)}, u32[]{:S(2)}, u32[]{:S(2)}) collective-permute-start(f32[32,128]{1,0:T(8,128)S(1)} %add_bitcast_fusion), channel_id=1, source_target_pairs={{0,8},{8,0},{16,24},{24,16},{1,9},{9,1},{17,25},{25,17},{2,10},{10... | collective-permute-start | bytes 49160 | tf_op jit(solution)/shard_map/ppermute | solution.py:30
  32.8 1.1 dynamic-slice_bitcast_fusion
  33.8 0.8 pad_maximum_fusion.slices
  35.0 4.9 %collective-permute-start.2 = (f32[32,128]{1,0:T(8,128)S(1)}, f32[32,128]{1,0:T(8,128)S(1)}, u32[]{:S(2)}, u32[]{:S(2)}) collective-permute-start(f32[32,128]{1,0:T(8,128)S(1)} %add.168), channel_id=1, source_target_pairs={{0,16},{8,24},{16,0},{24,8},{1,17},{9,25},{17,1},{25,9},{2,18},{10... | collective-permute-start | bytes 49160 | tf_op jit(solution)/shard_map/ppermute | solution.py:30
  39.9 1.7 %convolution_convert_fusion.5.first = bf16[96,4096]{1,0:T(8,128)(2,1)} fusion(bf16[256,384]{1,0:T(8,128)(2,1)S(1)} %convolution_convert_fusion.6, bf16[256,4096]{1,0:T(8,128)(2,1)S(1)} %copy-done.5, f32[4096]{0:T(1024)S(1)} %convert_element_type.61, f32[256]{0:T(256)S(1)} %add_rsqrt_fusion), kind=kOutput, calls=%fused_computation.8 | convolution fusion | flops 205914112 | bytes 2966528 | tf_op jit(solution)/shard_map/dot_general | solution.py:173
  41.7 1.7 %convolution_convert_fusion.4 = bf16[96,4096]{1,0:T(8,128)(2,1)} fusion(bf16[256,384]{1,0:T(8,128)(2,1)S(1)} %convolution_convert_fusion.6, bf16[256,4096]{1,0:T(8,128)(2,1)S(1)} %copy-done.5, f32[4096]{0:T(1024)S(1)} %convert_element_type.61, f32[256]{0:T(256)S(1)} %add_rsqrt_fusion), kind=kOutput, calls=%fused_computation.7 | convolution fusion | flops 205914112 | bytes 2966528 | tf_op jit(solution)/shard_map/dot_general | solution.py:173
  43.4 1.7 %convolution_convert_fusion.3 = bf16[96,4096]{1,0:T(8,128)(2,1)} fusion(bf16[256,384]{1,0:T(8,128)(2,1)S(1)} %convolution_convert_fusion.6, bf16[256,4096]{1,0:T(8,128)(2,1)S(1)} %copy-done.5, f32[4096]{0:T(1024)S(1)} %convert_element_type.61, f32[256]{0:T(256)S(1)} %add_rsqrt_fusion), kind=kOutput, calls=%fused_computation.6 | convolution fusion | flops 205914112 | bytes 2966528 | tf_op jit(solution)/shard_map/dot_general | solution.py:173
  45.1 1.7 %convolution_convert_fusion.2 = bf16[96,4096]{1,0:T(8,128)(2,1)} fusion(bf16[256,384]{1,0:T(8,128)(2,1)S(1)} %convolution_convert_fusion.6, bf16[256,4096]{1,0:T(8,128)(2,1)S(1)} %copy-done.5, f32[4096]{0:T(1024)S(1)} %convert_element_type.61, f32[256]{0:T(256)S(1)} %add_rsqrt_fusion), kind=kOutput, calls=%fused_computation.5 | convolution fusion | flops 205914112 | bytes 2966528 | tf_op jit(solution)/shard_map/dot_general | solution.py:173
  46.8 2.5 %collective-permute-start.3 = (bf16[96,4096]{1,0:T(8,128)(2,1)}, bf16[96,4096]{1,0:T(8,128)(2,1)}, u32[]{:S(2)}, u32[]{:S(2)}) collective-permute-start(bf16[96,4096]{1,0:T(8,128)(2,1)} %convolution_convert_fusion.4), channel_id=1, source_target_pairs={{0,8},{8,16},{16,24},{24,0},{1,9},{9,17},{17,25},{25,1},{2,10},{10... | collective-permute-start | bytes 2359304 | tf_op jit(solution)/shard_map/ppermute | solution.py:26
  49.3 3.9 %collective-permute-start.4 = (bf16[96,4096]{1,0:T(8,128)(2,1)}, bf16[96,4096]{1,0:T(8,128)(2,1)}, u32[]{:S(2)}, u32[]{:S(2)}) collective-permute-start(bf16[96,4096]{1,0:T(8,128)(2,1)} %convolution_convert_fusion.3), channel_id=1, source_target_pairs={{0,16},{8,24},{16,0},{24,8},{1,17},{9,25},{17,1},{25,9},{2,18},{10... | collective-permute-start | bytes 2359304 | tf_op jit(solution)/shard_map/ppermute | solution.py:26
  53.3 17.8 %all-to-all-done.summands = bf16[4,32,4096]{2,1,0:T(8,128)(2,1)} async-done(((bf16[4,32,4096]{2,1,0:T(8,128)(2,1)}), bf16[4,32,4096]{2,1,0:T(8,128)(2,1)}, u32[]{:S(2)}, u32[]{:S(2)}) %all-to-all-start) | async-done | bytes 1048608 | tf_op jit(solution)/shard_map/all_to_all | solution.py:17
  71.1 1.0 copy-done.2
  72.1 1.7 %result_rows.1 = bf16[32,4096]{1,0:T(8,128)(2,1)S(1)} custom-call(bf16[4,32,4096]{2,1,0:T(8,128)(2,1)} %all-to-all-done.summands, bf16[1,4096]{1,0:T(2,128)(2,1)S(1)} %reshape.90.gain, bf16[2,32,4096]{2,1,0:T(8,128)(2,1)S(1)} %copy-done.2), custom_call_target="tpu_custom_call" | custom-call | flops 1966080 | bytes 1835008 | tf_op jit(solution)/shard_map/result_rows/pallas_call | solution.py:114
  73.8 1.9 %collective-permute-start.6 = (bf16[32,4096]{1,0:T(8,128)(2,1)S(1)}, bf16[32,4096]{1,0:T(8,128)(2,1)}, u32[]{:S(2)}, u32[]{:S(2)}) collective-permute-start(bf16[32,4096]{1,0:T(8,128)(2,1)S(1)} %result_rows.1), channel_id=1, source_target_pairs={{0,1},{1,0},{2,3},{3,2},{4,5},{5,4},{6,7},{7,6},{8,9},{9,8},{10,11... | collective-permute-start | bytes 786440 | tf_op jit(solution)/shard_map/ppermute | solution.py:30
  75.8 4.0 %collective-permute-start.7 = (bf16[32,4096]{1,0:T(8,128)(2,1)S(1)}, bf16[32,4096]{1,0:T(8,128)(2,1)}, u32[]{:S(2)}, u32[]{:S(2)}) collective-permute-start(bf16[32,4096]{1,0:T(8,128)(2,1)S(1)} %result_rows.1), channel_id=1, source_target_pairs={{0,2},{2,4},{4,6},{6,0},{1,3},{3,5},{5,7},{7,1},{8,10},{10,12},{12... | collective-permute-start | bytes 786440 | tf_op jit(solution)/shard_map/ppermute | solution.py:26
  79.8 4.8 %collective-permute-start.9 = (bf16[32,4096]{1,0:T(8,128)(2,1)S(1)}, bf16[32,4096]{1,0:T(8,128)(2,1)}, u32[]{:S(2)}, u32[]{:S(2)}) collective-permute-start(bf16[32,4096]{1,0:T(8,128)(2,1)S(1)} %result_rows.1), channel_id=1, source_target_pairs={{0,6},{2,0},{4,2},{6,4},{1,7},{3,1},{5,3},{7,5},{8,14},{10,8},{12,... | collective-permute-start | bytes 786440 | tf_op jit(solution)/shard_map/ppermute | solution.py:26
  85.3 3.4 %all-to-all-start.1 = ((f32[8,32,128]{2,1,0:T(8,128)}), f32[8,32,128]{2,1,0:T(8,128)S(1)}, u32[]{:S(2)}, u32[]{:S(2)}) async-start(f32[8,32,128]{2,1,0:T(8,128)} %broadcast_in_dim.4), calls=%async_computation.1 | async-start | bytes 262144 | tf_op jit(solution)/shard_map/all_to_all | solution.py:17
  88.7 1.6 broadcast_in_dim.5
  91.0 2.5 %collective-permute-done.7 = bf16[32,4096]{1,0:T(8,128)(2,1)} collective-permute-done((bf16[32,4096]{1,0:T(8,128)(2,1)S(1)}, bf16[32,4096]{1,0:T(8,128)(2,1)}, u32[]{:S(2)}, u32[]{:S(2)}) %collective-permute-start.7) | collective-permute-done | bytes 262176 | tf_op jit(solution)/shard_map/ppermute | solution.py:26
  93.5 4.6 %collective-permute-start.5 = (bf16[96,4096]{1,0:T(8,128)(2,1)}, bf16[96,4096]{1,0:T(8,128)(2,1)}, u32[]{:S(2)}, u32[]{:S(2)}) collective-permute-start(bf16[96,4096]{1,0:T(8,128)(2,1)} %convolution_convert_fusion.2), channel_id=1, source_target_pairs={{0,24},{8,0},{16,8},{24,16},{1,25},{9,1},{17,9},{25,17},{2,26},{10... | collective-permute-start | bytes 2359304 | tf_op jit(solution)/shard_map/ppermute | solution.py:26
  98.1 1.6 slice.28
  99.6 3.6 %collective-permute-done.9 = bf16[32,4096]{1,0:T(8,128)(2,1)} collective-permute-done((bf16[32,4096]{1,0:T(8,128)(2,1)S(1)}, bf16[32,4096]{1,0:T(8,128)(2,1)}, u32[]{:S(2)}, u32[]{:S(2)}) %collective-permute-start.9) | collective-permute-done | bytes 262176 | tf_op jit(solution)/shard_map/ppermute | solution.py:26
  103.2 3.8 %collective-permute-start.11 = (bf16[16,4096]{1,0:T(8,128)(2,1)}, bf16[16,4096]{1,0:T(8,128)(2,1)}, u32[]{:S(2)}, u32[]{:S(2)}) collective-permute-start(bf16[16,4096]{1,0:T(8,128)(2,1)} %slice.28), channel_id=1, source_target_pairs={{0,2},{2,4},{4,6},{6,0},{1,3},{3,5},{5,7},{7,1},{8,10},{10,12},{12... | collective-permute-start | bytes 393224 | tf_op jit(solution)/shard_map/ppermute | solution.py:26
  107.1 1.6 slice.29
  108.7 5.0 %collective-permute-start.12 = (bf16[16,4096]{1,0:T(8,128)(2,1)}, bf16[16,4096]{1,0:T(8,128)(2,1)}, u32[]{:S(2)}, u32[]{:S(2)}) collective-permute-start(bf16[16,4096]{1,0:T(8,128)(2,1)} %slice.29), channel_id=1, source_target_pairs={{0,6},{2,0},{4,2},{6,4},{1,7},{3,1},{5,3},{7,5},{8,14},{10,8},{12,... | collective-permute-start | bytes 393224 | tf_op jit(solution)/shard_map/ppermute | solution.py:26
  113.7 1.7 constant_dynamic-update-slice_fusion.8
  115.3 1.7 constant_dynamic-update-slice_fusion.7
  117.1 1.9 %collective-permute-start.8 = (bf16[32,4096]{1,0:T(8,128)(2,1)}, bf16[32,4096]{1,0:T(8,128)(2,1)}, u32[]{:S(2)}, u32[]{:S(2)}) collective-permute-start(bf16[32,4096]{1,0:T(8,128)(2,1)} %collective-permute-done.7), channel_id=1, source_target_pairs={{0,1},{1,0},{2,3},{3,2},{4,5},{5,4},{6,7},{7,6},{8,9},{9,8},{10,11... | collective-permute-start | bytes 786440 | tf_op jit(solution)/shard_map/ppermute | solution.py:30
  119.0 2.4 %collective-permute-start.10 = (bf16[32,4096]{1,0:T(8,128)(2,1)}, bf16[32,4096]{1,0:T(8,128)(2,1)S(1)}, u32[]{:S(2)}, u32[]{:S(2)}) collective-permute-start(bf16[32,4096]{1,0:T(8,128)(2,1)} %collective-permute-done.9), channel_id=1, source_target_pairs={{0,1},{1,0},{2,3},{3,2},{4,5},{5,4},{6,7},{7,6},{8,9},{9,8},{10,11... | collective-permute-start | bytes 786440 | tf_op jit(solution)/shard_map/ppermute | solution.py:30
  121.4 1.1 copy-done.3
  122.6 2.0 %pack.1 = bf16[24,4,5120]{2,1,0:T(4,128)(2,1)S(1)} custom-call(bf16[96,4096]{1,0:T(8,128)(2,1)S(1)} %copy-done.3, bf16[96,4096]{1,0:T(8,128)(2,1)} %collective-permute-done.3.second, bf16[96,4096]{1,0:T(8,128)(2,1)} %collective-permute-done.4.third, bf16[96,4096]{1,0:T(8,128)(2,1)} %collective-permute-done.5.fourth, ...), custom_call_target="tpu_custom_call" | custom-call | flops 1179648 | bytes 3932160 | tf_op jit(solution)/shard_map/pack/pallas_call | solution.py:60
  124.6 1.0 copy-done.1
  125.6 13.4 %all-to-all-start.2 = ((bf16[24,4,5120]{2,1,0:T(4,128)(2,1)}), bf16[24,4,5120]{2,1,0:T(4,128)(2,1)}, u32[]{:S(2)}, u32[]{:S(2)}) async-start(bf16[24,4,5120]{2,1,0:T(4,128)(2,1)} %copy-done.1), calls=%async_computation.2 | async-start | bytes 1966080 | tf_op jit(solution)/shard_map/all_to_all | solution.py:17
  139.0 0.9 constant_dynamic-update-slice_fusion.1
  140.0 0.9 constant_dynamic-update-slice_fusion
  140.9 1.9 %collective-permute-start.13 = (bf16[32,4096]{1,0:T(8,128)(2,1)S(1)}, bf16[32,4096]{1,0:T(8,128)(2,1)S(1)}, u32[]{:S(2)}, u32[]{:S(2)}) collective-permute-start(bf16[32,4096]{1,0:T(8,128)(2,1)S(1)} %constant_dynamic-update-slice_fusion), channel_id=1, source_target_pairs={{0,1},{1,0},{2,3},{3,2},{4,5},{5,4},{6,7},{7,6},{8,9},{9,8},{10,11... | collective-permute-start | bytes 786440 | tf_op jit(solution)/shard_map/ppermute | solution.py:30
  142.8 1.7 constant_dynamic-update-slice_fusion.6
  144.5 1.7 constant_dynamic-update-slice_fusion.5
  148.3 19.1 %all-to-all-done.2.last = bf16[24,4,5120]{2,1,0:T(4,128)(2,1)} async-done(((bf16[24,4,5120]{2,1,0:T(4,128)(2,1)}), bf16[24,4,5120]{2,1,0:T(4,128)(2,1)}, u32[]{:S(2)}, u32[]{:S(2)}) %all-to-all-start.2) | async-done | bytes 983072 | tf_op jit(solution)/shard_map/all_to_all | solution.py:17
  167.4 2.0 %last_sums.1 = (f32[4,4096]{1,0:T(4,128)}, f32[1,4096]{1,0:T(1,128)}) custom-call(bf16[24,4,5120]{2,1,0:T(4,128)(2,1)} %all-to-all-done.2.last), custom_call_target="tpu_custom_call" | custom-call | flops 491520 | bytes 983040 | tf_op jit(solution)/shard_map/last_sums/pallas_call | solution.py:86
  (43 shorter events, 5.5 us)
Async XLA Ops:
  0.6 2.5 %copy-start = (bf16[384,4096]{1,0:T(8,128)(2,1)S(1)}, bf16[384,4096]{1,0:T(8,128)(2,1)}, u32[]{:S(2)}) copy-start(bf16[384,4096]{1,0:T(8,128)(2,1)} %param.8) | copy-start | bytes 9437188
  0.6 2.5 %copy-start.7 = (bf16[256,384]{1,0:T(8,128)(2,1)S(1)}, bf16[256,384]{1,0:T(8,128)(2,1)}, u32[]{:S(2)}) copy-start(bf16[256,384]{1,0:T(8,128)(2,1)} %param.7) | copy-start | bytes 589828
  3.2 3.6 %copy-start.8 = (bf16[4096]{0:T(1024)(128)(2,1)S(1)}, bf16[4096]{0:T(1024)(128)(2,1)}, u32[]{:S(2)}) copy-start(bf16[4096]{0:T(1024)(128)(2,1)} %param.6) | copy-start | bytes 24580
  4.9 4.9 %collective-permute-start = (bf16[128,4096]{1,0:T(8,128)(2,1)}, bf16[128,4096]{1,0:T(8,128)(2,1)}, u32[]{:S(2)}, u32[]{:S(2)}) collective-permute-start(bf16[128,4096]{1,0:T(8,128)(2,1)} %convolution_convert_fusion.1), channel_id=1, source_target_pairs={{0,1},{1,0},{2,3},{3,2},{4,5},{5,4},{6,7},{7,6},{8,9},{9,8},{10,11... | collective-permute-start | bytes 3145736 | tf_op jit(solution)/shard_map/ppermute | solution.py:30
  8.6 4.0 %copy-start.4 = (bf16[256,4096]{1,0:T(8,128)(2,1)S(1)}, bf16[256,4096]{1,0:T(8,128)(2,1)}, u32[]{:S(2)}) copy-start(bf16[256,4096]{1,0:T(8,128)(2,1)} %param.5) | copy-start | bytes 6291460
  12.6 1.2 copy-start.6
  15.6 55.5 %all-to-all-start = ((bf16[4,32,4096]{2,1,0:T(8,128)(2,1)}), bf16[4,32,4096]{2,1,0:T(8,128)(2,1)}, u32[]{:S(2)}, u32[]{:S(2)}) async-start(bf16[4,32,4096]{2,1,0:T(8,128)(2,1)} %bitcast.14), calls=%async_computation | async-start | bytes 2097152 | tf_op jit(solution)/shard_map/all_to_all | solution.py:17
  29.2 10.7 %copy-start.5 = (bf16[256,4096]{1,0:T(8,128)(2,1)S(1)}, bf16[256,4096]{1,0:T(8,128)(2,1)}, u32[]{:S(2)}) copy-start(bf16[256,4096]{1,0:T(8,128)(2,1)} %param.5) | copy-start | bytes 6291460
  29.2 5.8 %collective-permute-start.1 = (f32[32,128]{1,0:T(8,128)S(1)}, f32[32,128]{1,0:T(8,128)S(1)}, u32[]{:S(2)}, u32[]{:S(2)}) collective-permute-start(f32[32,128]{1,0:T(8,128)S(1)} %add_bitcast_fusion), channel_id=1, source_target_pairs={{0,8},{8,0},{16,24},{24,16},{1,9},{9,1},{17,25},{25,17},{2,10},{10... | collective-permute-start | bytes 49160 | tf_op jit(solution)/shard_map/ppermute | solution.py:30
  35.0 18.2 %collective-permute-start.2 = (f32[32,128]{1,0:T(8,128)S(1)}, f32[32,128]{1,0:T(8,128)S(1)}, u32[]{:S(2)}, u32[]{:S(2)}) collective-permute-start(f32[32,128]{1,0:T(8,128)S(1)} %add.168), channel_id=1, source_target_pairs={{0,16},{8,24},{16,0},{24,8},{1,17},{9,25},{17,1},{25,9},{2,18},{10... | collective-permute-start | bytes 49160 | tf_op jit(solution)/shard_map/ppermute | solution.py:30
  46.8 70.2 %collective-permute-start.3 = (bf16[96,4096]{1,0:T(8,128)(2,1)}, bf16[96,4096]{1,0:T(8,128)(2,1)}, u32[]{:S(2)}, u32[]{:S(2)}) collective-permute-start(bf16[96,4096]{1,0:T(8,128)(2,1)} %convolution_convert_fusion.4), channel_id=1, source_target_pairs={{0,8},{8,16},{16,24},{24,0},{1,9},{9,17},{17,25},{25,1},{2,10},{10... | collective-permute-start | bytes 2359304 | tf_op jit(solution)/shard_map/ppermute | solution.py:26
  49.3 69.7 %collective-permute-start.4 = (bf16[96,4096]{1,0:T(8,128)(2,1)}, bf16[96,4096]{1,0:T(8,128)(2,1)}, u32[]{:S(2)}, u32[]{:S(2)}) collective-permute-start(bf16[96,4096]{1,0:T(8,128)(2,1)} %convolution_convert_fusion.3), channel_id=1, source_target_pairs={{0,16},{8,24},{16,0},{24,8},{1,17},{9,25},{17,1},{25,9},{2,18},{10... | collective-permute-start | bytes 2359304 | tf_op jit(solution)/shard_map/ppermute | solution.py:26
  71.1 1.0 copy-start.2
  73.8 34.8 %collective-permute-start.6 = (bf16[32,4096]{1,0:T(8,128)(2,1)S(1)}, bf16[32,4096]{1,0:T(8,128)(2,1)}, u32[]{:S(2)}, u32[]{:S(2)}) collective-permute-start(bf16[32,4096]{1,0:T(8,128)(2,1)S(1)} %result_rows.1), channel_id=1, source_target_pairs={{0,1},{1,0},{2,3},{3,2},{4,5},{5,4},{6,7},{7,6},{8,9},{9,8},{10,11... | collective-permute-start | bytes 786440 | tf_op jit(solution)/shard_map/ppermute | solution.py:30
  75.8 17.7 %collective-permute-start.7 = (bf16[32,4096]{1,0:T(8,128)(2,1)S(1)}, bf16[32,4096]{1,0:T(8,128)(2,1)}, u32[]{:S(2)}, u32[]{:S(2)}) collective-permute-start(bf16[32,4096]{1,0:T(8,128)(2,1)S(1)} %result_rows.1), channel_id=1, source_target_pairs={{0,2},{2,4},{4,6},{6,0},{1,3},{3,5},{5,7},{7,1},{8,10},{10,12},{12... | collective-permute-start | bytes 786440 | tf_op jit(solution)/shard_map/ppermute | solution.py:26
  79.8 23.4 %collective-permute-start.9 = (bf16[32,4096]{1,0:T(8,128)(2,1)S(1)}, bf16[32,4096]{1,0:T(8,128)(2,1)}, u32[]{:S(2)}, u32[]{:S(2)}) collective-permute-start(bf16[32,4096]{1,0:T(8,128)(2,1)S(1)} %result_rows.1), channel_id=1, source_target_pairs={{0,6},{2,0},{4,2},{6,4},{1,7},{3,1},{5,3},{7,5},{8,14},{10,8},{12,... | collective-permute-start | bytes 786440 | tf_op jit(solution)/shard_map/ppermute | solution.py:26
  85.3 31.7 %all-to-all-start.1 = ((f32[8,32,128]{2,1,0:T(8,128)}), f32[8,32,128]{2,1,0:T(8,128)S(1)}, u32[]{:S(2)}, u32[]{:S(2)}) async-start(f32[8,32,128]{2,1,0:T(8,128)} %broadcast_in_dim.4), calls=%async_computation.1 | async-start | bytes 262144 | tf_op jit(solution)/shard_map/all_to_all | solution.py:17
  93.5 27.9 %collective-permute-start.5 = (bf16[96,4096]{1,0:T(8,128)(2,1)}, bf16[96,4096]{1,0:T(8,128)(2,1)}, u32[]{:S(2)}, u32[]{:S(2)}) collective-permute-start(bf16[96,4096]{1,0:T(8,128)(2,1)} %convolution_convert_fusion.2), channel_id=1, source_target_pairs={{0,24},{8,0},{16,8},{24,16},{1,25},{9,1},{17,9},{25,17},{2,26},{10... | collective-permute-start | bytes 2359304 | tf_op jit(solution)/shard_map/ppermute | solution.py:26
  103.2 35.8 %collective-permute-start.11 = (bf16[16,4096]{1,0:T(8,128)(2,1)}, bf16[16,4096]{1,0:T(8,128)(2,1)}, u32[]{:S(2)}, u32[]{:S(2)}) collective-permute-start(bf16[16,4096]{1,0:T(8,128)(2,1)} %slice.28), channel_id=1, source_target_pairs={{0,2},{2,4},{4,6},{6,0},{1,3},{3,5},{5,7},{7,1},{8,10},{10,12},{12... | collective-permute-start | bytes 393224 | tf_op jit(solution)/shard_map/ppermute | solution.py:26
  108.7 31.3 %collective-permute-start.12 = (bf16[16,4096]{1,0:T(8,128)(2,1)}, bf16[16,4096]{1,0:T(8,128)(2,1)}, u32[]{:S(2)}, u32[]{:S(2)}) collective-permute-start(bf16[16,4096]{1,0:T(8,128)(2,1)} %slice.29), channel_id=1, source_target_pairs={{0,6},{2,0},{4,2},{6,4},{1,7},{3,1},{5,3},{7,5},{8,14},{10,8},{12,... | collective-permute-start | bytes 393224 | tf_op jit(solution)/shard_map/ppermute | solution.py:26
  117.1 25.8 %collective-permute-start.8 = (bf16[32,4096]{1,0:T(8,128)(2,1)}, bf16[32,4096]{1,0:T(8,128)(2,1)}, u32[]{:S(2)}, u32[]{:S(2)}) collective-permute-start(bf16[32,4096]{1,0:T(8,128)(2,1)} %collective-permute-done.7), channel_id=1, source_target_pairs={{0,1},{1,0},{2,3},{3,2},{4,5},{5,4},{6,7},{7,6},{8,9},{9,8},{10,11... | collective-permute-start | bytes 786440 | tf_op jit(solution)/shard_map/ppermute | solution.py:30
  119.0 27.2 %collective-permute-start.10 = (bf16[32,4096]{1,0:T(8,128)(2,1)}, bf16[32,4096]{1,0:T(8,128)(2,1)S(1)}, u32[]{:S(2)}, u32[]{:S(2)}) collective-permute-start(bf16[32,4096]{1,0:T(8,128)(2,1)} %collective-permute-done.9), channel_id=1, source_target_pairs={{0,1},{1,0},{2,3},{3,2},{4,5},{5,4},{6,7},{7,6},{8,9},{9,8},{10,11... | collective-permute-start | bytes 786440 | tf_op jit(solution)/shard_map/ppermute | solution.py:30
  121.4 1.1 copy-start.3
  124.6 1.0 copy-start.1
  125.6 41.8 %all-to-all-start.2 = ((bf16[24,4,5120]{2,1,0:T(4,128)(2,1)}), bf16[24,4,5120]{2,1,0:T(4,128)(2,1)}, u32[]{:S(2)}, u32[]{:S(2)}) async-start(bf16[24,4,5120]{2,1,0:T(4,128)(2,1)} %copy-done.1), calls=%async_computation.2 | async-start | bytes 1966080 | tf_op jit(solution)/shard_map/all_to_all | solution.py:17
  140.9 6.7 %collective-permute-start.13 = (bf16[32,4096]{1,0:T(8,128)(2,1)S(1)}, bf16[32,4096]{1,0:T(8,128)(2,1)S(1)}, u32[]{:S(2)}, u32[]{:S(2)}) collective-permute-start(bf16[32,4096]{1,0:T(8,128)(2,1)S(1)} %constant_dynamic-update-slice_fusion), channel_id=1, source_target_pairs={{0,1},{1,0},{2,3},{3,2},{4,5},{5,4},{6,7},{7,6},{8,9},{9,8},{10,11... | collective-permute-start | bytes 786440 | tf_op jit(solution)/shard_map/ppermute | solution.py:30
